TPU v7x, 32 devices: a whole 2x2x4 slice. The times are simulated.
32 devices in a mesh: seq: 8 (over z, x), head: 4 (over y, core).
Axes of the slice: x: 2, y: 2, z: 4, core: 2. Of those that a mesh axis runs over, the one named last changes fastest.
Arguments:
- queries: bfloat16 [2048, 4096], P('seq', 'head'), may hold values from -6 to 6
- keys: bfloat16 [2048, 4096], P('seq', 'head'), may hold values from -6 to 6
- values: bfloat16 [2048, 4096], P('seq', 'head'), may hold values from -6 to 6
- outputs: bfloat16 [2048, 4096], P('seq', 'head'), may hold values from -6 to 6
- out_grad: bfloat16 [2048, 4096], P('seq', 'head'), may hold values from -6 to 6
- log_sum: float32 [32, 2048], P('head', 'seq'), may hold values from 4 to 6
- selected: int32 [32, 32, 16], P('head', 'seq'), may hold values from -1 to 31, as said below
- w_query: bfloat16 [4096, 4096], P(None, 'head'), may hold values from -0.09375 to 0.09375
Outputs:
- x_grad: bfloat16 [2048, 4096], P(('seq', 'head'))
- key_gradient: bfloat16 [2048, 4096], P('seq', 'head')
- value_gradient: bfloat16 [2048, 4096], P('seq', 'head')
Inputs may be any that keep to these rules, and one draw needn't show every extreme that they name: Row (h, b) lists distinct blocks: entry 0 is b itself, the others are blocks before b, and entries equal to -1 (unused) come last. Over the query blocks of one index of seq and the heads of one index of head, the distinct (head, block) pairs selected from the blocks of any one other index of seq number at most 2; some pair of indices reaches 2 in every draw.
All inputs are finite; a program needn't handle non-finite values.
Results may differ from a plain program's by a relative error of at most 0.0075.
Values may be sent and summed in bfloat16 or wider, within the bound.
No kernel may reach another device: no remote copies, remote signals or barrier semaphores. Data moves between devices by JAX's collectives and lax.ppermute only.
A program may use at most 128 MiB of HBM per device.

v0:
```python
import math

import jax
import jax.numpy as jnp
from jax import lax
from jax.sharding import PartitionSpec as P

CAP = 2


def head_units(matrix, head_count, block_count, block_size, head_size):
    shaped = matrix.reshape(block_count, block_size, head_count, head_size)
    return shaped.transpose(2, 0, 1, 3)


def slot_table(present, slot_rank, unit_count):
    slots = jnp.arange(CAP, dtype=jnp.int32)
    matched = (present[:, None, :] == 1) & (slot_rank[:, None, :] == slots[None, :, None])
    labels = jnp.arange(1, unit_count + 1, dtype=jnp.int32)
    return jnp.sum(jnp.where(matched, labels[None, None, :], 0), axis=2) - 1


def pick_units(table, index):
    table_rows = table.shape[0]
    flat_index = index.reshape(-1)
    selector = (flat_index[:, None] == jnp.arange(table_rows, dtype=jnp.int32)[None, :]).astype(
        table.dtype
    )
    picked = jnp.dot(selector, table.reshape(table_rows, -1), preferred_element_type=jnp.float32)
    return picked.astype(table.dtype).reshape(index.shape + table.shape[1:])


def add_units(total, index, rows):
    total_rows = total.shape[0]
    flat_index = index.reshape(-1)
    selector = (jnp.arange(total_rows, dtype=jnp.int32)[:, None] == flat_index[None, :]).astype(
        jnp.float32
    )
    summed = jnp.dot(
        selector,
        rows.reshape(flat_index.shape[0], -1),
        preferred_element_type=jnp.float32,
        precision=lax.Precision.HIGHEST,
    )
    return total + summed.reshape(total.shape)


def attend(
    key_pool,
    pool_index,
    chosen,
    query_units,
    grad_units,
    log_units,
    delta_units,
    first_block,
    carry_init,
):
    head_count, block_count, pick_count = pool_index.shape
    block_size = query_units.shape[2]
    head_size = query_units.shape[3]
    group_size = math.gcd(head_count, max(1, 512 // (block_count * block_size)))
    group_count = head_count // group_size
    logit_scale = head_size ** (-0.5)
    offsets = jnp.arange(block_size, dtype=jnp.int32)
    query_pos = (first_block + jnp.arange(block_count, dtype=jnp.int32))[
        :, None
    ] * block_size + offsets[None, :]

    def folded(array):
        return array.reshape((group_count, group_size) + array.shape[1:])

    def step(carry, inputs):
        query_slice, partial_gradient, log_part, delta_part, index_part, chosen_part = inputs
        gathered = pick_units(key_pool, index_part)
        key_part = gathered[..., :head_size]
        value_part = gathered[..., head_size:]
        attention_logits = (
            jnp.einsum(
                "gbqd,gbksd->gbqks", query_slice, key_part, preferred_element_type=jnp.float32
            )
            * logit_scale
        )
        key_pos = chosen_part[:, :, None, :, None] * block_size + offsets
        allowed = (chosen_part >= 0)[:, :, None, :, None] & (
            key_pos <= query_pos[None, :, :, None, None]
        )
        probs = jnp.where(
            allowed, jnp.exp(attention_logits - log_part[..., None, None]), jnp.float32(0.0)
        )
        reduced_probabilities = probs.astype(jnp.bfloat16)
        probability_gradient = jnp.einsum(
            "gbqd,gbksd->gbqks", partial_gradient, value_part, preferred_element_type=jnp.float32
        )
        score_gradient = (probs * (probability_gradient - delta_part[..., None, None])).astype(
            jnp.bfloat16
        )
        query_gradient = (
            jnp.einsum(
                "gbqks,gbksd->gbqd", score_gradient, key_part, preferred_element_type=jnp.float32
            )
            * logit_scale
        )
        key_gradient = (
            jnp.einsum(
                "gbqks,gbqd->gbksd", score_gradient, query_slice, preferred_element_type=jnp.float32
            )
            * logit_scale
        )
        value_gradient = jnp.einsum(
            "gbqks,gbqd->gbksd",
            reduced_probabilities,
            partial_gradient,
            preferred_element_type=jnp.float32,
        )
        both = jnp.concatenate((key_gradient, value_gradient), axis=-1).reshape(
            -1, block_size, 2 * head_size
        )
        carry = add_units(carry, index_part, both)
        return (carry, query_gradient)

    inputs = tuple(
        (
            folded(array)
            for array in (query_units, grad_units, log_units, delta_units, pool_index, chosen)
        )
    )
    totals, query_gradient = lax.scan(step, carry_init, inputs)
    return (totals, query_gradient.reshape(query_units.shape))


def per_device(queries, keys, values, outputs, out_grad, log_sum, selected, w_query):
    tok_rows, row_width = queries.shape
    head_count, block_count, pick_count = selected.shape
    head_size = row_width // head_count
    block_size = tok_rows // block_count
    unit_count = head_count * block_count
    shard_count = lax.axis_size("seq")
    my_index = lax.axis_index("seq")
    first_block = my_index * block_count
    query_units = head_units(queries, head_count, block_count, block_size, head_size)
    grad_units = head_units(out_grad, head_count, block_count, block_size, head_size)
    local_kv = jnp.concatenate(
        (
            head_units(keys, head_count, block_count, block_size, head_size),
            head_units(values, head_count, block_count, block_size, head_size),
        ),
        axis=-1,
    )
    local_kv = local_kv.reshape(unit_count, block_size, 2 * head_size)
    products = out_grad.astype(jnp.float32) * outputs.astype(jnp.float32)
    delta_units = jnp.sum(products.reshape(tok_rows, head_count, head_size), axis=-1).T.reshape(
        head_count, block_count, block_size
    )
    log_units = log_sum.reshape(head_count, block_count, block_size)
    owner_index = selected // block_count
    local_block = selected % block_count
    remote = (selected >= 0) & (owner_index != my_index)
    all_blocks = jnp.arange(shard_count * block_count, dtype=jnp.int32)
    matches = jnp.any(
        selected.reshape(head_count, block_count * pick_count, 1) == all_blocks[None, None, :],
        axis=1,
    )
    matches = matches & (all_blocks // block_count != my_index)[None, :]
    present = matches.reshape(head_count, shard_count, block_count).transpose(1, 0, 2)
    present = present.reshape(shard_count, unit_count).astype(jnp.int32)
    slot_rank = jnp.cumsum(present, axis=1) - present
    wanted = slot_table(present, slot_rank, unit_count)
    head_column = jnp.arange(head_count, dtype=jnp.int32)[:, None, None] * block_count
    owner_safe = jnp.clip(owner_index, 0, shard_count - 1)
    rank_at = slot_rank.reshape(-1)[owner_safe * unit_count + head_column + local_block]
    pool_index = jnp.where(
        remote, unit_count + owner_safe * CAP + rank_at, head_column + local_block
    )
    incoming = lax.all_to_all(wanted, "seq", split_axis=0, concat_axis=0, tiled=True)
    outgoing = pick_units(local_kv, incoming)
    zero_grads = jnp.zeros((unit_count, block_size, 2 * head_size), jnp.float32)
    remote_zero = jnp.zeros((shard_count * CAP, block_size, 2 * head_size), jnp.float32)
    pulled = lax.all_to_all(outgoing, "seq", split_axis=0, concat_axis=0, tiled=True)
    key_pool = jnp.concatenate(
        (local_kv, pulled.reshape(shard_count * CAP, block_size, 2 * head_size)), axis=0
    )
    pool_grads, query_gradient = attend(
        key_pool,
        pool_index[:, :, 1:],
        selected[:, :, 1:],
        query_units,
        grad_units,
        log_units,
        delta_units,
        first_block,
        jnp.concatenate((zero_grads, remote_zero), axis=0),
    )
    returned = lax.all_to_all(
        pool_grads[unit_count:]
        .reshape(shard_count, CAP, block_size, 2 * head_size)
        .astype(jnp.bfloat16),
        "seq",
        split_axis=0,
        concat_axis=0,
        tiled=True,
    ).astype(jnp.float32)
    own_grads = pool_grads[:unit_count]
    own_grads, own_query = attend(
        local_kv,
        pool_index[:, :, :1],
        selected[:, :, :1],
        query_units,
        grad_units,
        log_units,
        delta_units,
        first_block,
        own_grads,
    )
    query_gradient = query_gradient + own_query
    local_grads = add_units(own_grads, incoming, returned.reshape(-1, block_size, 2 * head_size))
    arranged = local_grads.reshape(head_count, block_count, block_size, 2 * head_size).transpose(
        1, 2, 0, 3
    )
    key_gradient = arranged[..., :head_size].reshape(tok_rows, row_width).astype(jnp.bfloat16)
    value_gradient = arranged[..., head_size:].reshape(tok_rows, row_width).astype(jnp.bfloat16)
    query_rows = (
        query_gradient.astype(jnp.bfloat16).transpose(1, 2, 0, 3).reshape(tok_rows, row_width)
    )
    x_grad = lax.psum_scatter(
        lax.dot_general(
            query_rows, w_query, (((1,), (1,)), ((), ())), preferred_element_type=jnp.float32
        ),
        "head",
        scatter_dimension=0,
        tiled=True,
    ).astype(jnp.bfloat16)
    return (x_grad, key_gradient, value_gradient)


def solution(mesh):
    return jax.shard_map(
        per_device,
        mesh=mesh,
        in_specs=(
            P("seq", "head"),
            P("seq", "head"),
            P("seq", "head"),
            P("seq", "head"),
            P("seq", "head"),
            P("head", "seq"),
            P("head", "seq", None),
            P(None, "head"),
        ),
        out_specs=(P(("seq", "head"), None), P("seq", "head"), P("seq", "head")),
        check_vma=False,
    )
```

profile of v0, /device:TPU:0, one launch (start us, length us, event | category | flops | bytes accessed | tf_op | source)
XLA Modules:
  0.0 232.7 jit_solution(10097874333445133495)
XLA Ops:
  9.7 7.3 %all-to-all-start = ((s32[8,1,2]{2,1,0:T(1,128)}), s32[8,1,2]{2,1,0:T(1,128)S(1)}, u32[]{:S(2)}, u32[]{:S(2)}) async-start(s32[8,1,2]{2,1,0:T(1,128)} %copy.139), calls=%async_computation | async-start | bytes 8192 | tf_op jit(solution)/shard_map/all_to_all | solution.py:175
  17.0 1.1 copy.170
  18.1 1.1 copy.171
  20.3 3.1 %all-to-all-done = s32[8,1,2]{2,1,0:T(1,128)S(1)} async-done(((s32[8,1,2]{2,1,0:T(1,128)}), s32[8,1,2]{2,1,0:T(1,128)S(1)}, u32[]{:S(2)}, u32[]{:S(2)}) %all-to-all-start) | async-done | bytes 96 | tf_op jit(solution)/shard_map/all_to_all | solution.py:175
  25.9 3.5 %all-to-all-start.1 = ((bf16[8,2,64,256]{3,2,1,0:T(8,128)(2,1)}), bf16[8,2,64,256]{3,2,1,0:T(8,128)(2,1)S(1)}, u32[]{:S(2)}, u32[]{:S(2)}) async-start(bf16[8,2,64,256]{3,2,1,0:T(8,128)(2,1)} %bitcast.99), calls=%async_computation.1 | async-start | bytes 1048576 | tf_op jit(solution)/shard_map/all_to_all | solution.py:179
  30.3 3.5 %gather_fusion = s32[512]{0:T(512)S(1)} fusion(s32[256]{0:T(256)S(1)} %sub.73, s32[1024]{0:T(1024)S(1)} %pad_clamp_fusion), kind=kCustom, calls=%fused_computation | custom fusion | bytes 6144 | tf_op jit(solution)/shard_map/gather | solution.py:171
  34.2 0.9 copy.135
  35.2 0.9 copy.141
  37.2 5.6 %all-to-all-done.1 = bf16[8,2,64,256]{3,2,1,0:T(8,128)(2,1)S(1)} async-done(((bf16[8,2,64,256]{3,2,1,0:T(8,128)(2,1)}), bf16[8,2,64,256]{3,2,1,0:T(8,128)(2,1)S(1)}, u32[]{:S(2)}, u32[]{:S(2)}) %all-to-all-start.1) | async-done | bytes 524320 | tf_op jit(solution)/shard_map/all_to_all | solution.py:179
  42.8 1.3 pad_maximum_fusion.2
  44.5 1.1 broadcast.205.clone
  45.6 91.4 %while.26 = (s32[]{:T(128)}, f32[48,64,256]{2,0,1:T(8,128)S(1)}, f32[4,2,4,64,128]{4,3,2,1,0:T(8,128)}, s32[4,2,4,15]{3,2,1,0:T(4,128)S(1)}, s32[4,2,4,15]{3,2,1...) while((s32[]{:T(128)}, f32[48,64,256]{2,0,1:T(8,128)S(1)}, ...), condition=%wide.region_5.6_spmd.clone, body=%wide.region_4.5_spmd.clone.sunk | while | flops 1963019520 | bytes 80082968 | solution.py:128
  45.9 2.3 %copy.217 = bf16[6,8,64,256]{3,1,2,0:T(8,128)(2,1)S(1)} copy(bf16[6,8,64,256]{3,2,1,0:T(8,128)(2,1)} %bitcast.306) | data formatting | bytes 3145728 | tf_op jit(solution)/shard_map/while
  48.2 1.2 convolution_convert_fusion.5
  49.5 1.2 copy.218
  50.7 1.8 fusion.152
  52.5 2.2 multiply_convert_fusion.2
  54.7 1.3 fusion.155
  56.0 2.0 fusion.153
  59.7 8.7 %fusion.154 = f32[48,64,256]{2,0,1:T(8,128)S(1)} fusion(f32[48,64,256]{2,0,1:T(8,128)S(1)} %get-tuple-element.480, s32[120]{0:T(128)S(1)} %eq.255, f32[15,8,64,256]{3,2,1,0:T(8,128)S(1)} %bitcast.296), kind=kOutput, calls=%fused_computation.22.clone.1 | convolution fusion | flops 1133254272 | bytes 14156256 | tf_op jit(solution)/shard_map/while/body/eval_jaxpr/dot_general | solution.py:39
  68.7 2.3 %copy.217 = bf16[6,8,64,256]{3,1,2,0:T(8,128)(2,1)S(1)} copy(bf16[6,8,64,256]{3,2,1,0:T(8,128)(2,1)} %bitcast.306) | data formatting | bytes 3145728 | tf_op jit(solution)/shard_map/while
  71.1 1.2 convolution_convert_fusion.5
  72.3 1.2 copy.218
  73.5 1.8 fusion.152
  75.3 2.2 multiply_convert_fusion.2
  77.5 1.3 fusion.155
  78.8 2.0 fusion.153
  82.5 8.7 %fusion.154 = f32[48,64,256]{2,0,1:T(8,128)S(1)} fusion(f32[48,64,256]{2,0,1:T(8,128)S(1)} %get-tuple-element.480, s32[120]{0:T(128)S(1)} %eq.255, f32[15,8,64,256]{3,2,1,0:T(8,128)S(1)} %bitcast.296), kind=kOutput, calls=%fused_computation.22.clone.1 | convolution fusion | flops 1133254272 | bytes 14156256 | tf_op jit(solution)/shard_map/while/body/eval_jaxpr/dot_general | solution.py:39
  91.5 2.3 %copy.217 = bf16[6,8,64,256]{3,1,2,0:T(8,128)(2,1)S(1)} copy(bf16[6,8,64,256]{3,2,1,0:T(8,128)(2,1)} %bitcast.306) | data formatting | bytes 3145728 | tf_op jit(solution)/shard_map/while
  93.9 1.2 convolution_convert_fusion.5
  95.1 1.2 copy.218
  96.3 1.8 fusion.152
  98.1 2.2 multiply_convert_fusion.2
  100.3 1.3 fusion.155
  101.6 2.0 fusion.153
  105.3 8.7 %fusion.154 = f32[48,64,256]{2,0,1:T(8,128)S(1)} fusion(f32[48,64,256]{2,0,1:T(8,128)S(1)} %get-tuple-element.480, s32[120]{0:T(128)S(1)} %eq.255, f32[15,8,64,256]{3,2,1,0:T(8,128)S(1)} %bitcast.296), kind=kOutput, calls=%fused_computation.22.clone.1 | convolution fusion | flops 1133254272 | bytes 14156256 | tf_op jit(solution)/shard_map/while/body/eval_jaxpr/dot_general | solution.py:39
  114.3 2.3 %copy.217 = bf16[6,8,64,256]{3,1,2,0:T(8,128)(2,1)S(1)} copy(bf16[6,8,64,256]{3,2,1,0:T(8,128)(2,1)} %bitcast.306) | data formatting | bytes 3145728 | tf_op jit(solution)/shard_map/while
  116.7 1.2 convolution_convert_fusion.5
  117.9 1.2 copy.218
  119.1 1.8 fusion.152
  120.9 2.2 multiply_convert_fusion.2
  123.1 1.3 fusion.155
  124.4 2.0 fusion.153
  128.1 8.7 %fusion.154 = f32[48,64,256]{2,0,1:T(8,128)S(1)} fusion(f32[48,64,256]{2,0,1:T(8,128)S(1)} %get-tuple-element.480, s32[120]{0:T(128)S(1)} %eq.255, f32[15,8,64,256]{3,2,1,0:T(8,128)S(1)} %bitcast.296), kind=kOutput, calls=%fused_computation.22.clone.1 | convolution fusion | flops 1133254272 | bytes 14156256 | tf_op jit(solution)/shard_map/while/body/eval_jaxpr/dot_general | solution.py:39
  137.1 1.5 slice.41
  138.6 1.1 broadcast.205
  139.7 30.4 %while.27 = (s32[]{:T(128)}, f32[32,64,256]{2,0,1:T(8,128)}, f32[4,2,4,64,128]{4,3,2,1,0:T(8,128)}, s32[4,2,4,1]{2,1,3,0:T(2,128)S(1)}, s32[4,2,4,1]{2,1,3,0:T(2...) while((s32[]{:T(128)}, f32[32,64,256]{2,0,1:T(8,128)}, ...), condition=%wide.region_7.8_spmd.clone, body=%wide.region_6.7_spmd.clone.sunk | while | flops 101877008 | bytes 33384552 | solution.py:128
  139.9 2.0 copy.220
  144.1 1.8 convolution_add_fusion.2
  146.0 1.3 copy-done.1
  147.5 2.0 copy.220
  151.8 1.8 convolution_add_fusion.2
  153.6 1.3 copy-done.1
  155.1 2.0 copy.220
  159.4 1.8 convolution_add_fusion.2
  161.2 1.3 copy-done.1
  162.7 2.0 copy.220
  167.0 1.8 convolution_add_fusion.2
  168.8 1.3 copy-done.1
  170.1 1.7 add_convert_fusion.1
  172.2 7.7 %fusion.83 = f32[256,4096]{1,0:T(8,128)} fusion(bf16[4096,1024]{1,0:T(8,128)(2,1)} %param.19, bf16[32,8,8,128]{3,2,1,0:T(8,128)(2,1)S(1)} %bitcast.335), kind=kOutput, calls=%fused_computation.110 | convolution fusion | flops 2147483648 | bytes 13107200 | tf_op jit(solution)/shard_map/dot_general | solution.py:226
  180.1 17.4 %all_to_all.16 = bf16[8,2,64,256]{3,2,1,0:T(8,128)(2,1)S(1)} all-to-all(bf16[8,2,64,256]{3,2,1,0:T(8,128)(2,1)S(1)} %bitcast.319), channel_id=1, replica_groups=mesh['seq'=8,'head'=4] {'seq'}, dimensions={0} | all-to-all | bytes 1048576 | tf_op jit(solution)/shard_map/all_to_all | solution.py:194
  200.7 23.1 %reduce-scatter.2.cloned.1.call-done = f32[64,4096]{1,0:T(8,128)} async-done(((f32[256,4096]{1,0:T(8,128)}), f32[64,4096]{1,0:T(8,128)}) %reduce-scatter.2.cloned.1.call-update) | async-done | bytes 1048592 | tf_op jit(solution)/shard_map/reduce_scatter | solution.py:225
  223.8 2.1 convert_element_type.90
  (220 shorter events, 30.1 us)
Async XLA Ops:
  9.7 13.7 %all-to-all-start = ((s32[8,1,2]{2,1,0:T(1,128)}), s32[8,1,2]{2,1,0:T(1,128)S(1)}, u32[]{:S(2)}, u32[]{:S(2)}) async-start(s32[8,1,2]{2,1,0:T(1,128)} %copy.139), calls=%async_computation | async-start | bytes 8192 | tf_op jit(solution)/shard_map/all_to_all | solution.py:175
  19.5 10.0 %copy-start.11 = (s32[8,4,16]{2,1,0:T(4,128)S(1)}, s32[8,4,16]{2,1,0:T(4,128)}, u32[]{:S(2)}) copy-start(s32[8,4,16]{2,1,0:T(4,128)} %param.18) | copy-start | bytes 6148
  19.5 10.5 %copy-start.12 = (f32[8,256]{1,0:T(8,128)S(1)}, f32[8,256]{1,0:T(8,128)}, u32[]{:S(2)}) copy-start(f32[8,256]{1,0:T(8,128)} %param.17) | copy-start | bytes 24580
  19.7 23.1 %copy-start.3 = (bf16[8,4,64,256]{3,2,1,0:T(8,128)(2,1)}, bf16[8,4,64,256]{3,2,1,0:T(8,128)(2,1)S(1)}, u32[]{:S(2)}) copy-start(bf16[8,4,64,256]{3,2,1,0:T(8,128)(2,1)S(1)} %copy.136) | copy-start | bytes 3145732
  24.6 4.9 %copy-start.13 = (s32[16]{0:T(128)}, s32[16]{0:T(128)S(1)}, u32[]{:S(2)}) copy-start(s32[16]{0:T(128)S(1)} %eq.134) | copy-start | bytes 196
  25.9 16.9 %all-to-all-start.1 = ((bf16[8,2,64,256]{3,2,1,0:T(8,128)(2,1)}), bf16[8,2,64,256]{3,2,1,0:T(8,128)(2,1)S(1)}, u32[]{:S(2)}, u32[]{:S(2)}) async-start(bf16[8,2,64,256]{3,2,1,0:T(8,128)(2,1)} %bitcast.99), calls=%async_computation.1 | async-start | bytes 1048576 | tf_op jit(solution)/shard_map/all_to_all | solution.py:179
  29.4 194.3 %reduce-scatter.2.cloned.1.call-start = ((), (), s32[]{:S(2)}) async-start(), calls=%async_computation.4 | async-start | bytes 5242880 | tf_op jit(solution)/shard_map/reduce_scatter | solution.py:225
  30.3 3.8 %copy-start.9 = (bf16[256,1024]{1,0:T(8,128)(2,1)S(1)}, bf16[256,1024]{1,0:T(8,128)(2,1)}, u32[]{:S(2)}) copy-start(bf16[256,1024]{1,0:T(8,128)(2,1)} %param.12) | copy-start | bytes 1572868
  30.3 4.8 %copy-start.8 = (bf16[256,1024]{1,0:T(8,128)(2,1)S(1)}, bf16[256,1024]{1,0:T(8,128)(2,1)}, u32[]{:S(2)}) copy-start(bf16[256,1024]{1,0:T(8,128)(2,1)} %param.16) | copy-start | bytes 1572868
  33.9 2.2 copy-start.10
  49.5 1.2 copy-start.6
  50.6 1.9 copy-start.4
  72.3 1.2 copy-start.6
  73.5 1.9 copy-start.4
  95.1 1.2 copy-start.6
  96.3 1.9 copy-start.4
  117.9 1.2 copy-start.6
  119.1 1.9 copy-start.4
  139.8 2.5 %copy-start.7 = (bf16[4,2,4,64,128]{4,3,2,1,0:T(8,128)(2,1)S(1)}, bf16[4,2,4,64,128]{4,3,2,1,0:T(8,128)(2,1)}, u32[]{:S(2)}) copy-start(bf16[4,2,4,64,128]{4,3,2,1,0:T(8,128)(2,1)} %get-tuple-element.532) | copy-start | bytes 1572868 | tf_op jit(solution)/shard_map/while
  139.8 2.7 %copy-start.5 = (bf16[4,2,4,64,128]{4,3,2,1,0:T(8,128)(2,1)S(1)}, bf16[4,2,4,64,128]{4,3,2,1,0:T(8,128)(2,1)}, u32[]{:S(2)}) copy-start(bf16[4,2,4,64,128]{4,3,2,1,0:T(8,128)(2,1)} %get-tuple-element.535) | copy-start | bytes 1572868 | tf_op jit(solution)/shard_map/while
  139.9 4.2 %copy-start = (f32[32,64,256]{2,0,1:T(8,128)S(1)}, f32[32,64,256]{2,0,1:T(8,128)}, u32[]{:S(2)}) copy-start(f32[32,64,256]{2,0,1:T(8,128)} %get-tuple-element.516) | copy-start | bytes 6291460 | tf_op jit(solution)/shard_map/while
  146.0 1.3 copy-start.1
  147.4 2.5 %copy-start.7 = (bf16[4,2,4,64,128]{4,3,2,1,0:T(8,128)(2,1)S(1)}, bf16[4,2,4,64,128]{4,3,2,1,0:T(8,128)(2,1)}, u32[]{:S(2)}) copy-start(bf16[4,2,4,64,128]{4,3,2,1,0:T(8,128)(2,1)} %get-tuple-element.532) | copy-start | bytes 1572868 | tf_op jit(solution)/shard_map/while
  147.4 2.7 %copy-start.5 = (bf16[4,2,4,64,128]{4,3,2,1,0:T(8,128)(2,1)S(1)}, bf16[4,2,4,64,128]{4,3,2,1,0:T(8,128)(2,1)}, u32[]{:S(2)}) copy-start(bf16[4,2,4,64,128]{4,3,2,1,0:T(8,128)(2,1)} %get-tuple-element.535) | copy-start | bytes 1572868 | tf_op jit(solution)/shard_map/while
  147.5 4.2 %copy-start = (f32[32,64,256]{2,0,1:T(8,128)S(1)}, f32[32,64,256]{2,0,1:T(8,128)}, u32[]{:S(2)}) copy-start(f32[32,64,256]{2,0,1:T(8,128)} %get-tuple-element.516) | copy-start | bytes 6291460 | tf_op jit(solution)/shard_map/while
  153.6 1.3 copy-start.1
  155.0 2.5 %copy-start.7 = (bf16[4,2,4,64,128]{4,3,2,1,0:T(8,128)(2,1)S(1)}, bf16[4,2,4,64,128]{4,3,2,1,0:T(8,128)(2,1)}, u32[]{:S(2)}) copy-start(bf16[4,2,4,64,128]{4,3,2,1,0:T(8,128)(2,1)} %get-tuple-element.532) | copy-start | bytes 1572868 | tf_op jit(solution)/shard_map/while
  155.0 2.7 %copy-start.5 = (bf16[4,2,4,64,128]{4,3,2,1,0:T(8,128)(2,1)S(1)}, bf16[4,2,4,64,128]{4,3,2,1,0:T(8,128)(2,1)}, u32[]{:S(2)}) copy-start(bf16[4,2,4,64,128]{4,3,2,1,0:T(8,128)(2,1)} %get-tuple-element.535) | copy-start | bytes 1572868 | tf_op jit(solution)/shard_map/while
  155.1 4.2 %copy-start = (f32[32,64,256]{2,0,1:T(8,128)S(1)}, f32[32,64,256]{2,0,1:T(8,128)}, u32[]{:S(2)}) copy-start(f32[32,64,256]{2,0,1:T(8,128)} %get-tuple-element.516) | copy-start | bytes 6291460 | tf_op jit(solution)/shard_map/while
  161.2 1.3 copy-start.1
  162.6 2.5 %copy-start.7 = (bf16[4,2,4,64,128]{4,3,2,1,0:T(8,128)(2,1)S(1)}, bf16[4,2,4,64,128]{4,3,2,1,0:T(8,128)(2,1)}, u32[]{:S(2)}) copy-start(bf16[4,2,4,64,128]{4,3,2,1,0:T(8,128)(2,1)} %get-tuple-element.532) | copy-start | bytes 1572868 | tf_op jit(solution)/shard_map/while
  162.6 2.7 %copy-start.5 = (bf16[4,2,4,64,128]{4,3,2,1,0:T(8,128)(2,1)S(1)}, bf16[4,2,4,64,128]{4,3,2,1,0:T(8,128)(2,1)}, u32[]{:S(2)}) copy-start(bf16[4,2,4,64,128]{4,3,2,1,0:T(8,128)(2,1)} %get-tuple-element.535) | copy-start | bytes 1572868 | tf_op jit(solution)/shard_map/while
  162.7 4.2 %copy-start = (f32[32,64,256]{2,0,1:T(8,128)S(1)}, f32[32,64,256]{2,0,1:T(8,128)}, u32[]{:S(2)}) copy-start(f32[32,64,256]{2,0,1:T(8,128)} %get-tuple-element.516) | copy-start | bytes 6291460 | tf_op jit(solution)/shard_map/while
  168.8 1.3 copy-start.1
  179.9 17.6 %copy-start.14 = (s32[16]{0:T(128)S(1)}, s32[16]{0:T(128)}, u32[]{:S(2)}) copy-start(s32[16]{0:T(128)} %copy-done.13) | copy-start | bytes 196
  179.9 17.6 %copy-start.2 = (f32[32,64,256]{2,0,1:T(8,128)S(1)}, f32[32,64,256]{2,0,1:T(8,128)}, u32[]{:S(2)}) copy-start(f32[32,64,256]{2,0,1:T(8,128)} %get-tuple-element.132) | copy-start | bytes 6291460
Sparse Core Ops, SparseCore 0:
  180.0 43.6 reduce-scatter.1
where the time goes:
time: 233 us
  matrix products  96.2 us (41%)
  local copies, waits for them, and re-layouts  48.9 us (21%)
  waiting for transfers between devices  31.7 us (14%)
  blocking collectives  17.4 us (7%)
  between operations  14.4 us (6%)
  other arithmetic  12.3 us (5%)
  starting transfers between devices  10.8 us (5%)
    dot_general x9, matrix products, add_units(): jnp.dot(selector, rows.reshape(flat_index.shape[0], -1), preferred_elemen...  42.7 us
    while x64, local copies, waits for them, and re-layouts  27.4 us
    reduce_scatter x1, waiting for transfers between devices, per_device(): lax.psum_scatter(lax.dot_general(query_rows, w_query, (((1,), (1,)), ((),...  23.1 us
    all_to_all x1, blocking collectives, per_device(): lax.all_to_all(pool_grads[unit_count:].reshape(shard_count, CAP, block_si...  17.4 us
    dot_general x8, matrix products, step(): jnp.einsum('gbqd,gbksd->gbqks', partial_gradient, value_part, preferred_e...  9.48 us
    dot_general x8, matrix products, step(): jnp.einsum('gbqks,gbqd->gbksd', reduced_probabilities, partial_gradient,...  9.03 us
    dot_general x8, matrix products, step(): jnp.einsum('gbqks,gbksd->gbqd', score_gradient, key_part, preferred_eleme...  8.56 us
    dot_general x8, matrix products, step(): jnp.einsum('gbqd,gbksd->gbqks', query_slice, key_part, preferred_element_...  8.24 us
  transfers between devices with their start and end apart: 3, of which 3 were waited for; matrix products, arithmetic and copies ran while one was open for 6% of the time, Pallas kernels for 0%

commit v1 on v0

v1 whole, which is shorter than its diff:
```python
import functools

import jax
import jax.numpy as jnp
from jax import lax
from jax.experimental import pallas as pl
from jax.experimental.pallas import tpu as pltpu
from jax.sharding import PartitionSpec as P

CAP = 2
LANES = 128
FAR = 1e30
NONE = 1 << 20

VMEM = pl.BlockSpec(memory_space=pltpu.VMEM)
SMEM = pl.BlockSpec(memory_space=pltpu.SMEM)


def dot_nt(a, b, precision=None):
    return lax.dot_general(
        a, b, (((1,), (1,)), ((), ())), preferred_element_type=jnp.float32, precision=precision
    )


def dot_nn(a, b):
    return lax.dot_general(a, b, (((1,), (0,)), ((), ())), preferred_element_type=jnp.float32)


def dot_tn(a, b):
    return lax.dot_general(a, b, (((0,), (0,)), ((), ())), preferred_element_type=jnp.float32)


def index_kernel(shards, selected_ref, wanted_ref, bits_ref):
    head_count, block_count, pick_count = selected_ref.shape
    width = bits_ref.shape[1]
    me = lax.axis_index("seq")
    lane = lax.broadcasted_iota(jnp.int32, (block_count, width), 1)
    weight = jnp.left_shift(1, lax.broadcasted_iota(jnp.int32, (block_count, width), 0))
    for head in range(head_count):
        rows = selected_ref[head]
        hits = jnp.zeros((block_count, width), jnp.int32)
        for pick in range(pick_count):
            hits = jnp.where(rows[:, pick : pick + 1] == lane, weight, hits)
        bits_ref[head : head + 1, :] = jnp.sum(hits, axis=0, keepdims=True)
    bits = bits_ref[...]
    lane = lax.broadcasted_iota(jnp.int32, (head_count, width), 1)
    label = lax.broadcasted_iota(jnp.int32, (head_count, width), 0) * block_count + lax.rem(
        lane, block_count
    )
    label = jnp.where((bits > 0) & (lax.div(lane, block_count) != me), label, NONE)
    owner_lane = lax.div(lax.broadcasted_iota(jnp.int32, (shards, width), 1), block_count)
    mine = owner_lane == lax.broadcasted_iota(jnp.int32, (shards, width), 0)
    column = lax.broadcasted_iota(jnp.int32, (shards, LANES), 1)
    wanted = jnp.full((shards, LANES), -1, jnp.int32)
    for slot in range(CAP):
        lowest = jnp.min(label, axis=0, keepdims=True)
        slot_value = jnp.min(jnp.where(mine, lowest, NONE), axis=1, keepdims=True)
        wanted = jnp.where((column == slot) & (slot_value < NONE), slot_value, wanted)
        taken = jnp.min(jnp.where(mine, slot_value, NONE), axis=0, keepdims=True)
        label = jnp.where(label == taken, NONE, label)
    for owner in range(shards):
        wanted_ref[owner] = wanted[owner : owner + 1, :]


def gather_kernel(block_count, incoming_ref, keys_ref, values_ref, out_ref):
    shards = incoming_ref.shape[0]
    head_size = out_ref.shape[2] // 2
    block_size = out_ref.shape[1] // CAP

    def owner_step(owner, carry):
        for slot in range(CAP):
            unit = jnp.maximum(incoming_ref[owner, 0, slot], 0)
            head = lax.div(unit, block_count)
            block = lax.rem(unit, block_count)
            rows = pl.ds(pl.multiple_of(block * block_size, block_size), block_size)
            lanes = pl.ds(pl.multiple_of(head * head_size, head_size), head_size)
            place = slice(slot * block_size, (slot + 1) * block_size)
            out_ref[owner, place, :head_size] = keys_ref[rows, lanes]
            out_ref[owner, place, head_size:] = values_ref[rows, lanes]
        return carry

    lax.fori_loop(0, shards, owner_step, 0, unroll=2)


def own_kernel(
    block_count,
    bits_ref,
    q_ref,
    k_ref,
    v_ref,
    o_ref,
    do_ref,
    lse_ref,
    dq_ref,
    dk_ref,
    dv_ref,
    delta_ref,
):
    tokens, head_size = q_ref.shape
    block_size = tokens // block_count
    scale = head_size ** (-0.5)
    head = pl.program_id(0)
    first = lax.axis_index("seq") * block_count
    q = q_ref[...]
    k = k_ref[...]
    v = v_ref[...]
    do = do_ref[...]
    product = do.astype(jnp.float32) * o_ref[...].astype(jnp.float32)
    ones = jnp.ones((8, head_size), jnp.float32)
    delta = dot_nt(ones, product, lax.Precision.HIGHEST)[:1]
    delta_ref[pl.ds(head, 1), :] = delta
    log_row = lse_ref[pl.ds(head, 1), :]
    lane_block = lax.div(lax.broadcasted_iota(jnp.int32, (1, tokens), 1), block_size)
    rows = []
    for block in range(block_count):
        bits = bits_ref[head, first + block]
        chosen = jnp.bitwise_and(jnp.right_shift(bits, lane_block), 1) == 1
        rows.append(
            jnp.broadcast_to(jnp.where(chosen, log_row, jnp.float32(FAR)), (block_size, tokens))
        )
    shift = jnp.concatenate(rows, axis=0)
    causal = lax.broadcasted_iota(jnp.int32, (tokens, tokens), 0) <= lax.broadcasted_iota(
        jnp.int32, (tokens, tokens), 1
    )
    scores = dot_nt(k, q) * scale
    probs = jnp.where(causal, jnp.exp(scores - shift), jnp.float32(0.0))
    dprobs = dot_nt(v, do)
    dscores = (probs * (dprobs - delta)).astype(jnp.bfloat16)
    dv_ref[...] = dot_nn(probs.astype(jnp.bfloat16), do)
    dk_ref[...] = dot_nn(dscores, q) * scale
    dq_ref[...] = dot_tn(dscores, k)


def pulled_kernel(
    block_count,
    wanted_ref,
    bits_ref,
    pulled_ref,
    q_ref,
    do_ref,
    lse_ref,
    delta_ref,
    own_dq_ref,
    far_ref,
    near_ref,
    grads_ref,
    dq_ref,
):
    tokens = q_ref.shape[0]
    head_size = pulled_ref.shape[2] // 2
    block_size = pulled_ref.shape[1] // CAP
    scale = head_size ** (-0.5)
    lane_block = lax.div(lax.broadcasted_iota(jnp.int32, (1, tokens), 1), block_size)
    dq_ref[...] = own_dq_ref[...]

    def owner_step(owner, carry):
        for slot in range(CAP):
            unit = wanted_ref[owner, 0, slot]
            safe = jnp.maximum(unit, 0)
            head = lax.div(safe, block_count)
            block = lax.rem(safe, block_count)
            bits = jnp.where(unit >= 0, bits_ref[head, owner * block_count + block], 0)
            lanes = pl.ds(pl.multiple_of(head * head_size, head_size), head_size)
            place = slice(slot * block_size, (slot + 1) * block_size)
            q = q_ref[:, lanes]
            do = do_ref[:, lanes]
            k = pulled_ref[owner, place, :head_size]
            v = pulled_ref[owner, place, head_size:]
            chosen = jnp.bitwise_and(jnp.right_shift(bits, lane_block), 1) == 1
            shift = jnp.where(chosen, lse_ref[pl.ds(head, 1), :], jnp.float32(FAR))
            probs = jnp.exp(dot_nt(k, q) * scale - shift)
            dprobs = dot_nt(v, do)
            dscores = (probs * (dprobs - delta_ref[pl.ds(head, 1), :])).astype(jnp.bfloat16)
            grads_ref[owner, place, :head_size] = (dot_nn(dscores, q) * scale).astype(
                grads_ref.dtype
            )
            grads_ref[owner, place, head_size:] = dot_nn(probs.astype(jnp.bfloat16), do).astype(
                grads_ref.dtype
            )
            dq_ref[:, lanes] += dot_tn(dscores, k)
        return carry

    lax.fori_loop(0, lax.axis_index("seq"), owner_step, 0)
    part = near_ref.shape[0] // 2
    here = lax.axis_index("head")
    for ref, offset, place in ((far_ref, 3, 0), (far_ref, 2, 1), (near_ref, 1, 0), (near_ref, 0, 1)):
        start = pl.multiple_of(jnp.bitwise_xor(here, offset) * part, part)
        ref[place * part : (place + 1) * part, :] = (dq_ref[pl.ds(start, part), :] * scale).astype(
            ref.dtype
        )


def finish_kernel(
    block_count, incoming_ref, returned_ref, own_dk_ref, own_dv_ref, dk_out, dv_out, dk_ref, dv_ref
):
    shards = incoming_ref.shape[0]
    head_size = returned_ref.shape[2] // 2
    block_size = returned_ref.shape[1] // CAP
    dk_ref[...] = own_dk_ref[...]
    dv_ref[...] = own_dv_ref[...]

    def owner_step(owner, carry):
        for slot in range(CAP):
            unit = incoming_ref[owner, 0, slot]

            @pl.when(unit >= 0)
            def _():
                head = lax.div(unit, block_count)
                block = lax.rem(unit, block_count)
                rows = pl.ds(pl.multiple_of(block * block_size, block_size), block_size)
                lanes = pl.ds(pl.multiple_of(head * head_size, head_size), head_size)
                place = slice(slot * block_size, (slot + 1) * block_size)
                dk_ref[rows, lanes] += returned_ref[owner, place, :head_size].astype(jnp.float32)
                dv_ref[rows, lanes] += returned_ref[owner, place, head_size:].astype(jnp.float32)

        return carry

    lax.fori_loop(lax.axis_index("seq") + 1, shards, owner_step, 0)
    dk_out[...] = dk_ref[...].astype(dk_out.dtype)
    dv_out[...] = dv_ref[...].astype(dv_out.dtype)


def per_device(queries, keys, values, outputs, out_grad, log_sum, selected, w_query):
    tokens, row_width = queries.shape
    head_count, block_count, pick_count = selected.shape
    head_size = row_width // head_count
    block_size = tokens // block_count
    shards = lax.axis_size("seq")
    groups = lax.axis_size("head")
    assert groups == 4
    width = pl.cdiv(shards * block_count, LANES) * LANES
    f32 = jnp.float32
    bf16 = jnp.bfloat16
    shape = jax.ShapeDtypeStruct

    def params(mib):
        return pltpu.CompilerParams(vmem_limit_bytes=mib << 20)

    def cost(flops, moved):
        return pl.CostEstimate(flops=flops, bytes_accessed=moved, transcendentals=0)

    wanted, bits = pl.pallas_call(
        functools.partial(index_kernel, shards),
        out_shape=(
            shape((shards, 1, LANES), jnp.int32),
            shape((head_count, width), jnp.int32),
        ),
        in_specs=[VMEM],
        out_specs=(VMEM, VMEM),
        compiler_params=params(4),
        name="index",
    )(selected)
    incoming = lax.all_to_all(wanted, "seq", split_axis=0, concat_axis=0, tiled=True)
    exchange = (shards, CAP * block_size, 2 * head_size)
    outgoing = pl.pallas_call(
        functools.partial(gather_kernel, block_count),
        out_shape=shape(exchange, bf16),
        in_specs=[SMEM, VMEM, VMEM],
        out_specs=VMEM,
        compiler_params=params(12),
        name="gather",
    )(incoming, keys, values)
    pulled = lax.all_to_all(outgoing, "seq", split_axis=0, concat_axis=0, tiled=True)

    column = pl.BlockSpec((tokens, head_size), lambda h: (0, h))
    whole = pl.BlockSpec((head_count, tokens), lambda h: (0, 0))
    unit_flops = 10 * tokens * block_size * head_size
    own_dq, own_dk, own_dv, delta = pl.pallas_call(
        functools.partial(own_kernel, block_count),
        grid=(head_count,),
        out_shape=(
            shape((tokens, row_width), f32),
            shape((tokens, row_width), f32),
            shape((tokens, row_width), f32),
            shape((head_count, tokens), f32),
        ),
        in_specs=[SMEM, column, column, column, column, column, whole],
        out_specs=(column, column, column, whole),
        compiler_params=params(12),
        cost_estimate=cost(
            8 * unit_flops * head_count * block_count, 22 * tokens * row_width
        ),
        name="own",
    )(bits, queries, keys, values, outputs, out_grad, log_sum)

    far, near, grads = pl.pallas_call(
        functools.partial(pulled_kernel, block_count),
        out_shape=(
            shape((tokens // 2, row_width), bf16),
            shape((tokens // 2, row_width), bf16),
            shape(exchange, bf16),
        ),
        in_specs=[SMEM, SMEM] + [VMEM] * 6,
        out_specs=(VMEM, VMEM, VMEM),
        scratch_shapes=[pltpu.VMEM((tokens, row_width), f32)],
        compiler_params=params(24),
        cost_estimate=cost(unit_flops * shards * CAP, 10 * tokens * row_width),
        name="pulled",
    )(wanted, bits, pulled, queries, out_grad, log_sum, delta, own_dq)

    returned = lax.all_to_all(grads, "seq", split_axis=0, concat_axis=0, tiled=True)
    key_gradient, value_gradient = pl.pallas_call(
        functools.partial(finish_kernel, block_count),
        out_shape=(shape((tokens, row_width), bf16), shape((tokens, row_width), bf16)),
        in_specs=[SMEM, VMEM, VMEM, VMEM],
        out_specs=(VMEM, VMEM),
        scratch_shapes=[pltpu.VMEM((tokens, row_width), f32)] * 2,
        compiler_params=params(16),
        name="finish",
    )(incoming, returned, own_dk, own_dv)

    part = tokens // groups
    beside = [(i, i ^ 1) for i in range(groups)]
    across = [(i, i ^ 2) for i in range(groups)]
    far_rows = dot_nt(far, w_query).astype(bf16)
    far_got = lax.ppermute(far_rows[:part], "head", beside)
    far_sum = (far_rows[part:].astype(f32) + far_got.astype(f32)).astype(bf16)
    across_got = lax.ppermute(far_sum, "head", across)
    near_rows = dot_nt(near, w_query)
    near_got = lax.ppermute(near_rows[:part].astype(bf16), "head", beside)
    x_grad = (near_rows[part:] + near_got.astype(f32) + across_got.astype(f32)).astype(bf16)
    return (x_grad, key_gradient, value_gradient)


def solution(mesh):
    return jax.shard_map(
        per_device,
        mesh=mesh,
        in_specs=(
            P("seq", "head"),
            P("seq", "head"),
            P("seq", "head"),
            P("seq", "head"),
            P("seq", "head"),
            P("head", "seq"),
            P("head", "seq", None),
            P(None, "head"),
        ),
        out_specs=(P(("seq", "head"), None), P("seq", "head"), P("seq", "head")),
        check_vma=False,
    )
```

time: 233 us -> 80.2 us (0.34)
  matrix products: 96.2 us -> 9.27 us
  local copies, waits for them, and re-layouts: 48.9 us -> 14.4 us
  waiting for transfers between devices: 31.7 us -> 10.7 us
  between operations: 14.4 us -> 0.78 us
  Pallas kernels: 0 us -> 11.5 us
  other arithmetic: 12.3 us -> 3.23 us
  starting transfers between devices: 10.8 us -> 15.9 us
  blocking collectives: 17.4 us -> 13.6 us
    dot_general x59 -> x2, matrix products: 96.2 us -> 9.27 us  [dot_nt(): lax.dot_general(a, b, (((1,), (1,)), ((), ())), preferred_element_type=jn...]
    while x64 -> x0, local copies, waits for them, and re-layouts: 27.4 us -> none
    reduce_scatter x1 -> x0, waiting for transfers between devices: 23.1 us -> none  [per_device(): lax.psum_scatter(lax.dot_general(query_rows, w_query, (((1,), (1,)), ((),...]
    pallas_call x0 -> x5, Pallas kernels: none -> 11.5 us  [the longest x1 6.56 us: per_device(): pl.pallas_call(functools.partial(own_kernel, block_count), grid=(head_cou...]
    ppermute x0 -> x3, waiting for transfers between devices: none -> 10.7 us  [the longest x1 10.7 us: per_device(): across_got = lax.ppermute(far_sum, 'head', across)]
    unnamed x28 -> x38, local copies, waits for them, and re-layouts: 6.12 us -> 13.4 us
    all_to_all x1, waiting for transfers between devices: 5.56 us -> 0.01 us  [per_device(): lax.all_to_all(outgoing, 'seq', split_axis=0, concat_axis=0, tiled=True)]
    concatenate x10 -> x0, other arithmetic: 5.22 us -> none  [the longest x8 3.82 us: step(): jnp.concatenate((key_gradient, value_gradient), axis=-1)]
  transfers between devices with their start and end apart: 3 -> 5, of which waited for: 3 -> 1; matrix products, arithmetic and copies ran while one was open for 6% -> 14% of each run, Pallas kernels for 0% -> 11%
where the time goes in v1:
time: 80.2 us; the launch traced here: 79.3 us
  starting transfers between devices  15.9 us (20%)
  local copies, waits for them, and re-layouts  14.4 us (18%)
  blocking collectives  13.6 us (17%)
  Pallas kernels  11.5 us (14%)
  waiting for transfers between devices  10.7 us (13%)
  matrix products  9.27 us (12%)
  other arithmetic  3.23 us (4%)
    all_to_all x1, blocking collectives, per_device(): lax.all_to_all(wanted, 'seq', split_axis=0, concat_axis=0, tiled=True)  13.6 us
    unnamed x38, local copies, waits for them, and re-layouts  13.4 us
    ppermute x1, waiting for transfers between devices, per_device(): across_got = lax.ppermute(far_sum, 'head', across)  10.7 us
    all_to_all x1, starting transfers between devices, per_device(): lax.all_to_all(grads, 'seq', split_axis=0, concat_axis=0, tiled=True)  10.3 us
    dot_general x2, matrix products, dot_nt(): lax.dot_general(a, b, (((1,), (1,)), ((), ())), preferred_element_type=jn...  9.27 us
    pallas_call x1, Pallas kernels, per_device(): pl.pallas_call(functools.partial(own_kernel, block_count), grid=(head_cou...  6.56 us
    all_to_all x1, starting transfers between devices, per_device(): lax.all_to_all(outgoing, 'seq', split_axis=0, concat_axis=0, tiled=True)  3.49 us
    convert_element_type x1, other arithmetic, per_device(): (near_rows[part:] + near_got.astype(f32) + across_got.astype(f32)).astype...  2.31 us
  transfers between devices with their start and end apart: 5, of which 1 were waited for; matrix products, arithmetic and copies ran while one was open for 14% of the time, Pallas kernels for 11%

profile of v1, /device:TPU:0, one launch (start us, length us, event | category | flops | bytes accessed | tf_op | source)
XLA Modules:
  0.0 79.3 jit_solution(10569281508192997209)
XLA Ops:
  0.6 0.0 copy-start.13
  0.6 0.7 copy-done.13
  1.3 0.6 index.1
  1.9 13.6 %all_to_all.15.incoming_ref = s32[8,1,128]{2,1,0:T(1,128)S(1)} all-to-all(s32[8,1,128]{2,1,0:T(1,128)S(1)} %get-tuple-element.14.wanted_ref), channel_id=1, replica_groups=mesh['seq'=8,'head'=4] {'seq'}, dimensions={0} | all-to-all | bytes 8192 | tf_op jit(solution)/shard_map/all_to_all | solution.py:253
  15.5 0.0 copy-start.2
  15.5 1.0 %copy-done.2 = bf16[256,1024]{1,0:T(8,128)(2,1)S(1)} copy-done((bf16[256,1024]{1,0:T(8,128)(2,1)S(1)}, bf16[256,1024]{1,0:T(8,128)(2,1)}, u32[]{:S(2)}) %copy-start.2) | copy-done | bytes 524312
  16.5 0.0 copy-start.4
  16.5 1.0 %copy-done.4 = bf16[256,1024]{1,0:T(8,128)(2,1)S(1)} copy-done((bf16[256,1024]{1,0:T(8,128)(2,1)S(1)}, bf16[256,1024]{1,0:T(8,128)(2,1)}, u32[]{:S(2)}) %copy-start.4) | copy-done | bytes 524312
  17.6 1.6 %gather.1 = bf16[8,128,256]{2,1,0:T(8,128)(2,1)} custom-call(s32[8,1,128]{2,1,0:T(1,128)S(1)} %all_to_all.15.incoming_ref, bf16[256,1024]{1,0:T(8,128)(2,1)S(1)} %copy-done.2, bf16[256,1024]{1,0:T(8,128)(2,1)S(1)} %copy-done.4), custom_call_target="tpu_custom_call" | custom-call | tf_op jit(solution)/shard_map/gather/pallas_call | solution.py:255
  19.1 3.5 %all-to-all-start.1 = ((bf16[8,128,256]{2,1,0:T(8,128)(2,1)}), bf16[8,128,256]{2,1,0:T(8,128)(2,1)S(1)}, u32[]{:S(2)}, u32[]{:S(2)}) async-start(bf16[8,128,256]{2,1,0:T(8,128)(2,1)} %gather.1), calls=%async_computation.1 | async-start | bytes 1048576 | tf_op jit(solution)/shard_map/all_to_all | solution.py:263
  22.6 0.0 copy-start.3
  22.7 1.0 %copy-done.3 = bf16[256,1024]{1,0:T(8,128)(2,1)S(1)} copy-done((bf16[256,1024]{1,0:T(8,128)(2,1)S(1)}, bf16[256,1024]{1,0:T(8,128)(2,1)}, u32[]{:S(2)}) %copy-start.3) | copy-done | bytes 524312
  23.7 0.0 copy-start.5
  23.7 1.0 %copy-done.5 = bf16[256,1024]{1,0:T(8,128)(2,1)S(1)} copy-done((bf16[256,1024]{1,0:T(8,128)(2,1)S(1)}, bf16[256,1024]{1,0:T(8,128)(2,1)}, u32[]{:S(2)}) %copy-start.5) | copy-done | bytes 524312
  24.7 0.0 copy-start.6
  24.7 1.0 %copy-done.6 = bf16[256,1024]{1,0:T(8,128)(2,1)S(1)} copy-done((bf16[256,1024]{1,0:T(8,128)(2,1)S(1)}, bf16[256,1024]{1,0:T(8,128)(2,1)}, u32[]{:S(2)}) %copy-start.6) | copy-done | bytes 524312
  25.8 0.0 copy-start.8
  25.8 1.0 %copy-done.8 = bf16[256,1024]{1,0:T(8,128)(2,1)S(1)} copy-done((bf16[256,1024]{1,0:T(8,128)(2,1)S(1)}, bf16[256,1024]{1,0:T(8,128)(2,1)}, u32[]{:S(2)}) %copy-start.8) | copy-done | bytes 524312
  26.8 0.0 copy-start.14
  26.8 0.7 copy-done.14
  27.5 0.0 copy-start.16
  27.5 1.0 %copy-done.16 = bf16[256,1024]{1,0:T(8,128)(2,1)S(1)} copy-done((bf16[256,1024]{1,0:T(8,128)(2,1)S(1)}, bf16[256,1024]{1,0:T(8,128)(2,1)}, u32[]{:S(2)}) %copy-start.16) | copy-done | bytes 524312
  28.6 0.0 copy-start.7
  28.6 0.0 copy-start.15
  28.6 6.6 %own.1 = (f32[256,1024]{1,0:T(8,128)S(1)}, f32[256,1024]{1,0:T(8,128)S(1)}, f32[256,1024]{1,0:T(8,128)S(1)}, f32[8,256]{1,0:T(8,128)S(1)}) custom-call(s32[8,128]{1,0:T(8,128)S(1)} %get-tuple-element.15.bits_ref, bf16[256,1024]{1,0:T(8,128)(2,1)S(1)} %copy-done.6, bf16[256,1024]{1,0:T(8,128)(2,1)S(1)} %copy-done.3, bf16[256,1024]{1,0:T(8,128)(2,1)S(1)} %copy-done.5, ...), custom_call_target="tpu_custom_call" | custom-call | flops 5368709120 | bytes 5767168 | tf_op jit(solution)/shard_map/own/pallas_call | solution.py:268
  35.1 0.0 copy-start
  35.1 1.0 %copy-done = f32[256,1024]{1,0:T(8,128)} copy-done((f32[256,1024]{1,0:T(8,128)}, f32[256,1024]{1,0:T(8,128)S(1)}, u32[]{:S(2)}) %copy-start) | copy-done | bytes 1048600
  36.1 0.0 all-to-all-done.1.pulled_ref
  36.1 0.0 copy-done.7
  36.1 0.0 copy-done.15
  36.1 0.0 copy-start.1
  36.1 1.2 %copy-done.1 = f32[256,1024]{1,0:T(8,128)S(1)} copy-done((f32[256,1024]{1,0:T(8,128)S(1)}, f32[256,1024]{1,0:T(8,128)}, u32[]{:S(2)}) %copy-start.1) | copy-done | bytes 1048600
  37.4 0.0 copy-start.9
  37.4 1.0 %copy-done.9 = bf16[256,1024]{1,0:T(8,128)(2,1)S(1)} copy-done((bf16[256,1024]{1,0:T(8,128)(2,1)S(1)}, bf16[256,1024]{1,0:T(8,128)(2,1)}, u32[]{:S(2)}) %copy-start.9) | copy-done | bytes 524312
  38.4 0.8 %pulled.1 = (bf16[128,1024]{1,0:T(8,128)(2,1)S(1)}, bf16[128,1024]{1,0:T(8,128)(2,1)S(1)}, bf16[8,128,256]{2,1,0:T(8,128)(2,1)S(1)}) custom-call(s32[8,1,128]{2,1,0:T(1,128)S(1)} %get-tuple-element.14.wanted_ref, s32[8,128]{1,0:T(8,128)S(1)} %get-tuple-element.15.bits_ref, bf16[8,128,256]{2,1,0:T(8,128)(2,1)S(1)} %all-to-all-done.1.pulled_ref, ...), custom_call_target="tpu_custom_call" | custom-call | flops 335544320 | bytes 2621440 | tf_op jit(solution)/shard_map/pulled/pallas_call | solution.py:286
  39.2 0.0 copy-start.10
  39.2 0.8 copy-done.10
  40.0 0.0 copy-start.11
  40.0 0.7 copy-done.11
  40.7 0.0 copy-start.12
  40.7 10.3 %all-to-all-start.2 = ((bf16[8,128,256]{2,1,0:T(8,128)(2,1)}), bf16[8,128,256]{2,1,0:T(8,128)(2,1)S(1)}, u32[]{:S(2)}, u32[]{:S(2)}) async-start(bf16[8,128,256]{2,1,0:T(8,128)(2,1)} %copy-done.10), calls=%async_computation.2 | async-start | bytes 1048576 | tf_op jit(solution)/shard_map/all_to_all | solution.py:301
  51.1 0.0 copy-start.17
  51.1 6.4 %convolution_convert_fusion = bf16[128,4096]{1,0:T(8,128)(2,1)S(1)} fusion(bf16[128,1024]{1,0:T(8,128)(2,1)S(1)} %get-tuple-element.19, bf16[4096,1024]{1,0:T(8,128)(2,1)} %param.15), kind=kOutput, calls=%fused_computation | convolution fusion | flops 1074266112 | bytes 9699328 | tf_op jit(solution)/shard_map/dot_general | solution.py:20
  57.5 0.1 collective-permute-start.1
  57.6 0.0 copy-done.12
  57.6 0.0 copy-done.17
  57.6 2.9 %fusion.2 = f32[128,4096]{1,0:T(8,128)S(1)} fusion(bf16[128,1024]{1,0:T(8,128)(2,1)S(1)} %copy-done.12, bf16[4096,1024]{1,0:T(8,128)(2,1)S(1)} %copy-done.17), kind=kOutput, calls=%fused_computation.6 | convolution fusion | flops 1073741824 | bytes 10747904 | tf_op jit(solution)/shard_map/dot_general | solution.py:20
  60.5 0.0 copy-start.18
  60.5 0.9 %slice.28 = bf16[64,4096]{1,0:T(8,128)(2,1)} slice(f32[128,4096]{1,0:T(8,128)S(1)} %fusion.2), slice={[0:64], [0:4096]} | slice | bytes 1048576 | tf_op jit(solution)/shard_map/slice | solution.py:320
  61.4 0.5 collective-permute-start
  61.9 0.0 collective-permute-done.1
  61.9 0.9 %add_convert_fusion = bf16[64,4096]{1,0:T(8,128)(2,1)} fusion(bf16[64,4096]{1,0:T(8,128)(2,1)S(1)} %collective-permute-done.1, bf16[128,4096]{1,0:T(8,128)(2,1)S(1)} %convolution_convert_fusion), kind=kLoop, calls=%fused_computation.5 | loop fusion | flops 1048576 | bytes 1572864 | tf_op jit(solution)/shard_map/convert_element_type | solution.py:317
  62.8 0.0 copy-done.18
  62.8 1.5 %collective-permute-start.2 = (bf16[64,4096]{1,0:T(8,128)(2,1)}, bf16[64,4096]{1,0:T(8,128)(2,1)}, u32[]{:S(2)}, u32[]{:S(2)}) collective-permute-start(bf16[64,4096]{1,0:T(8,128)(2,1)} %add_convert_fusion), channel_id=1, source_target_pairs={{0,2},{1,3},{2,0},{3,1},{4,6},{5,7},{6,4},{7,5},{8,10},{9,11},{10,... | collective-permute-start | bytes 1572872 | tf_op jit(solution)/shard_map/ppermute | solution.py:318
  64.3 0.0 all-to-all-done.2.returned_ref
  64.3 2.0 %finish.1 = (bf16[256,1024]{1,0:T(8,128)(2,1)}, bf16[256,1024]{1,0:T(8,128)(2,1)}) custom-call(s32[8,1,128]{2,1,0:T(1,128)S(1)} %all_to_all.15.incoming_ref, bf16[8,128,256]{2,1,0:T(8,128)(2,1)S(1)} %all-to-all-done.2.returned_ref, f32[256,1024]{1,0:T(8,128)S(1)} %get-tuple-element.21.own_dk_ref, f32[256,1024]{1,0:T(8,128)S(1)} %get-tuple-element.22.own_dv_ref), custom_call_target="tpu_custom_call" | custom-call | tf_op jit(solution)/shard_map/finish/pallas_call | solution.py:302
  66.3 0.0 collective-permute-done
  66.3 10.7 %collective-permute-done.2 = bf16[64,4096]{1,0:T(8,128)(2,1)} collective-permute-done((bf16[64,4096]{1,0:T(8,128)(2,1)}, bf16[64,4096]{1,0:T(8,128)(2,1)}, u32[]{:S(2)}, u32[]{:S(2)}) %collective-permute-start.2) | collective-permute-done | bytes 524320 | tf_op jit(solution)/shard_map/ppermute | solution.py:318
  77.0 2.3 %fusion.1 = bf16[64,4096]{1,0:T(8,128)(2,1)} fusion(f32[128,4096]{1,0:T(8,128)} %copy-done.18, bf16[64,4096]{1,0:T(8,128)(2,1)} %collective-permute-done.2, bf16[64,4096]{1,0:T(8,128)(2,1)S(1)} %collective-permute-done), kind=kLoop, calls=%fused_computation.4 | loop fusion | flops 1310720 | bytes 2621440 | tf_op jit(solution)/shard_map/convert_element_type | solution.py:321
  (1 shorter events, 0.0 us)
Async XLA Ops:
  0.6 0.7 copy-start.13
  15.5 1.0 %copy-start.2 = (bf16[256,1024]{1,0:T(8,128)(2,1)S(1)}, bf16[256,1024]{1,0:T(8,128)(2,1)}, u32[]{:S(2)}) copy-start(bf16[256,1024]{1,0:T(8,128)(2,1)} %k_ref.1) | copy-start | bytes 1572868
  16.5 1.0 %copy-start.4 = (bf16[256,1024]{1,0:T(8,128)(2,1)S(1)}, bf16[256,1024]{1,0:T(8,128)(2,1)}, u32[]{:S(2)}) copy-start(bf16[256,1024]{1,0:T(8,128)(2,1)} %v_ref.1) | copy-start | bytes 1572868
  19.1 17.0 %all-to-all-start.1 = ((bf16[8,128,256]{2,1,0:T(8,128)(2,1)}), bf16[8,128,256]{2,1,0:T(8,128)(2,1)S(1)}, u32[]{:S(2)}, u32[]{:S(2)}) async-start(bf16[8,128,256]{2,1,0:T(8,128)(2,1)} %gather.1), calls=%async_computation.1 | async-start | bytes 1048576 | tf_op jit(solution)/shard_map/all_to_all | solution.py:263
  22.6 1.0 %copy-start.3 = (bf16[256,1024]{1,0:T(8,128)(2,1)S(1)}, bf16[256,1024]{1,0:T(8,128)(2,1)}, u32[]{:S(2)}) copy-start(bf16[256,1024]{1,0:T(8,128)(2,1)} %k_ref.1) | copy-start | bytes 1572868
  23.7 1.0 %copy-start.5 = (bf16[256,1024]{1,0:T(8,128)(2,1)S(1)}, bf16[256,1024]{1,0:T(8,128)(2,1)}, u32[]{:S(2)}) copy-start(bf16[256,1024]{1,0:T(8,128)(2,1)} %v_ref.1) | copy-start | bytes 1572868
  24.7 1.0 %copy-start.6 = (bf16[256,1024]{1,0:T(8,128)(2,1)S(1)}, bf16[256,1024]{1,0:T(8,128)(2,1)}, u32[]{:S(2)}) copy-start(bf16[256,1024]{1,0:T(8,128)(2,1)} %q_ref.3) | copy-start | bytes 1572868
  25.8 1.0 %copy-start.8 = (bf16[256,1024]{1,0:T(8,128)(2,1)S(1)}, bf16[256,1024]{1,0:T(8,128)(2,1)}, u32[]{:S(2)}) copy-start(bf16[256,1024]{1,0:T(8,128)(2,1)} %do_ref.3) | copy-start | bytes 1572868
  26.8 0.7 copy-start.14
  27.5 1.0 %copy-start.16 = (bf16[256,1024]{1,0:T(8,128)(2,1)S(1)}, bf16[256,1024]{1,0:T(8,128)(2,1)}, u32[]{:S(2)}) copy-start(bf16[256,1024]{1,0:T(8,128)(2,1)} %o_ref.1) | copy-start | bytes 1572868
  28.6 7.6 %copy-start.7 = (bf16[256,1024]{1,0:T(8,128)(2,1)S(1)}, bf16[256,1024]{1,0:T(8,128)(2,1)}, u32[]{:S(2)}) copy-start(bf16[256,1024]{1,0:T(8,128)(2,1)} %q_ref.3) | copy-start | bytes 1572868
  28.6 7.6 %copy-start.15 = (f32[8,256]{1,0:T(8,128)S(1)}, f32[8,256]{1,0:T(8,128)}, u32[]{:S(2)}) copy-start(f32[8,256]{1,0:T(8,128)} %lse_ref.3) | copy-start | bytes 24580
  35.1 1.0 %copy-start = (f32[256,1024]{1,0:T(8,128)}, f32[256,1024]{1,0:T(8,128)S(1)}, u32[]{:S(2)}) copy-start(f32[256,1024]{1,0:T(8,128)S(1)} %get-tuple-element.17.own_dq_ref) | copy-start | bytes 3145732
  36.1 1.2 %copy-start.1 = (f32[256,1024]{1,0:T(8,128)S(1)}, f32[256,1024]{1,0:T(8,128)}, u32[]{:S(2)}) copy-start(f32[256,1024]{1,0:T(8,128)} %copy-done) | copy-start | bytes 3145732
  37.4 1.0 %copy-start.9 = (bf16[256,1024]{1,0:T(8,128)(2,1)S(1)}, bf16[256,1024]{1,0:T(8,128)(2,1)}, u32[]{:S(2)}) copy-start(bf16[256,1024]{1,0:T(8,128)(2,1)} %do_ref.3) | copy-start | bytes 1572868
  39.2 0.8 %copy-start.10 = (bf16[8,128,256]{2,1,0:T(8,128)(2,1)}, bf16[8,128,256]{2,1,0:T(8,128)(2,1)S(1)}, u32[]{:S(2)}) copy-start(bf16[8,128,256]{2,1,0:T(8,128)(2,1)S(1)} %get-tuple-element.20) | copy-start | bytes 1572868
  40.0 0.7 copy-start.11
  40.7 16.9 %copy-start.12 = (bf16[128,1024]{1,0:T(8,128)(2,1)S(1)}, bf16[128,1024]{1,0:T(8,128)(2,1)}, u32[]{:S(2)}) copy-start(bf16[128,1024]{1,0:T(8,128)(2,1)} %copy-done.11) | copy-start | bytes 786436
  40.7 23.6 %all-to-all-start.2 = ((bf16[8,128,256]{2,1,0:T(8,128)(2,1)}), bf16[8,128,256]{2,1,0:T(8,128)(2,1)S(1)}, u32[]{:S(2)}, u32[]{:S(2)}) async-start(bf16[8,128,256]{2,1,0:T(8,128)(2,1)} %copy-done.10), calls=%async_computation.2 | async-start | bytes 1048576 | tf_op jit(solution)/shard_map/all_to_all | solution.py:301
  51.1 6.5 %copy-start.17 = (bf16[4096,1024]{1,0:T(8,128)(2,1)S(1)}, bf16[4096,1024]{1,0:T(8,128)(2,1)}, u32[]{:S(2)}) copy-start(bf16[4096,1024]{1,0:T(8,128)(2,1)} %param.15) | copy-start | bytes 25165828
  57.5 4.4 %collective-permute-start.1 = (bf16[64,4096]{1,0:T(8,128)(2,1)S(1)}, bf16[64,4096]{1,0:T(8,128)(2,1)S(1)}, u32[]{:S(2)}, u32[]{:S(2)}) collective-permute-start(bf16[64,4096]{1,0:T(8,128)(2,1)S(1)} %slice.20), channel_id=1, source_target_pairs={{0,1},{1,0},{2,3},{3,2},{4,5},{5,4},{6,7},{7,6},{8,9},{9,8},{10,11... | collective-permute-start | bytes 1572872 | tf_op jit(solution)/shard_map/ppermute | solution.py:316
  60.5 2.3 %copy-start.18 = (f32[128,4096]{1,0:T(8,128)}, f32[128,4096]{1,0:T(8,128)S(1)}, u32[]{:S(2)}) copy-start(f32[128,4096]{1,0:T(8,128)S(1)} %fusion.2) | copy-start | bytes 6291460
  61.4 4.9 %collective-permute-start = (bf16[64,4096]{1,0:T(8,128)(2,1)}, bf16[64,4096]{1,0:T(8,128)(2,1)S(1)}, u32[]{:S(2)}, u32[]{:S(2)}) collective-permute-start(bf16[64,4096]{1,0:T(8,128)(2,1)} %slice.28), channel_id=1, source_target_pairs={{0,1},{1,0},{2,3},{3,2},{4,5},{5,4},{6,7},{7,6},{8,9},{9,8},{10,11... | collective-permute-start | bytes 1572872 | tf_op jit(solution)/shard_map/ppermute | solution.py:320
  62.8 14.2 %collective-permute-start.2 = (bf16[64,4096]{1,0:T(8,128)(2,1)}, bf16[64,4096]{1,0:T(8,128)(2,1)}, u32[]{:S(2)}, u32[]{:S(2)}) collective-permute-start(bf16[64,4096]{1,0:T(8,128)(2,1)} %add_convert_fusion), channel_id=1, source_target_pairs={{0,2},{1,3},{2,0},{3,1},{4,6},{5,7},{6,4},{7,5},{8,10},{9,11},{10,... | collective-permute-start | bytes 1572872 | tf_op jit(solution)/shard_map/ppermute | solution.py:318

commit v2 on v1

v2 whole, which is shorter than its diff:
```python
import functools

import jax
import jax.numpy as jnp
from jax import lax
from jax.experimental import pallas as pl
from jax.experimental.pallas import tpu as pltpu
from jax.sharding import PartitionSpec as P

CAP = 2
LANES = 128
FAR = 1e30
NONE = 1 << 20
VMEM_BYTES = 67043328
VMEM_SPARE = 256 << 10

VMEM = pl.BlockSpec(memory_space=pltpu.VMEM)
SMEM = pl.BlockSpec(memory_space=pltpu.SMEM)
HBM = pl.BlockSpec(memory_space=pltpu.HBM)


def dot_nt(a, b, precision=None):
    return lax.dot_general(
        a, b, (((1,), (1,)), ((), ())), preferred_element_type=jnp.float32, precision=precision
    )


def dot_nn(a, b):
    return lax.dot_general(a, b, (((1,), (0,)), ((), ())), preferred_element_type=jnp.float32)


def dot_tn(a, b):
    return lax.dot_general(a, b, (((0,), (0,)), ((), ())), preferred_element_type=jnp.float32)


def index_kernel(shards, selected_ref, wanted_ref, bits_ref):
    head_count, block_count, pick_count = selected_ref.shape
    width = bits_ref.shape[1]
    me = lax.axis_index("seq")
    lane = lax.broadcasted_iota(jnp.int32, (block_count, width), 1)
    weight = jnp.left_shift(1, lax.broadcasted_iota(jnp.int32, (block_count, width), 0))
    for head in range(head_count):
        rows = selected_ref[head]
        hits = jnp.zeros((block_count, width), jnp.int32)
        for pick in range(pick_count):
            hits = jnp.where(rows[:, pick : pick + 1] == lane, weight, hits)
        bits_ref[head : head + 1, :] = jnp.sum(hits, axis=0, keepdims=True)
    bits = bits_ref[...]
    lane = lax.broadcasted_iota(jnp.int32, (head_count, width), 1)
    label = lax.broadcasted_iota(jnp.int32, (head_count, width), 0) * block_count + lax.rem(
        lane, block_count
    )
    label = jnp.where((bits > 0) & (lax.div(lane, block_count) != me), label, NONE)
    owner_lane = lax.div(lax.broadcasted_iota(jnp.int32, (shards, width), 1), block_count)
    mine = owner_lane == lax.broadcasted_iota(jnp.int32, (shards, width), 0)
    column = lax.broadcasted_iota(jnp.int32, (shards, LANES), 1)
    wanted = jnp.full((shards, LANES), -1, jnp.int32)
    for slot in range(CAP):
        lowest = jnp.min(label, axis=0, keepdims=True)
        slot_value = jnp.min(jnp.where(mine, lowest, NONE), axis=1, keepdims=True)
        wanted = jnp.where((column == slot) & (slot_value < NONE), slot_value, wanted)
        taken = jnp.min(jnp.where(mine, slot_value, NONE), axis=0, keepdims=True)
        label = jnp.where(label == taken, NONE, label)
    for owner in range(shards):
        wanted_ref[owner] = wanted[owner : owner + 1, :]


def gather_kernel(block_count, incoming_ref, keys_ref, values_ref, out_ref, held_ref, in_sems, out_sems):
    shards = incoming_ref.shape[0]
    head_size = out_ref.shape[2] // 2
    block_size = out_ref.shape[1] // CAP

    def fetch(owner, carry):
        for slot in range(CAP):
            unit = jnp.maximum(incoming_ref[owner, 0, slot], 0)
            head = lax.div(unit, block_count)
            block = lax.rem(unit, block_count)
            rows = pl.ds(pl.multiple_of(block * block_size, block_size), block_size)
            lanes = pl.ds(pl.multiple_of(head * head_size, head_size), head_size)
            place = slice(slot * block_size, (slot + 1) * block_size)
            for ref, half in ((keys_ref, 0), (values_ref, 1)):
                pltpu.make_async_copy(
                    ref.at[rows, lanes],
                    held_ref.at[owner, place, half * head_size : (half + 1) * head_size],
                    in_sems.at[owner],
                ).start()
        return carry

    def forward(owner, carry):
        pltpu.make_async_copy(out_ref.at[owner], held_ref.at[owner], in_sems.at[owner]).wait()
        pltpu.make_async_copy(held_ref.at[owner], out_ref.at[owner], out_sems.at[owner]).start()
        return carry

    def drain(owner, carry):
        pltpu.make_async_copy(held_ref.at[owner], out_ref.at[owner], out_sems.at[owner]).wait()
        return carry

    lax.fori_loop(0, shards, fetch, 0)
    lax.fori_loop(0, shards, forward, 0)
    lax.fori_loop(0, shards, drain, 0)


def own_kernel(
    block_count,
    bits_ref,
    q_hbm,
    k_hbm,
    v_hbm,
    o_hbm,
    do_hbm,
    lse_hbm,
    dq_hbm,
    dk_hbm,
    dv_hbm,
    delta_ref,
    lse_ref,
    in_ref,
    out_ref,
    lse_sem,
    in_sems,
    out_sems,
):
    head_count, tokens = delta_ref.shape
    head_size = q_hbm.shape[1] // head_count
    block_size = tokens // block_count
    scale = head_size ** (-0.5)
    first = lax.axis_index("seq") * block_count

    def lanes(head):
        return pl.ds(pl.multiple_of(head * head_size, head_size), head_size)

    def load(head, at):
        source = (q_hbm, k_hbm, v_hbm, o_hbm, do_hbm)[at]
        return pltpu.make_async_copy(
            source.at[:, lanes(head)], in_ref.at[at, :, lanes(head)], in_sems.at[at, head]
        )

    def store(head, at):
        target = (dq_hbm, dk_hbm, dv_hbm)[at]
        return pltpu.make_async_copy(
            out_ref.at[at, :, lanes(head)], target.at[:, lanes(head)], out_sems.at[at, head]
        )

    load_lse = pltpu.make_async_copy(lse_hbm, lse_ref, lse_sem)
    load_lse.start()

    def begin(head, carry):
        for at in range(5):
            load(head, at).start()
        return carry

    lax.fori_loop(0, head_count, begin, 0)
    load_lse.wait()
    lane_block = lax.div(lax.broadcasted_iota(jnp.int32, (1, tokens), 1), block_size)
    causal = lax.broadcasted_iota(jnp.int32, (tokens, tokens), 0) <= lax.broadcasted_iota(
        jnp.int32, (tokens, tokens), 1
    )
    ones = jnp.ones((8, head_size), jnp.float32)

    def head_step(head, carry):
        for at in range(5):
            load(head, at).wait()
        q, k, v, o, do = (in_ref[at, :, lanes(head)] for at in range(5))
        product = do.astype(jnp.float32) * o.astype(jnp.float32)
        delta = dot_nt(ones, product, lax.Precision.HIGHEST)[:1]
        delta_ref[pl.ds(head, 1), :] = delta
        log_row = lse_ref[pl.ds(head, 1), :]
        rows = []
        for block in range(block_count):
            bits = bits_ref[head, first + block]
            chosen = jnp.bitwise_and(jnp.right_shift(bits, lane_block), 1) == 1
            rows.append(
                jnp.broadcast_to(jnp.where(chosen, log_row, jnp.float32(FAR)), (block_size, tokens))
            )
        shift = jnp.concatenate(rows, axis=0)
        scores = dot_nt(k, q) * scale
        probs = jnp.where(causal, jnp.exp(scores - shift), jnp.float32(0.0))
        dprobs = dot_nt(v, do)
        dscores = (probs * (dprobs - delta)).astype(jnp.bfloat16)
        out_ref[2, :, lanes(head)] = dot_nn(probs.astype(jnp.bfloat16), do)
        out_ref[1, :, lanes(head)] = dot_nn(dscores, q) * scale
        out_ref[0, :, lanes(head)] = dot_tn(dscores, k)
        for at in range(3):
            store(head, at).start()
        return carry

    lax.fori_loop(0, head_count, head_step, 0)

    def end(head, carry):
        for at in range(3):
            store(head, at).wait()
        return carry

    lax.fori_loop(0, head_count, end, 0)


def pulled_kernel(
    block_count,
    wanted_ref,
    bits_ref,
    pulled_hbm,
    q_hbm,
    do_hbm,
    lse_hbm,
    delta_hbm,
    own_dq_hbm,
    w_hbm,
    send_ref,
    keep_ref,
    near_ref,
    grads_hbm,
    pulled_ref,
    q_ref,
    do_ref,
    lse_ref,
    delta_ref,
    dq_ref,
    w_ref,
    grads_ref,
    rows_ref,
    in_sems,
    w_sems,
    out_sem,
):
    tokens = q_ref.shape[0]
    head_size = pulled_ref.shape[2] // 2
    block_size = pulled_ref.shape[1] // CAP
    scale = head_size ** (-0.5)
    loads = [
        pltpu.make_async_copy(source, target, in_sems.at[at])
        for at, (source, target) in enumerate(
            (
                (q_hbm, q_ref),
                (do_hbm, do_ref),
                (pulled_hbm, pulled_ref),
                (lse_hbm, lse_ref),
                (delta_hbm, delta_ref),
                (own_dq_hbm, dq_ref),
            )
        )
    ]
    chunks = w_sems.shape[0]
    chunk = w_ref.shape[0] // chunks

    def load_w(at):
        rows = pl.ds(pl.multiple_of(at * chunk, chunk), chunk)
        return pltpu.make_async_copy(w_hbm.at[rows], w_ref.at[rows], w_sems.at[at])

    for load in loads:
        load.start()
    for at in range(chunks):
        load_w(at).start()
    for load in loads:
        load.wait()
    lane_block = lax.div(lax.broadcasted_iota(jnp.int32, (1, tokens), 1), block_size)

    def owner_step(step, carry):
        sums = []
        for owner in (step * 2, step * 2 + 1):
            for slot in range(CAP):
                unit = wanted_ref[owner, 0, slot]
                safe = jnp.maximum(unit, 0)
                head = lax.div(safe, block_count)
                block = lax.rem(safe, block_count)
                bits = jnp.where(unit >= 0, bits_ref[head, owner * block_count + block], 0)
                lanes = pl.ds(pl.multiple_of(head * head_size, head_size), head_size)
                place = slice(slot * block_size, (slot + 1) * block_size)
                q = q_ref[:, lanes]
                do = do_ref[:, lanes]
                k = pulled_ref[owner, place, :head_size]
                v = pulled_ref[owner, place, head_size:]
                chosen = jnp.bitwise_and(jnp.right_shift(bits, lane_block), 1) == 1
                shift = jnp.where(chosen, lse_ref[pl.ds(head, 1), :], jnp.float32(FAR))
                probs = jnp.exp(dot_nt(k, q) * scale - shift)
                dprobs = dot_nt(v, do)
                dscores = (probs * (dprobs - delta_ref[pl.ds(head, 1), :])).astype(jnp.bfloat16)
                grads_ref[owner, place, :head_size] = (dot_nn(dscores, q) * scale).astype(
                    grads_ref.dtype
                )
                grads_ref[owner, place, head_size:] = dot_nn(
                    probs.astype(jnp.bfloat16), do
                ).astype(grads_ref.dtype)
                sums.append((lanes, dot_tn(dscores, k)))
        for lanes, value in sums:
            dq_ref[:, lanes] += value
        return carry

    lax.fori_loop(0, lax.div(lax.axis_index("seq") + 1, 2), owner_step, 0)
    store = pltpu.make_async_copy(grads_ref, grads_hbm, out_sem)
    store.start()
    part = near_ref.shape[0] // 2
    here = lax.axis_index("head")
    for ref, offset, place in (
        (rows_ref, 3, 0),
        (rows_ref, 2, 1),
        (near_ref, 1, 0),
        (near_ref, 0, 1),
    ):
        start = pl.multiple_of(jnp.bitwise_xor(here, offset) * part, part)
        ref[place * part : (place + 1) * part, :] = (dq_ref[pl.ds(start, part), :] * scale).astype(
            ref.dtype
        )
    for at in range(chunks):
        load_w(at).wait()
        columns = slice(at * chunk, (at + 1) * chunk)
        product = dot_nt(rows_ref[...], w_ref[columns, :]).astype(send_ref.dtype)
        send_ref[:, columns] = product[:part]
        keep_ref[:, columns] = product[part:]
    store.wait()


def near_kernel(rows_ref, w_ref, send_ref, keep_ref):
    part = send_ref.shape[0]
    product = dot_nt(rows_ref[...], w_ref[...])
    send_ref[...] = product[:part].astype(send_ref.dtype)
    keep_ref[...] = product[part:].astype(keep_ref.dtype)


def finish_kernel(
    block_count,
    incoming_ref,
    returned_hbm,
    own_dk_hbm,
    own_dv_hbm,
    dk_out,
    dv_out,
    returned_ref,
    dk_ref,
    dv_ref,
    sems,
):
    shards = incoming_ref.shape[0]
    head_size = returned_ref.shape[2] // 2
    block_size = returned_ref.shape[1] // CAP
    loads = [
        pltpu.make_async_copy(source, target, sems.at[at])
        for at, (source, target) in enumerate(
            ((returned_hbm, returned_ref), (own_dk_hbm, dk_ref), (own_dv_hbm, dv_ref))
        )
    ]
    for load in loads:
        load.start()
    for load in loads:
        load.wait()

    def owner_step(owner, carry):
        for slot in range(CAP):
            unit = incoming_ref[owner, 0, slot]

            @pl.when(unit >= 0)
            def _():
                head = lax.div(unit, block_count)
                block = lax.rem(unit, block_count)
                rows = pl.ds(pl.multiple_of(block * block_size, block_size), block_size)
                lanes = pl.ds(pl.multiple_of(head * head_size, head_size), head_size)
                place = slice(slot * block_size, (slot + 1) * block_size)
                dk_ref[rows, lanes] += returned_ref[owner, place, :head_size].astype(jnp.float32)
                dv_ref[rows, lanes] += returned_ref[owner, place, head_size:].astype(jnp.float32)

        return carry

    lax.fori_loop(lax.axis_index("seq") + 1, shards, owner_step, 0)
    dk_out[...] = dk_ref[...].astype(dk_out.dtype)
    dv_out[...] = dv_ref[...].astype(dv_out.dtype)


def per_device(queries, keys, values, outputs, out_grad, log_sum, selected, w_query):
    tokens, row_width = queries.shape
    head_count, block_count, pick_count = selected.shape
    head_size = row_width // head_count
    block_size = tokens // block_count
    shards = lax.axis_size("seq")
    groups = lax.axis_size("head")
    assert groups == 4
    width = pl.cdiv(shards * block_count, LANES) * LANES
    f32 = jnp.float32
    bf16 = jnp.bfloat16
    shape = jax.ShapeDtypeStruct

    def params(spare=VMEM_SPARE):
        return pltpu.CompilerParams(vmem_limit_bytes=VMEM_BYTES - spare)

    def cost(flops, moved):
        return pl.CostEstimate(flops=flops, bytes_accessed=moved, transcendentals=0)

    wanted, bits = pl.pallas_call(
        functools.partial(index_kernel, shards),
        out_shape=(
            shape((shards, 1, LANES), jnp.int32),
            shape((head_count, width), jnp.int32),
        ),
        in_specs=[VMEM],
        out_specs=(VMEM, VMEM),
        compiler_params=params(),
        name="index",
    )(selected)
    incoming = lax.all_to_all(wanted, "seq", split_axis=0, concat_axis=0, tiled=True)
    exchange = (shards, CAP * block_size, 2 * head_size)
    outgoing = pl.pallas_call(
        functools.partial(gather_kernel, block_count),
        out_shape=shape(exchange, bf16),
        in_specs=[SMEM, HBM, HBM],
        out_specs=HBM,
        scratch_shapes=[
            pltpu.VMEM(exchange, bf16),
            pltpu.SemaphoreType.DMA((shards,)),
            pltpu.SemaphoreType.DMA((shards,)),
        ],
        compiler_params=params(),
        name="gather",
    )(incoming, keys, values)
    pulled = lax.all_to_all(outgoing, "seq", split_axis=0, concat_axis=0, tiled=True)

    unit_flops = 10 * tokens * block_size * head_size
    own_dq, own_dk, own_dv, delta = pl.pallas_call(
        functools.partial(own_kernel, block_count),
        out_shape=(
            shape((tokens, row_width), f32),
            shape((tokens, row_width), f32),
            shape((tokens, row_width), f32),
            shape((head_count, tokens), f32),
        ),
        in_specs=[SMEM] + [HBM] * 6,
        out_specs=(HBM, HBM, HBM, VMEM),
        scratch_shapes=[
            pltpu.VMEM((head_count, tokens), f32),
            pltpu.VMEM((5, tokens, row_width), bf16),
            pltpu.VMEM((3, tokens, row_width), f32),
            pltpu.SemaphoreType.DMA,
            pltpu.SemaphoreType.DMA((5, head_count)),
            pltpu.SemaphoreType.DMA((3, head_count)),
        ],
        compiler_params=params(),
        cost_estimate=cost(8 * unit_flops * head_count * block_count, 22 * tokens * row_width),
        name="own",
    )(bits, queries, keys, values, outputs, out_grad, log_sum)

    part = tokens // groups
    features = w_query.shape[0]
    chunks = 8
    far_send, far_keep, near, grads = pl.pallas_call(
        functools.partial(pulled_kernel, block_count),
        out_shape=(
            shape((part, features), bf16),
            shape((part, features), bf16),
            shape((2 * part, row_width), bf16),
            shape(exchange, bf16),
        ),
        in_specs=[SMEM, SMEM] + [HBM] * 7,
        out_specs=(VMEM, VMEM, VMEM, HBM),
        scratch_shapes=[
            pltpu.VMEM(exchange, bf16),
            pltpu.VMEM((tokens, row_width), bf16),
            pltpu.VMEM((tokens, row_width), bf16),
            pltpu.VMEM((head_count, tokens), f32),
            pltpu.VMEM((head_count, tokens), f32),
            pltpu.VMEM((tokens, row_width), f32),
            pltpu.VMEM(w_query.shape, bf16),
            pltpu.VMEM(exchange, bf16),
            pltpu.VMEM((2 * part, row_width), bf16),
            pltpu.SemaphoreType.DMA((6,)),
            pltpu.SemaphoreType.DMA((chunks,)),
            pltpu.SemaphoreType.DMA,
        ],
        compiler_params=params(),
        cost_estimate=cost(unit_flops * shards * CAP, 10 * tokens * row_width),
        name="pulled",
    )(wanted, bits, pulled, queries, out_grad, log_sum, delta, own_dq, w_query)

    beside = [(i, i ^ 1) for i in range(groups)]
    across = [(i, i ^ 2) for i in range(groups)]
    far_got = lax.ppermute(far_send, "head", beside)
    far_sum = (far_keep.astype(f32) + far_got.astype(f32)).astype(bf16)
    across_got = lax.ppermute(far_sum, "head", across)

    near_send, near_keep = pl.pallas_call(
        near_kernel,
        grid=(chunks,),
        out_shape=(shape((part, features), bf16), shape((part, features), f32)),
        in_specs=[
            pl.BlockSpec((2 * part, row_width), lambda i: (0, 0)),
            pl.BlockSpec((features // chunks, row_width), lambda i: (i, 0)),
        ],
        out_specs=(
            pl.BlockSpec((part, features // chunks), lambda i: (0, i)),
            pl.BlockSpec((part, features // chunks), lambda i: (0, i)),
        ),
        compiler_params=params(),
        cost_estimate=cost(4 * part * row_width * features, 2 * row_width * features),
        name="near",
    )(near, w_query)
    near_got = lax.ppermute(near_send, "head", beside)
    near_sum = lax.optimization_barrier(near_keep + near_got.astype(f32))

    returned = lax.all_to_all(grads, "seq", split_axis=0, concat_axis=0, tiled=True)
    key_gradient, value_gradient = pl.pallas_call(
        functools.partial(finish_kernel, block_count),
        out_shape=(shape((tokens, row_width), bf16), shape((tokens, row_width), bf16)),
        in_specs=[SMEM, HBM, HBM, HBM],
        out_specs=(VMEM, VMEM),
        scratch_shapes=[
            pltpu.VMEM(exchange, bf16),
            pltpu.VMEM((tokens, row_width), f32),
            pltpu.VMEM((tokens, row_width), f32),
            pltpu.SemaphoreType.DMA((3,)),
        ],
        compiler_params=params(),
        name="finish",
    )(incoming, returned, own_dk, own_dv)
    x_grad = (near_sum + across_got.astype(f32)).astype(bf16)
    return (x_grad, key_gradient, value_gradient)


def solution(mesh):
    return jax.shard_map(
        per_device,
        mesh=mesh,
        in_specs=(
            P("seq", "head"),
            P("seq", "head"),
            P("seq", "head"),
            P("seq", "head"),
            P("seq", "head"),
            P("head", "seq"),
            P("head", "seq", None),
            P(None, "head"),
        ),
        out_specs=(P(("seq", "head"), None), P("seq", "head"), P("seq", "head")),
        check_vma=False,
    )
```

time: 80.2 us -> 83 us (1.035)
  Pallas kernels: 11.5 us -> 35.4 us
  local copies, waits for them, and re-layouts: 14.4 us -> 0 us
  matrix products: 9.27 us -> 0 us
  other arithmetic: 3.23 us -> 6.66 us
  starting transfers between devices: 15.9 us -> 13.5 us
  waiting for transfers between devices: 10.7 us -> 12 us
    unnamed x38 -> x0, local copies, waits for them, and re-layouts: 13.4 us -> none
    pallas_call x1 -> x2, Pallas kernels: 6.56 us -> 17.2 us  [the longest x1 8.64 us: per_device(): pl.pallas_call(near_kernel, grid=(chunks,), out_shape=(shape((part, featu...]
    dot_general x2 -> x0, matrix products: 9.27 us -> none  [dot_nt(): lax.dot_general(a, b, (((1,), (1,)), ((), ())), preferred_element_type=jn...]
    pallas_call x1, Pallas kernels: 0.81 us -> 9.76 us  [per_device(): pl.pallas_call(functools.partial(pulled_kernel, block_count), out_shape=(...]
    all_to_all x1, waiting for transfers between devices: 0.01 us -> 4.77 us  [per_device(): lax.all_to_all(outgoing, 'seq', split_axis=0, concat_axis=0, tiled=True)]
    ppermute x1, waiting for transfers between devices: 10.7 us -> 6.55 us  [per_device(): across_got = lax.ppermute(far_sum, 'head', across)]
    all_to_all x1, starting transfers between devices: 10.3 us -> 7.85 us  [per_device(): lax.all_to_all(grads, 'seq', split_axis=0, concat_axis=0, tiled=True)]
    add x0 -> x1, other arithmetic: none -> 2.3 us  [per_device(): near_sum = lax.optimization_barrier(near_keep + near_got.astype(f32))]
  transfers between devices with their start and end apart: 5 -> 5, of which waited for: 1 -> 3; matrix products, arithmetic and copies ran while one was open for 14% -> 5% of each run, Pallas kernels for 11% -> 25%
where the time goes in v2:
time: 83 us; the launch traced here: 82.2 us
  Pallas kernels  35.4 us (43%)
  blocking collectives  13.9 us (17%)
  starting transfers between devices  13.5 us (16%)
  waiting for transfers between devices  12 us (14%)
  other arithmetic  6.66 us (8%)
    all_to_all x1, blocking collectives, per_device(): lax.all_to_all(wanted, 'seq', split_axis=0, concat_axis=0, tiled=True)  13.9 us
    pallas_call x1, Pallas kernels, per_device(): pl.pallas_call(functools.partial(pulled_kernel, block_count), out_shape=(...  9.76 us
    pallas_call x1, Pallas kernels, per_device(): pl.pallas_call(near_kernel, grid=(chunks,), out_shape=(shape((part, featu...  8.64 us
    pallas_call x1, Pallas kernels, per_device(): pl.pallas_call(functools.partial(own_kernel, block_count), out_shape=(sha...  8.55 us
    all_to_all x1, starting transfers between devices, per_device(): lax.all_to_all(grads, 'seq', split_axis=0, concat_axis=0, tiled=True)  7.85 us
    ppermute x1, waiting for transfers between devices, per_device(): across_got = lax.ppermute(far_sum, 'head', across)  6.55 us
    all_to_all x1, waiting for transfers between devices, per_device(): lax.all_to_all(outgoing, 'seq', split_axis=0, concat_axis=0, tiled=True)  4.77 us
    all_to_all x1, starting transfers between devices, per_device(): lax.all_to_all(outgoing, 'seq', split_axis=0, concat_axis=0, tiled=True)  4.15 us
  transfers between devices with their start and end apart: 5, of which 3 were waited for; matrix products, arithmetic and copies ran while one was open for 5% of the time, Pallas kernels for 25%

profile of v2, /device:TPU:0, one launch (start us, length us, event | category | flops | bytes accessed | tf_op | source)
XLA Modules:
  0.0 82.2 jit_solution(18141496251837361955)
XLA Ops:
  0.6 1.9 %index.1 = (s32[8,1,128]{2,1,0:T(1,128)}, s32[8,128]{1,0:T(8,128)}) custom-call(s32[8,4,16]{2,1,0:T(4,128)} %selected_ref.1), custom_call_target="tpu_custom_call" | custom-call | tf_op jit(solution)/shard_map/index/pallas_call | solution.py:386
  2.5 13.9 %all_to_all.15.incoming_ref = s32[8,1,128]{2,1,0:T(1,128)} all-to-all(s32[8,1,128]{2,1,0:T(1,128)} %get-tuple-element.17.wanted_ref), channel_id=1, replica_groups=mesh['seq'=8,'head'=4] {'seq'}, dimensions={0} | all-to-all | bytes 8192 | tf_op jit(solution)/shard_map/all_to_all | solution.py:397
  16.4 2.9 %gather.1 = bf16[8,128,256]{2,1,0:T(8,128)(2,1)} custom-call(s32[8,1,128]{2,1,0:T(1,128)} %all_to_all.15.incoming_ref, bf16[256,1024]{1,0:T(8,128)(2,1)} %k_hbm.1, bf16[256,1024]{1,0:T(8,128)(2,1)} %v_hbm.1), custom_call_target="tpu_custom_call" | custom-call | tf_op jit(solution)/shard_map/gather/pallas_call | solution.py:399
  19.3 4.2 %all-to-all-start.1 = ((bf16[8,128,256]{2,1,0:T(8,128)(2,1)}), bf16[8,128,256]{2,1,0:T(8,128)(2,1)}, u32[]{:S(2)}, u32[]{:S(2)}) async-start(bf16[8,128,256]{2,1,0:T(8,128)(2,1)} %gather.1), calls=%async_computation.1 | async-start | bytes 1048576 | tf_op jit(solution)/shard_map/all_to_all | solution.py:412
  23.5 8.5 %own.1 = (f32[256,1024]{1,0:T(8,128)}, f32[256,1024]{1,0:T(8,128)}, f32[256,1024]{1,0:T(8,128)}, f32[8,256]{1,0:T(8,128)}) custom-call(s32[8,128]{1,0:T(8,128)} %get-tuple-element.18.bits_ref, bf16[256,1024]{1,0:T(8,128)(2,1)} %q_hbm.3, bf16[256,1024]{1,0:T(8,128)(2,1)} %k_hbm.1, bf16[256,1024]{1,0:T(8,128)(2,1)} %v_hbm.1, bf16[256,1024]{1,0:T(8,128)(2,1)} %o_hbm.1, ...), custom_call_target="tpu_custom_call" | custom-call | flops 5368709120 | bytes 5767168 | tf_op jit(solution)/shard_map/own/pallas_call | solution.py:415
  32.1 4.8 %all-to-all-done.1.pulled_hbm = bf16[8,128,256]{2,1,0:T(8,128)(2,1)} async-done(((bf16[8,128,256]{2,1,0:T(8,128)(2,1)}), bf16[8,128,256]{2,1,0:T(8,128)(2,1)}, u32[]{:S(2)}, u32[]{:S(2)}) %all-to-all-start.1) | async-done | bytes 524320 | tf_op jit(solution)/shard_map/all_to_all | solution.py:412
  36.8 9.8 %pulled.1 = (bf16[64,4096]{1,0:T(8,128)(2,1)}, bf16[64,4096]{1,0:T(8,128)(2,1)}, bf16[128,1024]{1,0:T(8,128)(2,1)}, bf16[8,128,256]{2,1,0:T(8,128)(2,1)}) custom-call(s32[8,1,128]{2,1,0:T(1,128)} %get-tuple-element.17.wanted_ref, s32[8,128]{1,0:T(8,128)} %get-tuple-element.18.bits_ref, bf16[8,128,256]{2,1,0:T(8,128)(2,1)} %all-to-all-done.1.pulled_hbm, ...), custom_call_target="tpu_custom_call" | custom-call | flops 335544320 | bytes 2621440 | tf_op jit(solution)/shard_map/pulled/pallas_call | solution.py:441
  46.6 0.1 collective-permute-start.1
  46.7 7.8 %all-to-all-start.2 = ((bf16[8,128,256]{2,1,0:T(8,128)(2,1)}), bf16[8,128,256]{2,1,0:T(8,128)(2,1)}, u32[]{:S(2)}, u32[]{:S(2)}) async-start(bf16[8,128,256]{2,1,0:T(8,128)(2,1)} %get-tuple-element.26), calls=%async_computation.2 | async-start | bytes 1048576 | tf_op jit(solution)/shard_map/all_to_all | solution.py:495
  54.5 8.6 %near.1 = (bf16[64,4096]{1,0:T(8,128)(2,1)}, f32[64,4096]{1,0:T(8,128)}) custom-call(bf16[128,1024]{1,0:T(8,128)(2,1)} %get-tuple-element.21.rows_ref, bf16[4096,1024]{1,0:T(8,128)(2,1)} %w_ref.1), custom_call_target="tpu_custom_call" | custom-call | flops 1073741824 | bytes 8388608 | tf_op jit(solution)/shard_map/near/pallas_call | solution.py:476
  63.2 0.2 collective-permute-start
  63.4 0.0 collective-permute-done.1
  63.4 2.1 %add_convert_fusion.1 = bf16[64,4096]{1,0:T(8,128)(2,1)} fusion(bf16[64,4096]{1,0:T(8,128)(2,1)} %collective-permute-done.1, bf16[64,4096]{1,0:T(8,128)(2,1)} %get-tuple-element.24), kind=kLoop, calls=%fused_computation.1 | loop fusion | flops 1048576 | bytes 1572864 | tf_op jit(solution)/shard_map/convert_element_type | solution.py:473
  65.5 1.2 %collective-permute-start.2 = (bf16[64,4096]{1,0:T(8,128)(2,1)}, bf16[64,4096]{1,0:T(8,128)(2,1)}, u32[]{:S(2)}, u32[]{:S(2)}) collective-permute-start(bf16[64,4096]{1,0:T(8,128)(2,1)} %add_convert_fusion.1), channel_id=1, source_target_pairs={{0,2},{1,3},{2,0},{3,1},{4,6},{5,7},{6,4},{7,5},{8,10},{9,11},{10,... | collective-permute-start | bytes 1572872 | tf_op jit(solution)/shard_map/ppermute | solution.py:474
  66.7 0.0 collective-permute-done
  66.8 2.3 %convert_add_fusion = f32[64,4096]{1,0:T(8,128)} fusion(f32[64,4096]{1,0:T(8,128)} %get-tuple-element.22, bf16[64,4096]{1,0:T(8,128)(2,1)S(1)} %collective-permute-done), kind=kLoop, calls=%fused_computation.2 | loop fusion | flops 524288 | bytes 2621440 | tf_op jit(solution)/shard_map/add | solution.py:493
  69.1 0.7 all-to-all-done.2.returned_hbm
  69.8 3.6 %finish.1 = (bf16[256,1024]{1,0:T(8,128)(2,1)}, bf16[256,1024]{1,0:T(8,128)(2,1)}) custom-call(s32[8,1,128]{2,1,0:T(1,128)} %all_to_all.15.incoming_ref, bf16[8,128,256]{2,1,0:T(8,128)(2,1)} %all-to-all-done.2.returned_hbm, f32[256,1024]{1,0:T(8,128)} %get-tuple-element.27.own_dk_hbm, f32[256,1024]{1,0:T(8,128)} %get-tuple-element.28.own_dv_hbm), custom_call_target="tpu_custom_call" | custom-call | tf_op jit(solution)/shard_map/finish/pallas_call | solution.py:496
  73.4 6.5 %collective-permute-done.2 = bf16[64,4096]{1,0:T(8,128)(2,1)} collective-permute-done((bf16[64,4096]{1,0:T(8,128)(2,1)}, bf16[64,4096]{1,0:T(8,128)(2,1)}, u32[]{:S(2)}, u32[]{:S(2)}) %collective-permute-start.2) | collective-permute-done | bytes 524320 | tf_op jit(solution)/shard_map/ppermute | solution.py:474
  80.0 2.2 %add_convert_fusion = bf16[64,4096]{1,0:T(8,128)(2,1)} fusion(f32[64,4096]{1,0:T(8,128)} %convert_add_fusion, bf16[64,4096]{1,0:T(8,128)(2,1)} %collective-permute-done.2), kind=kLoop, calls=%fused_computation | loop fusion | flops 786432 | bytes 2097152 | tf_op jit(solution)/shard_map/convert_element_type | solution.py:510
Async XLA Ops:
  19.3 17.5 %all-to-all-start.1 = ((bf16[8,128,256]{2,1,0:T(8,128)(2,1)}), bf16[8,128,256]{2,1,0:T(8,128)(2,1)}, u32[]{:S(2)}, u32[]{:S(2)}) async-start(bf16[8,128,256]{2,1,0:T(8,128)(2,1)} %gather.1), calls=%async_computation.1 | async-start | bytes 1048576 | tf_op jit(solution)/shard_map/all_to_all | solution.py:412
  46.6 16.8 %collective-permute-start.1 = (bf16[64,4096]{1,0:T(8,128)(2,1)}, bf16[64,4096]{1,0:T(8,128)(2,1)}, u32[]{:S(2)}, u32[]{:S(2)}) collective-permute-start(bf16[64,4096]{1,0:T(8,128)(2,1)} %get-tuple-element.25), channel_id=1, source_target_pairs={{0,1},{1,0},{2,3},{3,2},{4,5},{5,4},{6,7},{7,6},{8,9},{9,8},{10,11... | collective-permute-start | bytes 1572872 | tf_op jit(solution)/shard_map/ppermute | solution.py:472
  46.7 23.1 %all-to-all-start.2 = ((bf16[8,128,256]{2,1,0:T(8,128)(2,1)}), bf16[8,128,256]{2,1,0:T(8,128)(2,1)}, u32[]{:S(2)}, u32[]{:S(2)}) async-start(bf16[8,128,256]{2,1,0:T(8,128)(2,1)} %get-tuple-element.26), calls=%async_computation.2 | async-start | bytes 1048576 | tf_op jit(solution)/shard_map/all_to_all | solution.py:495
  63.2 3.6 %collective-permute-start = (bf16[64,4096]{1,0:T(8,128)(2,1)}, bf16[64,4096]{1,0:T(8,128)(2,1)S(1)}, u32[]{:S(2)}, u32[]{:S(2)}) collective-permute-start(bf16[64,4096]{1,0:T(8,128)(2,1)} %get-tuple-element.23), channel_id=1, source_target_pairs={{0,1},{1,0},{2,3},{3,2},{4,5},{5,4},{6,7},{7,6},{8,9},{9,8},{10,11... | collective-permute-start | bytes 1572872 | tf_op jit(solution)/shard_map/ppermute | solution.py:492
  65.5 14.5 %collective-permute-start.2 = (bf16[64,4096]{1,0:T(8,128)(2,1)}, bf16[64,4096]{1,0:T(8,128)(2,1)}, u32[]{:S(2)}, u32[]{:S(2)}) collective-permute-start(bf16[64,4096]{1,0:T(8,128)(2,1)} %add_convert_fusion.1), channel_id=1, source_target_pairs={{0,2},{1,3},{2,0},{3,1},{4,6},{5,7},{6,4},{7,5},{8,10},{9,11},{10,... | collective-permute-start | bytes 1572872 | tf_op jit(solution)/shard_map/ppermute | solution.py:474

commit v3 on v2

--- a/solution.py
+++ b/solution.py
@@ -12,7 +12,7 @@
 FAR = 1e30
 NONE = 1 << 20
 VMEM_BYTES = 67043328
-VMEM_SPARE = 256 << 10
+VMEM_SPARE = 40 << 20
 
 VMEM = pl.BlockSpec(memory_space=pltpu.VMEM)
 SMEM = pl.BlockSpec(memory_space=pltpu.SMEM)
@@ -109,13 +109,18 @@
     o_hbm,
     do_hbm,
     lse_hbm,
-    dq_hbm,
+    q_ref,
+    do_ref,
+    lse_ref,
+    delta_ref,
+    dq_ref,
     dk_hbm,
     dv_hbm,
-    delta_ref,
-    lse_ref,
-    in_ref,
-    out_ref,
+    k_ref,
+    v_ref,
+    o_ref,
+    dk_ref,
+    dv_ref,
     lse_sem,
     in_sems,
     out_sems,
@@ -125,20 +130,16 @@
     block_size = tokens // block_count
     scale = head_size ** (-0.5)
     first = lax.axis_index("seq") * block_count
-
-    def lanes(head):
+    pairs = ((q_hbm, q_ref), (k_hbm, k_ref), (v_hbm, v_ref), (o_hbm, o_ref), (do_hbm, do_ref))
+
+    def columns(head):
         return pl.ds(pl.multiple_of(head * head_size, head_size), head_size)
 
     def load(head, at):
-        source = (q_hbm, k_hbm, v_hbm, o_hbm, do_hbm)[at]
+        source, target = pairs[at]
+        lanes = columns(head)
         return pltpu.make_async_copy(
-            source.at[:, lanes(head)], in_ref.at[at, :, lanes(head)], in_sems.at[at, head]
-        )
-
-    def store(head, at):
-        target = (dq_hbm, dk_hbm, dv_hbm)[at]
-        return pltpu.make_async_copy(
-            out_ref.at[at, :, lanes(head)], target.at[:, lanes(head)], out_sems.at[at, head]
+            source.at[:, lanes], target.at[:, lanes], in_sems.at[at, head]
         )
 
     load_lse = pltpu.make_async_copy(lse_hbm, lse_ref, lse_sem)
@@ -160,7 +161,8 @@
     def head_step(head, carry):
         for at in range(5):
             load(head, at).wait()
-        q, k, v, o, do = (in_ref[at, :, lanes(head)] for at in range(5))
+        lanes = columns(head)
+        q, k, v, o, do = (ref[:, lanes] for ref in (q_ref, k_ref, v_ref, o_ref, do_ref))
         product = do.astype(jnp.float32) * o.astype(jnp.float32)
         delta = dot_nt(ones, product, lax.Precision.HIGHEST)[:1]
         delta_ref[pl.ds(head, 1), :] = delta
@@ -177,82 +179,73 @@
         probs = jnp.where(causal, jnp.exp(scores - shift), jnp.float32(0.0))
         dprobs = dot_nt(v, do)
         dscores = (probs * (dprobs - delta)).astype(jnp.bfloat16)
-        out_ref[2, :, lanes(head)] = dot_nn(probs.astype(jnp.bfloat16), do)
-        out_ref[1, :, lanes(head)] = dot_nn(dscores, q) * scale
-        out_ref[0, :, lanes(head)] = dot_tn(dscores, k)
-        for at in range(3):
-            store(head, at).start()
+        dv_ref[:, lanes] = dot_nn(probs.astype(jnp.bfloat16), do)
+        dk_ref[:, lanes] = dot_nn(dscores, q) * scale
+        dq_ref[:, lanes] = dot_tn(dscores, k)
         return carry
 
     lax.fori_loop(0, head_count, head_step, 0)
-
-    def end(head, carry):
-        for at in range(3):
-            store(head, at).wait()
-        return carry
-
-    lax.fori_loop(0, head_count, end, 0)
+    stores = (
+        pltpu.make_async_copy(dk_ref, dk_hbm, out_sems.at[0]),
+        pltpu.make_async_copy(dv_ref, dv_hbm, out_sems.at[1]),
+    )
+    for store in stores:
+        store.start()
+    for store in stores:
+        store.wait()
 
 
 def pulled_kernel(
     block_count,
     wanted_ref,
     bits_ref,
-    pulled_hbm,
-    q_hbm,
-    do_hbm,
-    lse_hbm,
-    delta_hbm,
-    own_dq_hbm,
-    w_hbm,
-    send_ref,
-    keep_ref,
-    near_ref,
-    grads_hbm,
     pulled_ref,
     q_ref,
     do_ref,
     lse_ref,
     delta_ref,
+    own_dq_ref,
+    w_hbm,
+    far_send_ref,
+    far_keep_ref,
+    near_send_hbm,
+    near_keep_hbm,
+    grads_hbm,
     dq_ref,
+    rows_ref,
+    grads_ref,
     w_ref,
-    grads_ref,
-    rows_ref,
-    in_sems,
+    near_send_ref,
+    near_keep_ref,
+    out_sem,
     w_sems,
-    out_sem,
+    near_sems,
 ):
+    chunks = w_sems.shape[0]
+    chunk = w_ref.shape[0] // chunks
+
+    def load_w(at):
+        return pltpu.make_async_copy(
+            w_hbm.at[pl.ds(at * chunk, chunk)], w_ref.at[pl.ds(at * chunk, chunk)], w_sems.at[at]
+        )
+
+    def store_near(at):
+        columns = pl.ds(at * chunk, chunk)
+        return [
+            pltpu.make_async_copy(ref.at[:, columns], out.at[:, columns], near_sems.at[side, at])
+            for side, (ref, out) in enumerate(
+                ((near_send_ref, near_send_hbm), (near_keep_ref, near_keep_hbm))
+            )
+        ]
+
+    for at in range(chunks):
+        load_w(at).start()
     tokens = q_ref.shape[0]
     head_size = pulled_ref.shape[2] // 2
     block_size = pulled_ref.shape[1] // CAP
     scale = head_size ** (-0.5)
-    loads = [
-        pltpu.make_async_copy(source, target, in_sems.at[at])
-        for at, (source, target) in enumerate(
-            (
-                (q_hbm, q_ref),
-                (do_hbm, do_ref),
-                (pulled_hbm, pulled_ref),
-                (lse_hbm, lse_ref),
-                (delta_hbm, delta_ref),
-                (own_dq_hbm, dq_ref),
-            )
-        )
-    ]
-    chunks = w_sems.shape[0]
-    chunk = w_ref.shape[0] // chunks
-
-    def load_w(at):
-        rows = pl.ds(pl.multiple_of(at * chunk, chunk), chunk)
-        return pltpu.make_async_copy(w_hbm.at[rows], w_ref.at[rows], w_sems.at[at])
-
-    for load in loads:
-        load.start()
-    for at in range(chunks):
-        load_w(at).start()
-    for load in loads:
-        load.wait()
     lane_block = lax.div(lax.broadcasted_iota(jnp.int32, (1, tokens), 1), block_size)
+    dq_ref[...] = own_dq_ref[...]
 
     def owner_step(step, carry):
         sums = []
@@ -288,43 +281,36 @@
     lax.fori_loop(0, lax.div(lax.axis_index("seq") + 1, 2), owner_step, 0)
     store = pltpu.make_async_copy(grads_ref, grads_hbm, out_sem)
     store.start()
-    part = near_ref.shape[0] // 2
+    targets = (far_send_ref, far_keep_ref, near_send_ref, near_keep_ref)
+    part = far_send_ref.shape[0]
     here = lax.axis_index("head")
-    for ref, offset, place in (
-        (rows_ref, 3, 0),
-        (rows_ref, 2, 1),
-        (near_ref, 1, 0),
-        (near_ref, 0, 1),
-    ):
-        start = pl.multiple_of(jnp.bitwise_xor(here, offset) * part, part)
-        ref[place * part : (place + 1) * part, :] = (dq_ref[pl.ds(start, part), :] * scale).astype(
-            ref.dtype
-        )
+    for place in range(4):
+        start = pl.multiple_of(jnp.bitwise_xor(here, 3 - place) * part, part)
+        rows_ref[place * part : (place + 1) * part, :] = (
+            dq_ref[pl.ds(start, part), :] * scale
+        ).astype(rows_ref.dtype)
     for at in range(chunks):
         load_w(at).wait()
         columns = slice(at * chunk, (at + 1) * chunk)
-        product = dot_nt(rows_ref[...], w_ref[columns, :]).astype(send_ref.dtype)
-        send_ref[:, columns] = product[:part]
-        keep_ref[:, columns] = product[part:]
+        product = dot_nt(rows_ref[...], w_ref[columns, :])
+        for place, ref in enumerate(targets):
+            ref[:, columns] = product[place * part : (place + 1) * part].astype(ref.dtype)
+        for copy in store_near(at):
+            copy.start()
+    for at in range(chunks):
+        for copy in store_near(at):
+            copy.wait()
     store.wait()
-
-
-def near_kernel(rows_ref, w_ref, send_ref, keep_ref):
-    part = send_ref.shape[0]
-    product = dot_nt(rows_ref[...], w_ref[...])
-    send_ref[...] = product[:part].astype(send_ref.dtype)
-    keep_ref[...] = product[part:].astype(keep_ref.dtype)
 
 
 def finish_kernel(
     block_count,
     incoming_ref,
-    returned_hbm,
+    returned_ref,
     own_dk_hbm,
     own_dv_hbm,
     dk_out,
     dv_out,
-    returned_ref,
     dk_ref,
     dv_ref,
     sems,
@@ -335,7 +321,7 @@
     loads = [
         pltpu.make_async_copy(source, target, sems.at[at])
         for at, (source, target) in enumerate(
-            ((returned_hbm, returned_ref), (own_dk_hbm, dk_ref), (own_dv_hbm, dv_ref))
+            ((own_dk_hbm, dk_ref), (own_dv_hbm, dv_ref))
         )
     ]
     for load in loads:
@@ -373,6 +359,10 @@
     groups = lax.axis_size("head")
     assert groups == 4
     width = pl.cdiv(shards * block_count, LANES) * LANES
+    queries, keys, values, outputs, out_grad, log_sum, w_query = (
+        pltpu.with_memory_space_constraint(a, pltpu.HBM)
+        for a in (queries, keys, values, outputs, out_grad, log_sum, w_query)
+    )
     f32 = jnp.float32
     bf16 = jnp.bfloat16
     shape = jax.ShapeDtypeStruct
@@ -412,23 +402,28 @@
     pulled = lax.all_to_all(outgoing, "seq", split_axis=0, concat_axis=0, tiled=True)
 
     unit_flops = 10 * tokens * block_size * head_size
-    own_dq, own_dk, own_dv, delta = pl.pallas_call(
+    q_here, do_here, lse_here, delta, own_dq, own_dk, own_dv = pl.pallas_call(
         functools.partial(own_kernel, block_count),
         out_shape=(
+            shape((tokens, row_width), bf16),
+            shape((tokens, row_width), bf16),
+            shape((head_count, tokens), f32),
+            shape((head_count, tokens), f32),
             shape((tokens, row_width), f32),
-            shape((tokens, row_width), f32),
-            shape((tokens, row_width), f32),
-            shape((head_count, tokens), f32),
+            pltpu.HBM((tokens, row_width), f32),
+            pltpu.HBM((tokens, row_width), f32),
         ),
         in_specs=[SMEM] + [HBM] * 6,
-        out_specs=(HBM, HBM, HBM, VMEM),
+        out_specs=(VMEM,) * 5 + (HBM, HBM),
         scratch_shapes=[
-            pltpu.VMEM((head_count, tokens), f32),
-            pltpu.VMEM((5, tokens, row_width), bf16),
-            pltpu.VMEM((3, tokens, row_width), f32),
+            pltpu.VMEM((tokens, row_width), bf16),
+            pltpu.VMEM((tokens, row_width), bf16),
+            pltpu.VMEM((tokens, row_width), bf16),
+            pltpu.VMEM((tokens, row_width), f32),
+            pltpu.VMEM((tokens, row_width), f32),
             pltpu.SemaphoreType.DMA,
             pltpu.SemaphoreType.DMA((5, head_count)),
-            pltpu.SemaphoreType.DMA((3, head_count)),
+            pltpu.SemaphoreType.DMA((2,)),
         ],
         compiler_params=params(),
         cost_estimate=cost(8 * unit_flops * head_count * block_count, 22 * tokens * row_width),
@@ -437,35 +432,32 @@
 
     part = tokens // groups
     features = w_query.shape[0]
-    chunks = 8
-    far_send, far_keep, near, grads = pl.pallas_call(
+    far_send, far_keep, near_send, near_keep, grads = pl.pallas_call(
         functools.partial(pulled_kernel, block_count),
         out_shape=(
             shape((part, features), bf16),
             shape((part, features), bf16),
-            shape((2 * part, row_width), bf16),
-            shape(exchange, bf16),
+            pltpu.HBM((part, features), bf16),
+            pltpu.HBM((part, features), bf16),
+            pltpu.HBM(exchange, bf16),
         ),
-        in_specs=[SMEM, SMEM] + [HBM] * 7,
-        out_specs=(VMEM, VMEM, VMEM, HBM),
+        in_specs=[SMEM, SMEM] + [VMEM] * 6 + [HBM],
+        out_specs=(VMEM, VMEM, HBM, HBM, HBM),
         scratch_shapes=[
+            pltpu.VMEM((tokens, row_width), f32),
+            pltpu.VMEM((tokens, row_width), bf16),
             pltpu.VMEM(exchange, bf16),
-            pltpu.VMEM((tokens, row_width), bf16),
-            pltpu.VMEM((tokens, row_width), bf16),
-            pltpu.VMEM((head_count, tokens), f32),
-            pltpu.VMEM((head_count, tokens), f32),
-            pltpu.VMEM((tokens, row_width), f32),
             pltpu.VMEM(w_query.shape, bf16),
-            pltpu.VMEM(exchange, bf16),
-            pltpu.VMEM((2 * part, row_width), bf16),
-            pltpu.SemaphoreType.DMA((6,)),
-            pltpu.SemaphoreType.DMA((chunks,)),
+            pltpu.VMEM((part, features), bf16),
+            pltpu.VMEM((part, features), bf16),
             pltpu.SemaphoreType.DMA,
+            pltpu.SemaphoreType.DMA((8,)),
+            pltpu.SemaphoreType.DMA((2, 8)),
         ],
         compiler_params=params(),
         cost_estimate=cost(unit_flops * shards * CAP, 10 * tokens * row_width),
         name="pulled",
-    )(wanted, bits, pulled, queries, out_grad, log_sum, delta, own_dq, w_query)
+    )(wanted, bits, pulled, q_here, do_here, lse_here, delta, own_dq, w_query)
 
     beside = [(i, i ^ 1) for i in range(groups)]
     across = [(i, i ^ 2) for i in range(groups)]
@@ -473,41 +465,25 @@
     far_sum = (far_keep.astype(f32) + far_got.astype(f32)).astype(bf16)
     across_got = lax.ppermute(far_sum, "head", across)
 
-    near_send, near_keep = pl.pallas_call(
-        near_kernel,
-        grid=(chunks,),
-        out_shape=(shape((part, features), bf16), shape((part, features), f32)),
-        in_specs=[
-            pl.BlockSpec((2 * part, row_width), lambda i: (0, 0)),
-            pl.BlockSpec((features // chunks, row_width), lambda i: (i, 0)),
-        ],
-        out_specs=(
-            pl.BlockSpec((part, features // chunks), lambda i: (0, i)),
-            pl.BlockSpec((part, features // chunks), lambda i: (0, i)),
-        ),
-        compiler_params=params(),
-        cost_estimate=cost(4 * part * row_width * features, 2 * row_width * features),
-        name="near",
-    )(near, w_query)
     near_got = lax.ppermute(near_send, "head", beside)
-    near_sum = lax.optimization_barrier(near_keep + near_got.astype(f32))
-
     returned = lax.all_to_all(grads, "seq", split_axis=0, concat_axis=0, tiled=True)
+    own_dk, own_dv = (
+        pltpu.with_memory_space_constraint(a, pltpu.HBM) for a in (own_dk, own_dv)
+    )
     key_gradient, value_gradient = pl.pallas_call(
         functools.partial(finish_kernel, block_count),
         out_shape=(shape((tokens, row_width), bf16), shape((tokens, row_width), bf16)),
-        in_specs=[SMEM, HBM, HBM, HBM],
+        in_specs=[SMEM, VMEM, HBM, HBM],
         out_specs=(VMEM, VMEM),
         scratch_shapes=[
-            pltpu.VMEM(exchange, bf16),
             pltpu.VMEM((tokens, row_width), f32),
             pltpu.VMEM((tokens, row_width), f32),
-            pltpu.SemaphoreType.DMA((3,)),
+            pltpu.SemaphoreType.DMA((2,)),
         ],
         compiler_params=params(),
         name="finish",
     )(incoming, returned, own_dk, own_dv)
-    x_grad = (near_sum + across_got.astype(f32)).astype(bf16)
+    x_grad = (near_keep.astype(f32) + near_got.astype(f32) + across_got.astype(f32)).astype(bf16)
     return (x_grad, key_gradient, value_gradient)
 
 

time: 83 us -> 70.3 us (0.85)
  Pallas kernels: 35.4 us -> 22.2 us
  waiting for transfers between devices: 12 us -> 18.5 us
  other arithmetic: 6.66 us -> 2.15 us
  starting transfers between devices: 13.5 us -> 11.9 us
    all_to_all x1, waiting for transfers between devices: 0.72 us -> 13.3 us  [per_device(): lax.all_to_all(grads, 'seq', split_axis=0, concat_axis=0, tiled=True)]
    pallas_call x1 -> x0, Pallas kernels: 8.64 us -> none  [per_device(): pl.pallas_call(near_kernel, grid=(chunks,), out_shape=(shape((part, featu...]
    ppermute x1, waiting for transfers between devices: 6.55 us -> 0.01 us  [per_device(): across_got = lax.ppermute(far_sum, 'head', across)]
    add x1 -> x0, other arithmetic: 2.3 us -> none  [per_device(): near_sum = lax.optimization_barrier(near_keep + near_got.astype(f32))]
    pallas_call x1, Pallas kernels: 9.76 us -> 7.5 us  [per_device(): pl.pallas_call(functools.partial(pulled_kernel, block_count), out_shape=(...]
    convert_element_type x1, other arithmetic: 2.12 us -> 0.12 us  [per_device(): far_sum = (far_keep.astype(f32) + far_got.astype(f32)).astype(bf16)]
    pallas_call x1, Pallas kernels: 1.89 us -> 0.58 us  [per_device(): pl.pallas_call(functools.partial(index_kernel, shards), out_shape=(shape(...]
    all_to_all x1, starting transfers between devices: 7.85 us -> 6.59 us  [per_device(): lax.all_to_all(grads, 'seq', split_axis=0, concat_axis=0, tiled=True)]
  transfers between devices with their start and end apart: 5 -> 5, of which waited for: 3 -> 2; matrix products, arithmetic and copies ran while one was open for 5% -> 0% of each run, Pallas kernels for 25% -> 16%
where the time goes in v3:
time: 70.3 us; the launch traced here: 69.7 us
  Pallas kernels  22.2 us (32%)
  waiting for transfers between devices  18.5 us (26%)
  blocking collectives  13.6 us (19%)
  starting transfers between devices  11.9 us (17%)
  other arithmetic  2.15 us (3%)
  local copies, waits for them, and re-layouts  0.71 us (1%)
  between operations  0.71 us (1%)
    all_to_all x1, blocking collectives, per_device(): lax.all_to_all(wanted, 'seq', split_axis=0, concat_axis=0, tiled=True)  13.6 us
    all_to_all x1, waiting for transfers between devices, per_device(): lax.all_to_all(grads, 'seq', split_axis=0, concat_axis=0, tiled=True)  13.3 us
    pallas_call x1, Pallas kernels, per_device(): pl.pallas_call(functools.partial(own_kernel, block_count), out_shape=(sha...  8.1 us
    pallas_call x1, Pallas kernels, per_device(): pl.pallas_call(functools.partial(pulled_kernel, block_count), out_shape=(...  7.5 us
    all_to_all x1, starting transfers between devices, per_device(): lax.all_to_all(grads, 'seq', split_axis=0, concat_axis=0, tiled=True)  6.59 us
    all_to_all x1, waiting for transfers between devices, per_device(): lax.all_to_all(outgoing, 'seq', split_axis=0, concat_axis=0, tiled=True)  5.19 us
    all_to_all x1, starting transfers between devices, per_device(): lax.all_to_all(outgoing, 'seq', split_axis=0, concat_axis=0, tiled=True)  3.51 us
    pallas_call x1, Pallas kernels, per_device(): pl.pallas_call(functools.partial(finish_kernel, block_count), out_shape=(...  3.35 us
  transfers between devices with their start and end apart: 5, of which 2 were waited for; matrix products, arithmetic and copies ran while one was open for 0% of the time, Pallas kernels for 16%

profile of v3, /device:TPU:0, one launch (start us, length us, event | category | flops | bytes accessed | tf_op | source)
XLA Modules:
  0.0 69.7 jit_solution(2886387341271906155)
XLA Ops:
  0.6 0.0 copy-start
  0.6 0.7 %copy-done = s32[8,4,16]{2,1,0:T(4,128)S(1)} copy-done((s32[8,4,16]{2,1,0:T(4,128)S(1)}, s32[8,4,16]{2,1,0:T(4,128)}, u32[]{:S(2)}) %copy-start) | copy-done | bytes 2072
  1.3 0.6 index.1
  1.9 13.6 %all_to_all.15.incoming_ref = s32[8,1,128]{2,1,0:T(1,128)S(1)} all-to-all(s32[8,1,128]{2,1,0:T(1,128)S(1)} %get-tuple-element.19.wanted_ref), channel_id=1, replica_groups=mesh['seq'=8,'head'=4] {'seq'}, dimensions={0} | all-to-all | bytes 8192 | tf_op jit(solution)/shard_map/all_to_all | solution.py:387
  15.5 2.7 %gather.1 = bf16[8,128,256]{2,1,0:T(8,128)(2,1)} custom-call(s32[8,1,128]{2,1,0:T(1,128)S(1)} %all_to_all.15.incoming_ref, bf16[256,1024]{1,0:T(8,128)(2,1)} %k_hbm.1, bf16[256,1024]{1,0:T(8,128)(2,1)} %v_hbm.1), custom_call_target="tpu_custom_call" | custom-call | tf_op jit(solution)/shard_map/gather/pallas_call | solution.py:389
  18.2 3.5 %all-to-all-start.1 = ((bf16[8,128,256]{2,1,0:T(8,128)(2,1)}), bf16[8,128,256]{2,1,0:T(8,128)(2,1)S(1)}, u32[]{:S(2)}, u32[]{:S(2)}) async-start(bf16[8,128,256]{2,1,0:T(8,128)(2,1)} %gather.1), calls=%async_computation.1 | async-start | bytes 1048576 | tf_op jit(solution)/shard_map/all_to_all | solution.py:402
  21.7 8.1 %own.1 = (bf16[256,1024]{1,0:T(8,128)(2,1)S(1)}, bf16[256,1024]{1,0:T(8,128)(2,1)S(1)}, f32[8,256]{1,0:T(8,128)S(1)}, f32[8,256]{1,0:T(8,128)S(1)}, f32[256,1024...) custom-call(s32[8,128]{1,0:T(8,128)S(1)} %get-tuple-element.20.bits_ref, bf16[256,1024]{1,0:T(8,128)(2,1)} %q_hbm.1, ...), custom_call_target="tpu_custom_call" | custom-call | flops 5368709120 | bytes 5767168 | tf_op jit(solution)/shard_map/own/pallas_call | solution.py:405
  29.8 5.2 %all-to-all-done.1.pulled_ref = bf16[8,128,256]{2,1,0:T(8,128)(2,1)S(1)} async-done(((bf16[8,128,256]{2,1,0:T(8,128)(2,1)}), bf16[8,128,256]{2,1,0:T(8,128)(2,1)S(1)}, u32[]{:S(2)}, u32[]{:S(2)}) %all-to-all-start.1) | async-done | bytes 524320 | tf_op jit(solution)/shard_map/all_to_all | solution.py:402
  35.0 7.5 %pulled.1 = (bf16[64,4096]{1,0:T(8,128)(2,1)}, bf16[64,4096]{1,0:T(8,128)(2,1)S(1)}, bf16[64,4096]{1,0:T(8,128)(2,1)}, bf16[64,4096]{1,0:T(8,128)(2,1)}, bf16[8,128,256]{2,1,0:T(8,128)(2,1)}) custom-call(s32[8,1,128]{2,1,0:T(1,128)S(1)} %get-tuple-element.19.wanted_ref, s32[8,128]{1,0:T(8,128)S(1)} %get-tuple-element.20.bits_ref, ...), custom_call_target="tpu_custom_call" | custom-call | flops 335544320 | bytes 2621440 | tf_op jit(solution)/shard_map/pulled/pallas_call | solution.py:435
  42.5 0.1 collective-permute-start.1
  42.6 6.6 %all-to-all-start.2 = ((bf16[8,128,256]{2,1,0:T(8,128)(2,1)}), bf16[8,128,256]{2,1,0:T(8,128)(2,1)S(1)}, u32[]{:S(2)}, u32[]{:S(2)}) async-start(bf16[8,128,256]{2,1,0:T(8,128)(2,1)} %get-tuple-element.30), calls=%async_computation.2 | async-start | bytes 1048576 | tf_op jit(solution)/shard_map/all_to_all | solution.py:469
  49.2 0.2 collective-permute-start
  49.4 0.0 collective-permute-done.1
  49.4 0.1 add_convert_fusion.1
  49.5 1.5 %collective-permute-start.2 = (bf16[64,4096]{1,0:T(8,128)(2,1)S(1)}, bf16[64,4096]{1,0:T(8,128)(2,1)S(1)}, u32[]{:S(2)}, u32[]{:S(2)}) collective-permute-start(bf16[64,4096]{1,0:T(8,128)(2,1)S(1)} %add_convert_fusion.1), channel_id=1, source_target_pairs={{0,2},{1,3},{2,0},{3,1},{4,6},{5,7},{6,4},{7,5},{8,10},{9,11},{10,... | collective-permute-start | bytes 1572872 | tf_op jit(solution)/shard_map/ppermute | solution.py:466
  51.1 13.3 %all-to-all-done.2.returned_ref = bf16[8,128,256]{2,1,0:T(8,128)(2,1)S(1)} async-done(((bf16[8,128,256]{2,1,0:T(8,128)(2,1)}), bf16[8,128,256]{2,1,0:T(8,128)(2,1)S(1)}, u32[]{:S(2)}, u32[]{:S(2)}) %all-to-all-start.2) | async-done | bytes 524320 | tf_op jit(solution)/shard_map/all_to_all | solution.py:469
  64.3 3.4 %finish.1 = (bf16[256,1024]{1,0:T(8,128)(2,1)}, bf16[256,1024]{1,0:T(8,128)(2,1)}) custom-call(s32[8,1,128]{2,1,0:T(1,128)S(1)} %all_to_all.15.incoming_ref, bf16[8,128,256]{2,1,0:T(8,128)(2,1)S(1)} %all-to-all-done.2.returned_ref, f32[256,1024]{1,0:T(8,128)} %get-tuple-element.31.own_dk_hbm, f32[256,1024]{1,0:T(8,128)} %get-tuple-element.32.own_dv_hbm), custom_call_target="tpu_custom_call" | custom-call | tf_op jit(solution)/shard_map/finish/pallas_call | solution.py:473
  67.7 0.0 collective-permute-done
  67.7 0.0 collective-permute-done.2
  67.7 2.0 %add_convert_fusion = bf16[64,4096]{1,0:T(8,128)(2,1)} fusion(bf16[64,4096]{1,0:T(8,128)(2,1)S(1)} %collective-permute-done.2, bf16[64,4096]{1,0:T(8,128)(2,1)S(1)} %collective-permute-done, bf16[64,4096]{1,0:T(8,128)(2,1)} %get-tuple-element.26), kind=kLoop, calls=%fused_computation | loop fusion | flops 1572864 | bytes 2097152 | tf_op jit(solution)/shard_map/convert_element_type | solution.py:486
Async XLA Ops:
  0.6 0.7 %copy-start = (s32[8,4,16]{2,1,0:T(4,128)S(1)}, s32[8,4,16]{2,1,0:T(4,128)}, u32[]{:S(2)}) copy-start(s32[8,4,16]{2,1,0:T(4,128)} %selected_ref.1) | copy-start | bytes 6148
  18.2 16.8 %all-to-all-start.1 = ((bf16[8,128,256]{2,1,0:T(8,128)(2,1)}), bf16[8,128,256]{2,1,0:T(8,128)(2,1)S(1)}, u32[]{:S(2)}, u32[]{:S(2)}) async-start(bf16[8,128,256]{2,1,0:T(8,128)(2,1)} %gather.1), calls=%async_computation.1 | async-start | bytes 1048576 | tf_op jit(solution)/shard_map/all_to_all | solution.py:402
  42.5 6.9 %collective-permute-start.1 = (bf16[64,4096]{1,0:T(8,128)(2,1)}, bf16[64,4096]{1,0:T(8,128)(2,1)S(1)}, u32[]{:S(2)}, u32[]{:S(2)}) collective-permute-start(bf16[64,4096]{1,0:T(8,128)(2,1)} %get-tuple-element.29), channel_id=1, source_target_pairs={{0,1},{1,0},{2,3},{3,2},{4,5},{5,4},{6,7},{7,6},{8,9},{9,8},{10,11... | collective-permute-start | bytes 1572872 | tf_op jit(solution)/shard_map/ppermute | solution.py:464
  42.6 21.7 %all-to-all-start.2 = ((bf16[8,128,256]{2,1,0:T(8,128)(2,1)}), bf16[8,128,256]{2,1,0:T(8,128)(2,1)S(1)}, u32[]{:S(2)}, u32[]{:S(2)}) async-start(bf16[8,128,256]{2,1,0:T(8,128)(2,1)} %get-tuple-element.30), calls=%async_computation.2 | async-start | bytes 1048576 | tf_op jit(solution)/shard_map/all_to_all | solution.py:469
  49.2 18.5 %collective-permute-start = (bf16[64,4096]{1,0:T(8,128)(2,1)}, bf16[64,4096]{1,0:T(8,128)(2,1)S(1)}, u32[]{:S(2)}, u32[]{:S(2)}) collective-permute-start(bf16[64,4096]{1,0:T(8,128)(2,1)} %get-tuple-element.27), channel_id=1, source_target_pairs={{0,1},{1,0},{2,3},{3,2},{4,5},{5,4},{6,7},{7,6},{8,9},{9,8},{10,11... | collective-permute-start | bytes 1572872 | tf_op jit(solution)/shard_map/ppermute | solution.py:468
  49.5 18.2 %collective-permute-start.2 = (bf16[64,4096]{1,0:T(8,128)(2,1)S(1)}, bf16[64,4096]{1,0:T(8,128)(2,1)S(1)}, u32[]{:S(2)}, u32[]{:S(2)}) collective-permute-start(bf16[64,4096]{1,0:T(8,128)(2,1)S(1)} %add_convert_fusion.1), channel_id=1, source_target_pairs={{0,2},{1,3},{2,0},{3,1},{4,6},{5,7},{6,4},{7,5},{8,10},{9,11},{10,... | collective-permute-start | bytes 1572872 | tf_op jit(solution)/shard_map/ppermute | solution.py:466

commit v4 on v3

--- a/solution.py
+++ b/solution.py
@@ -7,7 +7,9 @@
 from jax.experimental.pallas import tpu as pltpu
 from jax.sharding import PartitionSpec as P
 
+
 CAP = 2
+UNROLL = 4
 LANES = 128
 FAR = 1e30
 NONE = 1 << 20
@@ -156,16 +158,15 @@
     causal = lax.broadcasted_iota(jnp.int32, (tokens, tokens), 0) <= lax.broadcasted_iota(
         jnp.int32, (tokens, tokens), 1
     )
-    ones = jnp.ones((8, head_size), jnp.float32)
-
-    def head_step(head, carry):
-        for at in range(5):
-            load(head, at).wait()
+    ones = jnp.ones((8, 2 * head_size), jnp.bfloat16)
+
+    def head_work(head):
         lanes = columns(head)
         q, k, v, o, do = (ref[:, lanes] for ref in (q_ref, k_ref, v_ref, o_ref, do_ref))
         product = do.astype(jnp.float32) * o.astype(jnp.float32)
-        delta = dot_nt(ones, product, lax.Precision.HIGHEST)[:1]
-        delta_ref[pl.ds(head, 1), :] = delta
+        high = product.astype(jnp.bfloat16)
+        rest = (product - high.astype(jnp.float32)).astype(jnp.bfloat16)
+        delta = dot_nt(ones, jnp.concatenate((high, rest), axis=1))[:1]
         log_row = lse_ref[pl.ds(head, 1), :]
         rows = []
         for block in range(block_count):
@@ -179,23 +180,45 @@
         probs = jnp.where(causal, jnp.exp(scores - shift), jnp.float32(0.0))
         dprobs = dot_nt(v, do)
         dscores = (probs * (dprobs - delta)).astype(jnp.bfloat16)
-        dv_ref[:, lanes] = dot_nn(probs.astype(jnp.bfloat16), do)
-        dk_ref[:, lanes] = dot_nn(dscores, q) * scale
-        dq_ref[:, lanes] = dot_tn(dscores, k)
-        return carry
-
-    lax.fori_loop(0, head_count, head_step, 0)
-    stores = (
-        pltpu.make_async_copy(dk_ref, dk_hbm, out_sems.at[0]),
-        pltpu.make_async_copy(dv_ref, dv_hbm, out_sems.at[1]),
-    )
-    for store in stores:
-        store.start()
-    for store in stores:
-        store.wait()
-
-
-def pulled_kernel(
+        dv = dot_nn(probs.astype(jnp.bfloat16), do)
+        dk = dot_nn(dscores, q) * scale
+        dq = dot_tn(dscores, k)
+        return delta, dq, dk, dv
+
+    def store(head, side):
+        ref, out = ((dk_ref, dk_hbm), (dv_ref, dv_hbm))[side]
+        lanes = columns(head)
+        return pltpu.make_async_copy(ref.at[:, lanes], out.at[:, lanes], out_sems.at[side, head])
+
+    group = 2 - head_count % 2
+
+    def head_step(step, carry):
+        heads = [step * group + at for at in range(group)]
+        for head in heads:
+            for at in range(5):
+                load(head, at).wait()
+        results = [head_work(head) for head in heads]
+        for head, (delta, dq, dk, dv) in zip(heads, results):
+            lanes = columns(head)
+            delta_ref[pl.ds(head, 1), :] = delta
+            dq_ref[:, lanes] = dq
+            dk_ref[:, lanes] = dk
+            dv_ref[:, lanes] = dv
+            for side in range(2):
+                store(head, side).start()
+        return carry
+
+    lax.fori_loop(0, head_count // group, head_step, 0)
+
+    def drain(head, carry):
+        for side in range(2):
+            store(head, side).wait()
+        return carry
+
+    lax.fori_loop(0, head_count, drain, 0)
+
+
+def units_kernel(
     block_count,
     wanted_ref,
     bits_ref,
@@ -205,51 +228,23 @@
     lse_ref,
     delta_ref,
     own_dq_ref,
-    w_hbm,
-    far_send_ref,
-    far_keep_ref,
-    near_send_hbm,
-    near_keep_hbm,
+    rows_ref,
     grads_hbm,
     dq_ref,
-    rows_ref,
     grads_ref,
-    w_ref,
-    near_send_ref,
-    near_keep_ref,
     out_sem,
-    w_sems,
-    near_sems,
 ):
-    chunks = w_sems.shape[0]
-    chunk = w_ref.shape[0] // chunks
-
-    def load_w(at):
-        return pltpu.make_async_copy(
-            w_hbm.at[pl.ds(at * chunk, chunk)], w_ref.at[pl.ds(at * chunk, chunk)], w_sems.at[at]
-        )
-
-    def store_near(at):
-        columns = pl.ds(at * chunk, chunk)
-        return [
-            pltpu.make_async_copy(ref.at[:, columns], out.at[:, columns], near_sems.at[side, at])
-            for side, (ref, out) in enumerate(
-                ((near_send_ref, near_send_hbm), (near_keep_ref, near_keep_hbm))
-            )
-        ]
-
-    for at in range(chunks):
-        load_w(at).start()
     tokens = q_ref.shape[0]
-    head_size = pulled_ref.shape[2] // 2
-    block_size = pulled_ref.shape[1] // CAP
+    head_size = grads_ref.shape[2] // 2
+    block_size = grads_ref.shape[1] // CAP
     scale = head_size ** (-0.5)
     lane_block = lax.div(lax.broadcasted_iota(jnp.int32, (1, tokens), 1), block_size)
     dq_ref[...] = own_dq_ref[...]
 
     def owner_step(step, carry):
         sums = []
-        for owner in (step * 2, step * 2 + 1):
+        for at in range(UNROLL):
+            owner = step * UNROLL + at
             for slot in range(CAP):
                 unit = wanted_ref[owner, 0, slot]
                 safe = jnp.maximum(unit, 0)
@@ -267,40 +262,46 @@
                 probs = jnp.exp(dot_nt(k, q) * scale - shift)
                 dprobs = dot_nt(v, do)
                 dscores = (probs * (dprobs - delta_ref[pl.ds(head, 1), :])).astype(jnp.bfloat16)
-                grads_ref[owner, place, :head_size] = (dot_nn(dscores, q) * scale).astype(
-                    grads_ref.dtype
-                )
-                grads_ref[owner, place, head_size:] = dot_nn(
-                    probs.astype(jnp.bfloat16), do
-                ).astype(grads_ref.dtype)
-                sums.append((lanes, dot_tn(dscores, k)))
-        for lanes, value in sums:
+                dk = (dot_nn(dscores, q) * scale).astype(grads_ref.dtype)
+                dv = dot_nn(probs.astype(jnp.bfloat16), do).astype(grads_ref.dtype)
+                sums.append((owner, place, dk, dv, lanes, dot_tn(dscores, k)))
+        for owner, place, dk, dv, lanes, value in sums:
+            grads_ref[owner, place, :head_size] = dk
+            grads_ref[owner, place, head_size:] = dv
             dq_ref[:, lanes] += value
         return carry
 
-    lax.fori_loop(0, lax.div(lax.axis_index("seq") + 1, 2), owner_step, 0)
+    lax.fori_loop(0, lax.div(lax.axis_index("seq") + UNROLL - 1, UNROLL), owner_step, 0)
     store = pltpu.make_async_copy(grads_ref, grads_hbm, out_sem)
     store.start()
-    targets = (far_send_ref, far_keep_ref, near_send_ref, near_keep_ref)
-    part = far_send_ref.shape[0]
+    part = tokens // 4
     here = lax.axis_index("head")
     for place in range(4):
         start = pl.multiple_of(jnp.bitwise_xor(here, 3 - place) * part, part)
         rows_ref[place * part : (place + 1) * part, :] = (
             dq_ref[pl.ds(start, part), :] * scale
         ).astype(rows_ref.dtype)
+    store.wait()
+
+
+def product_kernel(rows_ref, w_hbm, *refs):
+    targets, w_ref, w_sems = refs[:4], refs[4], refs[5]
+    part = targets[0].shape[0]
+    chunks = w_sems.shape[0]
+    chunk = w_ref.shape[0] // chunks
+
+    def load_w(at):
+        rows = pl.ds(at * chunk, chunk)
+        return pltpu.make_async_copy(w_hbm.at[rows], w_ref.at[rows], w_sems.at[at])
+
+    for at in range(chunks):
+        load_w(at).start()
     for at in range(chunks):
         load_w(at).wait()
         columns = slice(at * chunk, (at + 1) * chunk)
         product = dot_nt(rows_ref[...], w_ref[columns, :])
         for place, ref in enumerate(targets):
             ref[:, columns] = product[place * part : (place + 1) * part].astype(ref.dtype)
-        for copy in store_near(at):
-            copy.start()
-    for at in range(chunks):
-        for copy in store_near(at):
-            copy.wait()
-    store.wait()
 
 
 def finish_kernel(
@@ -329,9 +330,9 @@
     for load in loads:
         load.wait()
 
-    def owner_step(owner, carry):
+    def asker_step(asker, carry):
         for slot in range(CAP):
-            unit = incoming_ref[owner, 0, slot]
+            unit = incoming_ref[asker, 0, slot]
 
             @pl.when(unit >= 0)
             def _():
@@ -340,19 +341,19 @@
                 rows = pl.ds(pl.multiple_of(block * block_size, block_size), block_size)
                 lanes = pl.ds(pl.multiple_of(head * head_size, head_size), head_size)
                 place = slice(slot * block_size, (slot + 1) * block_size)
-                dk_ref[rows, lanes] += returned_ref[owner, place, :head_size].astype(jnp.float32)
-                dv_ref[rows, lanes] += returned_ref[owner, place, head_size:].astype(jnp.float32)
-
-        return carry
-
-    lax.fori_loop(lax.axis_index("seq") + 1, shards, owner_step, 0)
+                dk_ref[rows, lanes] += returned_ref[asker, place, :head_size].astype(jnp.float32)
+                dv_ref[rows, lanes] += returned_ref[asker, place, head_size:].astype(jnp.float32)
+
+        return carry
+
+    lax.fori_loop(lax.axis_index("seq") + 1, shards, asker_step, 0)
     dk_out[...] = dk_ref[...].astype(dk_out.dtype)
     dv_out[...] = dv_ref[...].astype(dv_out.dtype)
 
 
 def per_device(queries, keys, values, outputs, out_grad, log_sum, selected, w_query):
     tokens, row_width = queries.shape
-    head_count, block_count, pick_count = selected.shape
+    head_count, block_count, _ = selected.shape
     head_size = row_width // head_count
     block_size = tokens // block_count
     shards = lax.axis_size("seq")
@@ -386,6 +387,7 @@
     )(selected)
     incoming = lax.all_to_all(wanted, "seq", split_axis=0, concat_axis=0, tiled=True)
     exchange = (shards, CAP * block_size, 2 * head_size)
+    assert shards % UNROLL == 0
     outgoing = pl.pallas_call(
         functools.partial(gather_kernel, block_count),
         out_shape=shape(exchange, bf16),
@@ -423,7 +425,7 @@
             pltpu.VMEM((tokens, row_width), f32),
             pltpu.SemaphoreType.DMA,
             pltpu.SemaphoreType.DMA((5, head_count)),
-            pltpu.SemaphoreType.DMA((2,)),
+            pltpu.SemaphoreType.DMA((2, head_count)),
         ],
         compiler_params=params(),
         cost_estimate=cost(8 * unit_flops * head_count * block_count, 22 * tokens * row_width),
@@ -432,32 +434,32 @@
 
     part = tokens // groups
     features = w_query.shape[0]
-    far_send, far_keep, near_send, near_keep, grads = pl.pallas_call(
-        functools.partial(pulled_kernel, block_count),
-        out_shape=(
-            shape((part, features), bf16),
-            shape((part, features), bf16),
-            pltpu.HBM((part, features), bf16),
-            pltpu.HBM((part, features), bf16),
-            pltpu.HBM(exchange, bf16),
-        ),
-        in_specs=[SMEM, SMEM] + [VMEM] * 6 + [HBM],
-        out_specs=(VMEM, VMEM, HBM, HBM, HBM),
+    rows, grads = pl.pallas_call(
+        functools.partial(units_kernel, block_count),
+        out_shape=(shape((tokens, row_width), bf16), pltpu.HBM(exchange, bf16)),
+        in_specs=[SMEM, SMEM] + [VMEM] * 6,
+        out_specs=(VMEM, HBM),
         scratch_shapes=[
             pltpu.VMEM((tokens, row_width), f32),
-            pltpu.VMEM((tokens, row_width), bf16),
             pltpu.VMEM(exchange, bf16),
-            pltpu.VMEM(w_query.shape, bf16),
-            pltpu.VMEM((part, features), bf16),
-            pltpu.VMEM((part, features), bf16),
             pltpu.SemaphoreType.DMA,
-            pltpu.SemaphoreType.DMA((8,)),
-            pltpu.SemaphoreType.DMA((2, 8)),
         ],
         compiler_params=params(),
         cost_estimate=cost(unit_flops * shards * CAP, 10 * tokens * row_width),
-        name="pulled",
-    )(wanted, bits, pulled, q_here, do_here, lse_here, delta, own_dq, w_query)
+        name="units",
+    )(wanted, bits, pulled, q_here, do_here, lse_here, delta, own_dq)
+    returned = lax.all_to_all(grads, "seq", split_axis=0, concat_axis=0, tiled=True)
+
+    far_send, far_keep, near_send, near_keep = pl.pallas_call(
+        product_kernel,
+        out_shape=(shape((part, features), bf16),) * 4,
+        in_specs=[VMEM, HBM],
+        out_specs=(VMEM,) * 4,
+        scratch_shapes=[pltpu.VMEM(w_query.shape, bf16), pltpu.SemaphoreType.DMA((8,))],
+        compiler_params=params(),
+        cost_estimate=cost(8 * part * row_width * features, 2 * row_width * features),
+        name="product",
+    )(rows, w_query)
 
     beside = [(i, i ^ 1) for i in range(groups)]
     across = [(i, i ^ 2) for i in range(groups)]
@@ -466,7 +468,6 @@
     across_got = lax.ppermute(far_sum, "head", across)
 
     near_got = lax.ppermute(near_send, "head", beside)
-    returned = lax.all_to_all(grads, "seq", split_axis=0, concat_axis=0, tiled=True)
     own_dk, own_dv = (
         pltpu.with_memory_space_constraint(a, pltpu.HBM) for a in (own_dk, own_dv)
     )

time: 70.3 us -> 70.5 us (level)
  Pallas kernels: 22.2 us -> 19.6 us
  waiting for transfers between devices: 18.5 us -> 20.3 us
  starting transfers between devices: 11.9 us -> 12.8 us
    all_to_all x1, waiting for transfers between devices: 5.19 us -> 6.98 us  [per_device(): lax.all_to_all(outgoing, 'seq', split_axis=0, concat_axis=0, tiled=True)]
    pallas_call x1, Pallas kernels: 8.1 us -> 6.33 us  [per_device(): pl.pallas_call(functools.partial(own_kernel, block_count), out_shape=(sha...]
    all_to_all x1, starting transfers between devices: 6.59 us -> 7.49 us  [per_device(): lax.all_to_all(grads, 'seq', split_axis=0, concat_axis=0, tiled=True)]
    pallas_call x1 -> x2, Pallas kernels: 7.5 us -> 6.6 us  [the longest x1 5.07 us: per_device(): pl.pallas_call(product_kernel, out_shape=(shape((part, features), bf16),)...]
  transfers between devices with their start and end apart: 5 -> 5, of which waited for: 2 -> 2; matrix products, arithmetic and copies ran while one was open for 0% -> 0% of each run, Pallas kernels for 16% -> 14%
where the time goes in v4:
time: 70.5 us; the launch traced here: 69.8 us
  waiting for transfers between devices  20.3 us (29%)
  Pallas kernels  19.6 us (28%)
  blocking collectives  13.6 us (19%)
  starting transfers between devices  12.8 us (18%)
  other arithmetic  2.15 us (3%)
  between operations  0.72 us (1%)
  local copies, waits for them, and re-layouts  0.71 us (1%)
    all_to_all x1, blocking collectives, per_device(): lax.all_to_all(wanted, 'seq', split_axis=0, concat_axis=0, tiled=True)  13.6 us
    all_to_all x1, waiting for transfers between devices, per_device(): lax.all_to_all(grads, 'seq', split_axis=0, concat_axis=0, tiled=True)  13.3 us
    all_to_all x1, starting transfers between devices, per_device(): lax.all_to_all(grads, 'seq', split_axis=0, concat_axis=0, tiled=True)  7.49 us
    all_to_all x1, waiting for transfers between devices, per_device(): lax.all_to_all(outgoing, 'seq', split_axis=0, concat_axis=0, tiled=True)  6.98 us
    pallas_call x1, Pallas kernels, per_device(): pl.pallas_call(functools.partial(own_kernel, block_count), out_shape=(sha...  6.33 us
    pallas_call x1, Pallas kernels, per_device(): pl.pallas_call(product_kernel, out_shape=(shape((part, features), bf16),)...  5.07 us
    all_to_all x1, starting transfers between devices, per_device(): lax.all_to_all(outgoing, 'seq', split_axis=0, concat_axis=0, tiled=True)  3.51 us
    pallas_call x1, Pallas kernels, per_device(): pl.pallas_call(functools.partial(finish_kernel, block_count), out_shape=(...  3.33 us
  transfers between devices with their start and end apart: 5, of which 2 were waited for; matrix products, arithmetic and copies ran while one was open for 0% of the time, Pallas kernels for 14%

profile of v4, /device:TPU:0, one launch (start us, length us, event | category | flops | bytes accessed | tf_op | source)
XLA Modules:
  0.0 69.8 jit_solution(14689877720796367778)
XLA Ops:
  0.6 0.0 copy-start
  0.6 0.7 %copy-done = s32[8,4,16]{2,1,0:T(4,128)S(1)} copy-done((s32[8,4,16]{2,1,0:T(4,128)S(1)}, s32[8,4,16]{2,1,0:T(4,128)}, u32[]{:S(2)}) %copy-start) | copy-done | bytes 2072
  1.3 0.6 index.1
  1.9 13.6 %all_to_all.15.incoming_ref = s32[8,1,128]{2,1,0:T(1,128)S(1)} all-to-all(s32[8,1,128]{2,1,0:T(1,128)S(1)} %get-tuple-element.20.wanted_ref), channel_id=1, replica_groups=mesh['seq'=8,'head'=4] {'seq'}, dimensions={0} | all-to-all | bytes 8192 | tf_op jit(solution)/shard_map/all_to_all | solution.py:388
  15.5 2.8 %gather.1 = bf16[8,128,256]{2,1,0:T(8,128)(2,1)} custom-call(s32[8,1,128]{2,1,0:T(1,128)S(1)} %all_to_all.15.incoming_ref, bf16[256,1024]{1,0:T(8,128)(2,1)} %k_hbm.1, bf16[256,1024]{1,0:T(8,128)(2,1)} %v_hbm.1), custom_call_target="tpu_custom_call" | custom-call | tf_op jit(solution)/shard_map/gather/pallas_call | solution.py:391
  18.3 3.5 %all-to-all-start.1 = ((bf16[8,128,256]{2,1,0:T(8,128)(2,1)}), bf16[8,128,256]{2,1,0:T(8,128)(2,1)S(1)}, u32[]{:S(2)}, u32[]{:S(2)}) async-start(bf16[8,128,256]{2,1,0:T(8,128)(2,1)} %gather.1), calls=%async_computation.1 | async-start | bytes 1048576 | tf_op jit(solution)/shard_map/all_to_all | solution.py:404
  21.8 6.3 %own.1 = (bf16[256,1024]{1,0:T(8,128)(2,1)S(1)}, bf16[256,1024]{1,0:T(8,128)(2,1)S(1)}, f32[8,256]{1,0:T(8,128)S(1)}, f32[8,256]{1,0:T(8,128)S(1)}, f32[256,1024...) custom-call(s32[8,128]{1,0:T(8,128)S(1)} %get-tuple-element.21.bits_ref, bf16[256,1024]{1,0:T(8,128)(2,1)} %q_hbm.1, ...), custom_call_target="tpu_custom_call" | custom-call | flops 5368709120 | bytes 5767168 | tf_op jit(solution)/shard_map/own/pallas_call | solution.py:407
  28.1 7.0 %all-to-all-done.1.pulled_ref = bf16[8,128,256]{2,1,0:T(8,128)(2,1)S(1)} async-done(((bf16[8,128,256]{2,1,0:T(8,128)(2,1)}), bf16[8,128,256]{2,1,0:T(8,128)(2,1)S(1)}, u32[]{:S(2)}, u32[]{:S(2)}) %all-to-all-start.1) | async-done | bytes 524320 | tf_op jit(solution)/shard_map/all_to_all | solution.py:404
  35.1 1.5 %units.1 = (bf16[256,1024]{1,0:T(8,128)(2,1)S(1)}, bf16[8,128,256]{2,1,0:T(8,128)(2,1)}) custom-call(s32[8,1,128]{2,1,0:T(1,128)S(1)} %get-tuple-element.20.wanted_ref, s32[8,128]{1,0:T(8,128)S(1)} %get-tuple-element.21.bits_ref, bf16[8,128,256]{2,1,0:T(8,128)(2,1)S(1)} %all-to-all-done.1.pulled_ref, bf16[256,1024]{1,0:T(8,128)(2,1)S(1)} %get-tuple-element.22.q_ref, ...), custom_call_target="tpu_custom_call" | custom-call | flops 335544320 | bytes 2621440 | tf_op jit(solution)/shard_map/units/pallas_call | solution.py:437
  36.7 5.1 %product.1 = (bf16[64,4096]{1,0:T(8,128)(2,1)S(1)}, bf16[64,4096]{1,0:T(8,128)(2,1)S(1)}, bf16[64,4096]{1,0:T(8,128)(2,1)S(1)}, bf16[64,4096]{1,0:T(8,128)(2,1)S(1)}) custom-call(bf16[256,1024]{1,0:T(8,128)(2,1)S(1)} %get-tuple-element.27.rows_ref, bf16[4096,1024]{1,0:T(8,128)(2,1)} %w_hbm.1), custom_call_target="tpu_custom_call" | custom-call | flops 2147483648 | bytes 8388608 | tf_op jit(solution)/shard_map/product/pallas_call | solution.py:453
  41.8 0.1 collective-permute-start.1
  41.8 7.5 %all-to-all-start.2 = ((bf16[8,128,256]{2,1,0:T(8,128)(2,1)}), bf16[8,128,256]{2,1,0:T(8,128)(2,1)S(1)}, u32[]{:S(2)}, u32[]{:S(2)}) async-start(bf16[8,128,256]{2,1,0:T(8,128)(2,1)} %get-tuple-element.32), calls=%async_computation.2 | async-start | bytes 1048576 | tf_op jit(solution)/shard_map/all_to_all | solution.py:451
  49.3 0.2 collective-permute-start
  49.5 0.0 collective-permute-done.1
  49.5 0.1 add_convert_fusion.1
  49.7 1.5 %collective-permute-start.2 = (bf16[64,4096]{1,0:T(8,128)(2,1)S(1)}, bf16[64,4096]{1,0:T(8,128)(2,1)S(1)}, u32[]{:S(2)}, u32[]{:S(2)}) collective-permute-start(bf16[64,4096]{1,0:T(8,128)(2,1)S(1)} %add_convert_fusion.1), channel_id=1, source_target_pairs={{0,2},{1,3},{2,0},{3,1},{4,6},{5,7},{6,4},{7,5},{8,10},{9,11},{10,... | collective-permute-start | bytes 1572872 | tf_op jit(solution)/shard_map/ppermute | solution.py:468
  51.2 13.3 %all-to-all-done.2.returned_ref = bf16[8,128,256]{2,1,0:T(8,128)(2,1)S(1)} async-done(((bf16[8,128,256]{2,1,0:T(8,128)(2,1)}), bf16[8,128,256]{2,1,0:T(8,128)(2,1)S(1)}, u32[]{:S(2)}, u32[]{:S(2)}) %all-to-all-start.2) | async-done | bytes 524320 | tf_op jit(solution)/shard_map/all_to_all | solution.py:451
  64.5 3.3 %finish.1 = (bf16[256,1024]{1,0:T(8,128)(2,1)}, bf16[256,1024]{1,0:T(8,128)(2,1)}) custom-call(s32[8,1,128]{2,1,0:T(1,128)S(1)} %all_to_all.15.incoming_ref, bf16[8,128,256]{2,1,0:T(8,128)(2,1)S(1)} %all-to-all-done.2.returned_ref, f32[256,1024]{1,0:T(8,128)} %get-tuple-element.33.own_dk_hbm, f32[256,1024]{1,0:T(8,128)} %get-tuple-element.34.own_dv_hbm), custom_call_target="tpu_custom_call" | custom-call | tf_op jit(solution)/shard_map/finish/pallas_call | solution.py:474
  67.8 0.0 collective-permute-done
  67.8 0.0 collective-permute-done.2
  67.8 2.0 %add_convert_fusion = bf16[64,4096]{1,0:T(8,128)(2,1)} fusion(bf16[64,4096]{1,0:T(8,128)(2,1)S(1)} %collective-permute-done.2, bf16[64,4096]{1,0:T(8,128)(2,1)} %collective-permute-done, bf16[64,4096]{1,0:T(8,128)(2,1)S(1)} %get-tuple-element.28), kind=kLoop, calls=%fused_computation | loop fusion | flops 1572864 | bytes 2097152 | tf_op jit(solution)/shard_map/convert_element_type | solution.py:487
Async XLA Ops:
  0.6 0.7 %copy-start = (s32[8,4,16]{2,1,0:T(4,128)S(1)}, s32[8,4,16]{2,1,0:T(4,128)}, u32[]{:S(2)}) copy-start(s32[8,4,16]{2,1,0:T(4,128)} %selected_ref.1) | copy-start | bytes 6148
  18.3 16.8 %all-to-all-start.1 = ((bf16[8,128,256]{2,1,0:T(8,128)(2,1)}), bf16[8,128,256]{2,1,0:T(8,128)(2,1)S(1)}, u32[]{:S(2)}, u32[]{:S(2)}) async-start(bf16[8,128,256]{2,1,0:T(8,128)(2,1)} %gather.1), calls=%async_computation.1 | async-start | bytes 1048576 | tf_op jit(solution)/shard_map/all_to_all | solution.py:404
  41.8 7.8 %collective-permute-start.1 = (bf16[64,4096]{1,0:T(8,128)(2,1)S(1)}, bf16[64,4096]{1,0:T(8,128)(2,1)S(1)}, u32[]{:S(2)}, u32[]{:S(2)}) collective-permute-start(bf16[64,4096]{1,0:T(8,128)(2,1)S(1)} %get-tuple-element.31), channel_id=1, source_target_pairs={{0,1},{1,0},{2,3},{3,2},{4,5},{5,4},{6,7},{7,6},{8,9},{9,8},{10,11... | collective-permute-start | bytes 1572872 | tf_op jit(solution)/shard_map/ppermute | solution.py:466
  41.8 22.6 %all-to-all-start.2 = ((bf16[8,128,256]{2,1,0:T(8,128)(2,1)}), bf16[8,128,256]{2,1,0:T(8,128)(2,1)S(1)}, u32[]{:S(2)}, u32[]{:S(2)}) async-start(bf16[8,128,256]{2,1,0:T(8,128)(2,1)} %get-tuple-element.32), calls=%async_computation.2 | async-start | bytes 1048576 | tf_op jit(solution)/shard_map/all_to_all | solution.py:451
  49.3 18.5 %collective-permute-start = (bf16[64,4096]{1,0:T(8,128)(2,1)S(1)}, bf16[64,4096]{1,0:T(8,128)(2,1)}, u32[]{:S(2)}, u32[]{:S(2)}) collective-permute-start(bf16[64,4096]{1,0:T(8,128)(2,1)S(1)} %get-tuple-element.29), channel_id=1, source_target_pairs={{0,1},{1,0},{2,3},{3,2},{4,5},{5,4},{6,7},{7,6},{8,9},{9,8},{10,11... | collective-permute-start | bytes 1572872 | tf_op jit(solution)/shard_map/ppermute | solution.py:470
  49.7 18.1 %collective-permute-start.2 = (bf16[64,4096]{1,0:T(8,128)(2,1)S(1)}, bf16[64,4096]{1,0:T(8,128)(2,1)S(1)}, u32[]{:S(2)}, u32[]{:S(2)}) collective-permute-start(bf16[64,4096]{1,0:T(8,128)(2,1)S(1)} %add_convert_fusion.1), channel_id=1, source_target_pairs={{0,2},{1,3},{2,0},{3,1},{4,6},{5,7},{6,4},{7,5},{8,10},{9,11},{10,... | collective-permute-start | bytes 1572872 | tf_op jit(solution)/shard_map/ppermute | solution.py:468

commit v5 on v4

--- a/solution.py
+++ b/solution.py
@@ -6,7 +6,6 @@
 from jax.experimental import pallas as pl
 from jax.experimental.pallas import tpu as pltpu
 from jax.sharding import PartitionSpec as P
-
 
 CAP = 2
 UNROLL = 4
@@ -218,7 +217,7 @@
     lax.fori_loop(0, head_count, drain, 0)
 
 
-def units_kernel(
+def pulled_kernel(
     block_count,
     wanted_ref,
     bits_ref,
@@ -228,12 +227,40 @@
     lse_ref,
     delta_ref,
     own_dq_ref,
-    rows_ref,
+    w_hbm,
+    far_send_ref,
+    far_keep_ref,
+    near_send_hbm,
+    near_keep_hbm,
     grads_hbm,
     dq_ref,
+    rows_ref,
     grads_ref,
-    out_sem,
+    w_ref,
+    near_send_ref,
+    near_keep_ref,
+    out_sems,
+    w_sems,
+    near_sems,
 ):
+    chunks = w_sems.shape[0]
+    chunk = w_ref.shape[0] // chunks
+
+    def load_w(at):
+        rows = pl.ds(at * chunk, chunk)
+        return pltpu.make_async_copy(w_hbm.at[rows], w_ref.at[rows], w_sems.at[at])
+
+    def store_near(at):
+        columns = pl.ds(at * chunk, chunk)
+        return [
+            pltpu.make_async_copy(ref.at[:, columns], out.at[:, columns], near_sems.at[side, at])
+            for side, (ref, out) in enumerate(
+                ((near_send_ref, near_send_hbm), (near_keep_ref, near_keep_hbm))
+            )
+        ]
+
+    for at in range(chunks):
+        load_w(at).start()
     tokens = q_ref.shape[0]
     head_size = grads_ref.shape[2] // 2
     block_size = grads_ref.shape[1] // CAP
@@ -269,11 +296,17 @@
             grads_ref[owner, place, :head_size] = dk
             grads_ref[owner, place, head_size:] = dv
             dq_ref[:, lanes] += value
-        return carry
-
-    lax.fori_loop(0, lax.div(lax.axis_index("seq") + UNROLL - 1, UNROLL), owner_step, 0)
-    store = pltpu.make_async_copy(grads_ref, grads_hbm, out_sem)
-    store.start()
+        store(step).start()
+        return carry
+
+    def store(step):
+        owners = pl.ds(step * UNROLL, UNROLL)
+        return pltpu.make_async_copy(
+            grads_ref.at[owners], grads_hbm.at[owners], out_sems.at[step]
+        )
+
+    steps = lax.div(lax.axis_index("seq") + UNROLL - 1, UNROLL)
+    lax.fori_loop(0, steps, owner_step, 0)
     part = tokens // 4
     here = lax.axis_index("head")
     for place in range(4):
@@ -281,27 +314,24 @@
         rows_ref[place * part : (place + 1) * part, :] = (
             dq_ref[pl.ds(start, part), :] * scale
         ).astype(rows_ref.dtype)
-    store.wait()
-
-
-def product_kernel(rows_ref, w_hbm, *refs):
-    targets, w_ref, w_sems = refs[:4], refs[4], refs[5]
-    part = targets[0].shape[0]
-    chunks = w_sems.shape[0]
-    chunk = w_ref.shape[0] // chunks
-
-    def load_w(at):
-        rows = pl.ds(at * chunk, chunk)
-        return pltpu.make_async_copy(w_hbm.at[rows], w_ref.at[rows], w_sems.at[at])
-
-    for at in range(chunks):
-        load_w(at).start()
+    targets = (far_send_ref, far_keep_ref, near_send_ref, near_keep_ref)
     for at in range(chunks):
         load_w(at).wait()
         columns = slice(at * chunk, (at + 1) * chunk)
         product = dot_nt(rows_ref[...], w_ref[columns, :])
         for place, ref in enumerate(targets):
             ref[:, columns] = product[place * part : (place + 1) * part].astype(ref.dtype)
+        for copy in store_near(at):
+            copy.start()
+    for at in range(chunks):
+        for copy in store_near(at):
+            copy.wait()
+
+    def drain(step, carry):
+        store(step).wait()
+        return carry
+
+    lax.fori_loop(0, steps, drain, 0)
 
 
 def finish_kernel(
@@ -314,21 +344,36 @@
     dv_out,
     dk_ref,
     dv_ref,
-    sems,
+    dk_low_ref,
+    dv_low_ref,
+    in_sems,
+    out_sems,
 ):
     shards = incoming_ref.shape[0]
     head_size = returned_ref.shape[2] // 2
     block_size = returned_ref.shape[1] // CAP
-    loads = [
-        pltpu.make_async_copy(source, target, sems.at[at])
-        for at, (source, target) in enumerate(
-            ((own_dk_hbm, dk_ref), (own_dv_hbm, dv_ref))
+    groups = in_sems.shape[1]
+    group = dk_ref.shape[1] // groups
+
+    def load(at, side):
+        source, target = ((own_dk_hbm, dk_ref), (own_dv_hbm, dv_ref))[side]
+        lanes = pl.ds(at * group, group)
+        return pltpu.make_async_copy(
+            source.at[:, lanes], target.at[:, lanes], in_sems.at[side, at]
         )
-    ]
-    for load in loads:
-        load.start()
-    for load in loads:
-        load.wait()
+
+    def store(at, side):
+        source, target = ((dk_low_ref, dk_out), (dv_low_ref, dv_out))[side]
+        lanes = pl.ds(at * group, group)
+        return pltpu.make_async_copy(
+            source.at[:, lanes], target.at[:, lanes], out_sems.at[side, at]
+        )
+
+    every = [(at, side) for at in range(groups) for side in range(2)]
+    for at, side in every:
+        load(at, side).start()
+    for at, side in every:
+        load(at, side).wait()
 
     def asker_step(asker, carry):
         for slot in range(CAP):
@@ -347,8 +392,13 @@
         return carry
 
     lax.fori_loop(lax.axis_index("seq") + 1, shards, asker_step, 0)
-    dk_out[...] = dk_ref[...].astype(dk_out.dtype)
-    dv_out[...] = dv_ref[...].astype(dv_out.dtype)
+    for at, side in every:
+        lanes = slice(at * group, (at + 1) * group)
+        source, target = ((dk_ref, dk_low_ref), (dv_ref, dv_low_ref))[side]
+        target[:, lanes] = source[:, lanes].astype(target.dtype)
+        store(at, side).start()
+    for at, side in every:
+        store(at, side).wait()
 
 
 def per_device(queries, keys, values, outputs, out_grad, log_sum, selected, w_query):
@@ -434,32 +484,33 @@
 
     part = tokens // groups
     features = w_query.shape[0]
-    rows, grads = pl.pallas_call(
-        functools.partial(units_kernel, block_count),
-        out_shape=(shape((tokens, row_width), bf16), pltpu.HBM(exchange, bf16)),
-        in_specs=[SMEM, SMEM] + [VMEM] * 6,
-        out_specs=(VMEM, HBM),
+    far_send, far_keep, near_send, near_keep, grads = pl.pallas_call(
+        functools.partial(pulled_kernel, block_count),
+        out_shape=(
+            shape((part, features), bf16),
+            shape((part, features), bf16),
+            pltpu.HBM((part, features), bf16),
+            pltpu.HBM((part, features), bf16),
+            pltpu.HBM(exchange, bf16),
+        ),
+        in_specs=[SMEM, SMEM] + [VMEM] * 6 + [HBM],
+        out_specs=(VMEM, VMEM, HBM, HBM, HBM),
         scratch_shapes=[
             pltpu.VMEM((tokens, row_width), f32),
+            pltpu.VMEM((tokens, row_width), bf16),
             pltpu.VMEM(exchange, bf16),
-            pltpu.SemaphoreType.DMA,
+            pltpu.VMEM(w_query.shape, bf16),
+            pltpu.VMEM((part, features), bf16),
+            pltpu.VMEM((part, features), bf16),
+            pltpu.SemaphoreType.DMA((shards // UNROLL,)),
+            pltpu.SemaphoreType.DMA((8,)),
+            pltpu.SemaphoreType.DMA((2, 8)),
         ],
         compiler_params=params(),
         cost_estimate=cost(unit_flops * shards * CAP, 10 * tokens * row_width),
-        name="units",
-    )(wanted, bits, pulled, q_here, do_here, lse_here, delta, own_dq)
+        name="pulled",
+    )(wanted, bits, pulled, q_here, do_here, lse_here, delta, own_dq, w_query)
     returned = lax.all_to_all(grads, "seq", split_axis=0, concat_axis=0, tiled=True)
-
-    far_send, far_keep, near_send, near_keep = pl.pallas_call(
-        product_kernel,
-        out_shape=(shape((part, features), bf16),) * 4,
-        in_specs=[VMEM, HBM],
-        out_specs=(VMEM,) * 4,
-        scratch_shapes=[pltpu.VMEM(w_query.shape, bf16), pltpu.SemaphoreType.DMA((8,))],
-        compiler_params=params(),
-        cost_estimate=cost(8 * part * row_width * features, 2 * row_width * features),
-        name="product",
-    )(rows, w_query)
 
     beside = [(i, i ^ 1) for i in range(groups)]
     across = [(i, i ^ 2) for i in range(groups)]
@@ -475,16 +526,20 @@
         functools.partial(finish_kernel, block_count),
         out_shape=(shape((tokens, row_width), bf16), shape((tokens, row_width), bf16)),
         in_specs=[SMEM, VMEM, HBM, HBM],
-        out_specs=(VMEM, VMEM),
+        out_specs=(HBM, HBM),
         scratch_shapes=[
             pltpu.VMEM((tokens, row_width), f32),
             pltpu.VMEM((tokens, row_width), f32),
-            pltpu.SemaphoreType.DMA((2,)),
+            pltpu.VMEM((tokens, row_width), bf16),
+            pltpu.VMEM((tokens, row_width), bf16),
+            pltpu.SemaphoreType.DMA((2, 4)),
+            pltpu.SemaphoreType.DMA((2, 4)),
         ],
         compiler_params=params(),
         name="finish",
     )(incoming, returned, own_dk, own_dv)
-    x_grad = (near_keep.astype(f32) + near_got.astype(f32) + across_got.astype(f32)).astype(bf16)
+    near_sum = lax.optimization_barrier(near_keep.astype(f32) + near_got.astype(f32))
+    x_grad = (near_sum + across_got.astype(f32)).astype(bf16)
     return (x_grad, key_gradient, value_gradient)
 
 

time: 70.5 us -> 69 us (0.979)
  waiting for transfers between devices: 20.3 us -> 19.1 us
  starting transfers between devices: 12.8 us -> 11.7 us
  Pallas kernels: 19.6 us -> 20.4 us
    all_to_all x1, waiting for transfers between devices: 13.3 us -> 11.9 us  [per_device(): lax.all_to_all(grads, 'seq', split_axis=0, concat_axis=0, tiled=True)]
    add x0 -> x1, other arithmetic: none -> 1.15 us  [per_device(): near_keep.astype(f32) + near_got.astype(f32)]
    convert_element_type x1, other arithmetic: 2.03 us -> 0.88 us  [per_device(): x_grad = (near_sum + across_got.astype(f32)).astype(bf16)]
    all_to_all x1, starting transfers between devices: 7.49 us -> 6.43 us  [per_device(): lax.all_to_all(grads, 'seq', split_axis=0, concat_axis=0, tiled=True)]
    pallas_call x2 -> x1, Pallas kernels: 6.6 us -> 7.31 us  [per_device(): pl.pallas_call(functools.partial(pulled_kernel, block_count), out_shape=(...]
  transfers between devices with their start and end apart: 5 -> 5, of which waited for: 2 -> 3; matrix products, arithmetic and copies ran while one was open for 0% -> 2% of each run, Pallas kernels for 14% -> 14%
where the time goes in v5:
time: 69 us; the launch traced here: 68.4 us
  Pallas kernels  20.4 us (30%)
  waiting for transfers between devices  19.1 us (28%)
  blocking collectives  13.6 us (20%)
  starting transfers between devices  11.7 us (17%)
  other arithmetic  2.15 us (3%)
  local copies, waits for them, and re-layouts  0.71 us (1%)
  between operations  0.71 us (1%)
    all_to_all x1, blocking collectives, per_device(): lax.all_to_all(wanted, 'seq', split_axis=0, concat_axis=0, tiled=True)  13.6 us
    all_to_all x1, waiting for transfers between devices, per_device(): lax.all_to_all(grads, 'seq', split_axis=0, concat_axis=0, tiled=True)  11.9 us
    pallas_call x1, Pallas kernels, per_device(): pl.pallas_call(functools.partial(pulled_kernel, block_count), out_shape=(...  7.31 us
    all_to_all x1, waiting for transfers between devices, per_device(): lax.all_to_all(outgoing, 'seq', split_axis=0, concat_axis=0, tiled=True)  6.96 us
    all_to_all x1, starting transfers between devices, per_device(): lax.all_to_all(grads, 'seq', split_axis=0, concat_axis=0, tiled=True)  6.43 us
    pallas_call x1, Pallas kernels, per_device(): pl.pallas_call(functools.partial(own_kernel, block_count), out_shape=(sha...  6.36 us
    all_to_all x1, starting transfers between devices, per_device(): lax.all_to_all(outgoing, 'seq', split_axis=0, concat_axis=0, tiled=True)  3.51 us
    pallas_call x1, Pallas kernels, per_device(): pl.pallas_call(functools.partial(finish_kernel, block_count), out_shape=(...  3.39 us
  transfers between devices with their start and end apart: 5, of which 3 were waited for; matrix products, arithmetic and copies ran while one was open for 2% of the time, Pallas kernels for 14%

profile of v5, /device:TPU:0, one launch (start us, length us, event | category | flops | bytes accessed | tf_op | source)
XLA Modules:
  0.0 68.4 jit_solution(14162472388423381642)
XLA Ops:
  0.6 0.0 copy-start
  0.6 0.7 %copy-done = s32[8,4,16]{2,1,0:T(4,128)S(1)} copy-done((s32[8,4,16]{2,1,0:T(4,128)S(1)}, s32[8,4,16]{2,1,0:T(4,128)}, u32[]{:S(2)}) %copy-start) | copy-done | bytes 2072
  1.3 0.6 index.1
  1.9 13.6 %all_to_all.15.incoming_ref = s32[8,1,128]{2,1,0:T(1,128)S(1)} all-to-all(s32[8,1,128]{2,1,0:T(1,128)S(1)} %get-tuple-element.19.wanted_ref), channel_id=1, replica_groups=mesh['seq'=8,'head'=4] {'seq'}, dimensions={0} | all-to-all | bytes 8192 | tf_op jit(solution)/shard_map/all_to_all | solution.py:438
  15.5 2.8 %gather.1 = bf16[8,128,256]{2,1,0:T(8,128)(2,1)} custom-call(s32[8,1,128]{2,1,0:T(1,128)S(1)} %all_to_all.15.incoming_ref, bf16[256,1024]{1,0:T(8,128)(2,1)} %k_hbm.1, bf16[256,1024]{1,0:T(8,128)(2,1)} %v_hbm.1), custom_call_target="tpu_custom_call" | custom-call | tf_op jit(solution)/shard_map/gather/pallas_call | solution.py:441
  18.3 3.5 %all-to-all-start.1 = ((bf16[8,128,256]{2,1,0:T(8,128)(2,1)}), bf16[8,128,256]{2,1,0:T(8,128)(2,1)S(1)}, u32[]{:S(2)}, u32[]{:S(2)}) async-start(bf16[8,128,256]{2,1,0:T(8,128)(2,1)} %gather.1), calls=%async_computation.1 | async-start | bytes 1048576 | tf_op jit(solution)/shard_map/all_to_all | solution.py:454
  21.8 6.4 %own.1 = (bf16[256,1024]{1,0:T(8,128)(2,1)S(1)}, bf16[256,1024]{1,0:T(8,128)(2,1)S(1)}, f32[8,256]{1,0:T(8,128)S(1)}, f32[8,256]{1,0:T(8,128)S(1)}, f32[256,1024...) custom-call(s32[8,128]{1,0:T(8,128)S(1)} %get-tuple-element.20.bits_ref, bf16[256,1024]{1,0:T(8,128)(2,1)} %q_hbm.1, ...), custom_call_target="tpu_custom_call" | custom-call | flops 5368709120 | bytes 5767168 | tf_op jit(solution)/shard_map/own/pallas_call | solution.py:457
  28.2 7.0 %all-to-all-done.1.pulled_ref = bf16[8,128,256]{2,1,0:T(8,128)(2,1)S(1)} async-done(((bf16[8,128,256]{2,1,0:T(8,128)(2,1)}), bf16[8,128,256]{2,1,0:T(8,128)(2,1)S(1)}, u32[]{:S(2)}, u32[]{:S(2)}) %all-to-all-start.1) | async-done | bytes 524320 | tf_op jit(solution)/shard_map/all_to_all | solution.py:454
  35.1 7.3 %pulled.1 = (bf16[64,4096]{1,0:T(8,128)(2,1)}, bf16[64,4096]{1,0:T(8,128)(2,1)S(1)}, bf16[64,4096]{1,0:T(8,128)(2,1)}, bf16[64,4096]{1,0:T(8,128)(2,1)}, bf16[8,128,256]{2,1,0:T(8,128)(2,1)}) custom-call(s32[8,1,128]{2,1,0:T(1,128)S(1)} %get-tuple-element.19.wanted_ref, s32[8,128]{1,0:T(8,128)S(1)} %get-tuple-element.20.bits_ref, ...), custom_call_target="tpu_custom_call" | custom-call | flops 335544320 | bytes 2621440 | tf_op jit(solution)/shard_map/pulled/pallas_call | solution.py:487
  42.5 0.1 collective-permute-start.1
  42.5 6.4 %all-to-all-start.2 = ((bf16[8,128,256]{2,1,0:T(8,128)(2,1)}), bf16[8,128,256]{2,1,0:T(8,128)(2,1)S(1)}, u32[]{:S(2)}, u32[]{:S(2)}) async-start(bf16[8,128,256]{2,1,0:T(8,128)(2,1)} %get-tuple-element.30), calls=%async_computation.2 | async-start | bytes 1048576 | tf_op jit(solution)/shard_map/all_to_all | solution.py:513
  49.0 0.2 collective-permute-start
  49.2 0.0 collective-permute-done.1
  49.2 0.1 add_convert_fusion.1
  49.3 1.5 %collective-permute-start.2 = (bf16[64,4096]{1,0:T(8,128)(2,1)S(1)}, bf16[64,4096]{1,0:T(8,128)(2,1)S(1)}, u32[]{:S(2)}, u32[]{:S(2)}) collective-permute-start(bf16[64,4096]{1,0:T(8,128)(2,1)S(1)} %add_convert_fusion.1), channel_id=1, source_target_pairs={{0,2},{1,3},{2,0},{3,1},{4,6},{5,7},{6,4},{7,5},{8,10},{9,11},{10,... | collective-permute-start | bytes 1572872 | tf_op jit(solution)/shard_map/ppermute | solution.py:519
  50.8 0.3 collective-permute-done
  51.1 1.1 %convert_add_fusion = f32[64,4096]{1,0:T(8,128)S(1)} fusion(bf16[64,4096]{1,0:T(8,128)(2,1)S(1)} %collective-permute-done, bf16[64,4096]{1,0:T(8,128)(2,1)} %get-tuple-element.26), kind=kLoop, calls=%fused_computation.2 | loop fusion | flops 786432 | bytes 2097152 | tf_op jit(solution)/shard_map/add | solution.py:541
  52.2 11.9 %all-to-all-done.2.returned_ref = bf16[8,128,256]{2,1,0:T(8,128)(2,1)S(1)} async-done(((bf16[8,128,256]{2,1,0:T(8,128)(2,1)}), bf16[8,128,256]{2,1,0:T(8,128)(2,1)S(1)}, u32[]{:S(2)}, u32[]{:S(2)}) %all-to-all-start.2) | async-done | bytes 524320 | tf_op jit(solution)/shard_map/all_to_all | solution.py:513
  64.1 3.4 %finish.1 = (bf16[256,1024]{1,0:T(8,128)(2,1)}, bf16[256,1024]{1,0:T(8,128)(2,1)}) custom-call(s32[8,1,128]{2,1,0:T(1,128)S(1)} %all_to_all.15.incoming_ref, bf16[8,128,256]{2,1,0:T(8,128)(2,1)S(1)} %all-to-all-done.2.returned_ref, f32[256,1024]{1,0:T(8,128)} %get-tuple-element.31.own_dk_hbm, f32[256,1024]{1,0:T(8,128)} %get-tuple-element.32.own_dv_hbm), custom_call_target="tpu_custom_call" | custom-call | tf_op jit(solution)/shard_map/finish/pallas_call | solution.py:525
  67.5 0.0 collective-permute-done.2
  67.5 0.9 %add_convert_fusion = bf16[64,4096]{1,0:T(8,128)(2,1)} fusion(f32[64,4096]{1,0:T(8,128)S(1)} %convert_add_fusion, bf16[64,4096]{1,0:T(8,128)(2,1)S(1)} %collective-permute-done.2), kind=kLoop, calls=%fused_computation | loop fusion | flops 786432 | bytes 2097152 | tf_op jit(solution)/shard_map/convert_element_type | solution.py:542
Async XLA Ops:
  0.6 0.7 %copy-start = (s32[8,4,16]{2,1,0:T(4,128)S(1)}, s32[8,4,16]{2,1,0:T(4,128)}, u32[]{:S(2)}) copy-start(s32[8,4,16]{2,1,0:T(4,128)} %selected_ref.1) | copy-start | bytes 6148
  18.3 16.8 %all-to-all-start.1 = ((bf16[8,128,256]{2,1,0:T(8,128)(2,1)}), bf16[8,128,256]{2,1,0:T(8,128)(2,1)S(1)}, u32[]{:S(2)}, u32[]{:S(2)}) async-start(bf16[8,128,256]{2,1,0:T(8,128)(2,1)} %gather.1), calls=%async_computation.1 | async-start | bytes 1048576 | tf_op jit(solution)/shard_map/all_to_all | solution.py:454
  42.5 6.7 %collective-permute-start.1 = (bf16[64,4096]{1,0:T(8,128)(2,1)}, bf16[64,4096]{1,0:T(8,128)(2,1)S(1)}, u32[]{:S(2)}, u32[]{:S(2)}) collective-permute-start(bf16[64,4096]{1,0:T(8,128)(2,1)} %get-tuple-element.29), channel_id=1, source_target_pairs={{0,1},{1,0},{2,3},{3,2},{4,5},{5,4},{6,7},{7,6},{8,9},{9,8},{10,11... | collective-permute-start | bytes 1572872 | tf_op jit(solution)/shard_map/ppermute | solution.py:517
  42.5 21.6 %all-to-all-start.2 = ((bf16[8,128,256]{2,1,0:T(8,128)(2,1)}), bf16[8,128,256]{2,1,0:T(8,128)(2,1)S(1)}, u32[]{:S(2)}, u32[]{:S(2)}) async-start(bf16[8,128,256]{2,1,0:T(8,128)(2,1)} %get-tuple-element.30), calls=%async_computation.2 | async-start | bytes 1048576 | tf_op jit(solution)/shard_map/all_to_all | solution.py:513
  49.0 2.1 %collective-permute-start = (bf16[64,4096]{1,0:T(8,128)(2,1)}, bf16[64,4096]{1,0:T(8,128)(2,1)S(1)}, u32[]{:S(2)}, u32[]{:S(2)}) collective-permute-start(bf16[64,4096]{1,0:T(8,128)(2,1)} %get-tuple-element.27), channel_id=1, source_target_pairs={{0,1},{1,0},{2,3},{3,2},{4,5},{5,4},{6,7},{7,6},{8,9},{9,8},{10,11... | collective-permute-start | bytes 1572872 | tf_op jit(solution)/shard_map/ppermute | solution.py:521
  49.3 18.2 %collective-permute-start.2 = (bf16[64,4096]{1,0:T(8,128)(2,1)S(1)}, bf16[64,4096]{1,0:T(8,128)(2,1)S(1)}, u32[]{:S(2)}, u32[]{:S(2)}) collective-permute-start(bf16[64,4096]{1,0:T(8,128)(2,1)S(1)} %add_convert_fusion.1), channel_id=1, source_target_pairs={{0,2},{1,3},{2,0},{3,1},{4,6},{5,7},{6,4},{7,5},{8,10},{9,11},{10,... | collective-permute-start | bytes 1572872 | tf_op jit(solution)/shard_map/ppermute | solution.py:519

commit v6 on v4

--- a/solution.py
+++ b/solution.py
@@ -10,6 +10,7 @@
 
 CAP = 2
 UNROLL = 4
+PARTS = 2
 LANES = 128
 FAR = 1e30
 NONE = 1 << 20
@@ -284,15 +285,15 @@
     store.wait()
 
 
-def product_kernel(rows_ref, w_hbm, *refs):
+def product_kernel(first, rows_ref, w_hbm, *refs):
     targets, w_ref, w_sems = refs[:4], refs[4], refs[5]
     part = targets[0].shape[0]
     chunks = w_sems.shape[0]
     chunk = w_ref.shape[0] // chunks
 
     def load_w(at):
-        rows = pl.ds(at * chunk, chunk)
-        return pltpu.make_async_copy(w_hbm.at[rows], w_ref.at[rows], w_sems.at[at])
+        source = w_hbm.at[pl.ds(first + at * chunk, chunk)]
+        return pltpu.make_async_copy(source, w_ref.at[pl.ds(at * chunk, chunk)], w_sems.at[at])
 
     for at in range(chunks):
         load_w(at).start()
@@ -302,6 +303,14 @@
         product = dot_nt(rows_ref[...], w_ref[columns, :])
         for place, ref in enumerate(targets):
             ref[:, columns] = product[place * part : (place + 1) * part].astype(ref.dtype)
+
+
+def join_kernel(*refs):
+    out_ref = refs[-1]
+    share = refs[0].shape[1]
+    for at in range(out_ref.shape[1] // share):
+        keep, got, crossed = (ref[...].astype(jnp.float32) for ref in refs[3 * at : 3 * at + 3])
+        out_ref[:, at * share : (at + 1) * share] = (keep + got + crossed).astype(out_ref.dtype)
 
 
 def finish_kernel(
@@ -450,24 +459,26 @@
     )(wanted, bits, pulled, q_here, do_here, lse_here, delta, own_dq)
     returned = lax.all_to_all(grads, "seq", split_axis=0, concat_axis=0, tiled=True)
 
-    far_send, far_keep, near_send, near_keep = pl.pallas_call(
-        product_kernel,
-        out_shape=(shape((part, features), bf16),) * 4,
-        in_specs=[VMEM, HBM],
-        out_specs=(VMEM,) * 4,
-        scratch_shapes=[pltpu.VMEM(w_query.shape, bf16), pltpu.SemaphoreType.DMA((8,))],
-        compiler_params=params(),
-        cost_estimate=cost(8 * part * row_width * features, 2 * row_width * features),
-        name="product",
-    )(rows, w_query)
-
     beside = [(i, i ^ 1) for i in range(groups)]
     across = [(i, i ^ 2) for i in range(groups)]
-    far_got = lax.ppermute(far_send, "head", beside)
-    far_sum = (far_keep.astype(f32) + far_got.astype(f32)).astype(bf16)
-    across_got = lax.ppermute(far_sum, "head", across)
-
-    near_got = lax.ppermute(near_send, "head", beside)
+    share = features // PARTS
+    x_parts = []
+    for at in range(PARTS):
+        far_send, far_keep, near_send, near_keep = pl.pallas_call(
+            functools.partial(product_kernel, at * share),
+            out_shape=(shape((part, share), bf16),) * 4,
+            in_specs=[VMEM, HBM],
+            out_specs=(VMEM,) * 4,
+            scratch_shapes=[pltpu.VMEM((share, row_width), bf16), pltpu.SemaphoreType.DMA((4,))],
+            compiler_params=params(),
+            cost_estimate=cost(8 * part * row_width * share, 2 * row_width * share),
+            name="product",
+        )(rows, w_query)
+        far_got = lax.ppermute(far_send, "head", beside)
+        far_sum = (far_keep.astype(f32) + far_got.astype(f32)).astype(bf16)
+        across_got = lax.ppermute(far_sum, "head", across)
+        near_got = lax.ppermute(near_send, "head", beside)
+        x_parts.append((near_keep, near_got, across_got))
     own_dk, own_dv = (
         pltpu.with_memory_space_constraint(a, pltpu.HBM) for a in (own_dk, own_dv)
     )
@@ -484,7 +495,14 @@
         compiler_params=params(),
         name="finish",
     )(incoming, returned, own_dk, own_dv)
-    x_grad = (near_keep.astype(f32) + near_got.astype(f32) + across_got.astype(f32)).astype(bf16)
+    x_grad = pl.pallas_call(
+        join_kernel,
+        out_shape=shape((part, features), bf16),
+        in_specs=[VMEM] * (3 * PARTS),
+        out_specs=VMEM,
+        compiler_params=params(),
+        name="join",
+    )(*[piece for pieces in x_parts for piece in pieces])
     return (x_grad, key_gradient, value_gradient)
 
 

time: 70.5 us -> 70.5 us (level)
  Pallas kernels: 19.6 us -> 21.8 us
  other arithmetic: 2.15 us -> 0.13 us
  waiting for transfers between devices: 20.3 us -> 18.3 us
  starting transfers between devices: 12.8 us -> 14.7 us
    all_to_all x1, waiting for transfers between devices: 13.3 us -> 0.01 us  [per_device(): lax.all_to_all(grads, 'seq', split_axis=0, concat_axis=0, tiled=True)]
    ppermute x1 -> x2, waiting for transfers between devices: 0.01 us -> 11.3 us  [per_device(): across_got = lax.ppermute(far_sum, 'head', across)]
    pallas_call x1 -> x3, Pallas kernels: 5.07 us -> 7.28 us  [the longest x2 6.3 us: per_device(): pl.pallas_call(functools.partial(product_kernel, at * share), out_shape=(...]
    convert_element_type x1 -> x0, other arithmetic: 2.03 us -> none  [per_device(): (near_keep.astype(f32) + near_got.astype(f32) + across_got.astype(f32)).a...]
    ppermute x1 -> x2, starting transfers between devices: 1.5 us -> 2.82 us  [per_device(): across_got = lax.ppermute(far_sum, 'head', across)]
  transfers between devices with their start and end apart: 5 -> 8, of which waited for: 2 -> 3; matrix products, arithmetic and copies ran while one was open for 0% -> 0% of each run, Pallas kernels for 14% -> 15%
where the time goes in v6:
time: 70.5 us; the launch traced here: 69.9 us
  Pallas kernels  21.8 us (31%)
  waiting for transfers between devices  18.3 us (26%)
  starting transfers between devices  14.7 us (21%)
  blocking collectives  13.6 us (19%)
  local copies, waits for them, and re-layouts  0.71 us (1%)
  between operations  0.71 us (1%)
    all_to_all x1, blocking collectives, per_device(): lax.all_to_all(wanted, 'seq', split_axis=0, concat_axis=0, tiled=True)  13.6 us
    ppermute x2, waiting for transfers between devices, per_device(): across_got = lax.ppermute(far_sum, 'head', across)  11.3 us
    all_to_all x1, starting transfers between devices, per_device(): lax.all_to_all(grads, 'seq', split_axis=0, concat_axis=0, tiled=True)  7.49 us
    all_to_all x1, waiting for transfers between devices, per_device(): lax.all_to_all(outgoing, 'seq', split_axis=0, concat_axis=0, tiled=True)  6.97 us
    pallas_call x1, Pallas kernels, per_device(): pl.pallas_call(functools.partial(own_kernel, block_count), out_shape=(sha...  6.34 us
    pallas_call x2, Pallas kernels, per_device(): pl.pallas_call(functools.partial(product_kernel, at * share), out_shape=(...  6.3 us
    all_to_all x1, starting transfers between devices, per_device(): lax.all_to_all(outgoing, 'seq', split_axis=0, concat_axis=0, tiled=True)  3.51 us
    pallas_call x1, Pallas kernels, per_device(): pl.pallas_call(functools.partial(finish_kernel, block_count), out_shape=(...  3.33 us
  transfers between devices with their start and end apart: 8, of which 3 were waited for; matrix products, arithmetic and copies ran while one was open for 0% of the time, Pallas kernels for 15%

profile of v6, /device:TPU:0, one launch (start us, length us, event | category | flops | bytes accessed | tf_op | source)
XLA Modules:
  0.0 69.9 jit_solution(5218711912804759113)
XLA Ops:
  0.6 0.0 copy-start
  0.6 0.7 %copy-done = s32[8,4,16]{2,1,0:T(4,128)S(1)} copy-done((s32[8,4,16]{2,1,0:T(4,128)S(1)}, s32[8,4,16]{2,1,0:T(4,128)}, u32[]{:S(2)}) %copy-start) | copy-done | bytes 2072
  1.3 0.6 index.1
  1.9 13.6 %all_to_all.15.incoming_ref = s32[8,1,128]{2,1,0:T(1,128)S(1)} all-to-all(s32[8,1,128]{2,1,0:T(1,128)S(1)} %get-tuple-element.24.wanted_ref), channel_id=1, replica_groups=mesh['seq'=8,'head'=4] {'seq'}, dimensions={0} | all-to-all | bytes 8192 | tf_op jit(solution)/shard_map/all_to_all | solution.py:397
  15.5 2.8 %gather.1 = bf16[8,128,256]{2,1,0:T(8,128)(2,1)} custom-call(s32[8,1,128]{2,1,0:T(1,128)S(1)} %all_to_all.15.incoming_ref, bf16[256,1024]{1,0:T(8,128)(2,1)} %k_hbm.1, bf16[256,1024]{1,0:T(8,128)(2,1)} %v_hbm.1), custom_call_target="tpu_custom_call" | custom-call | tf_op jit(solution)/shard_map/gather/pallas_call | solution.py:400
  18.3 3.5 %all-to-all-start.1 = ((bf16[8,128,256]{2,1,0:T(8,128)(2,1)}), bf16[8,128,256]{2,1,0:T(8,128)(2,1)S(1)}, u32[]{:S(2)}, u32[]{:S(2)}) async-start(bf16[8,128,256]{2,1,0:T(8,128)(2,1)} %gather.1), calls=%async_computation.1 | async-start | bytes 1048576 | tf_op jit(solution)/shard_map/all_to_all | solution.py:413
  21.8 6.3 %own.1 = (bf16[256,1024]{1,0:T(8,128)(2,1)S(1)}, bf16[256,1024]{1,0:T(8,128)(2,1)S(1)}, f32[8,256]{1,0:T(8,128)S(1)}, f32[8,256]{1,0:T(8,128)S(1)}, f32[256,1024...) custom-call(s32[8,128]{1,0:T(8,128)S(1)} %get-tuple-element.25.bits_ref, bf16[256,1024]{1,0:T(8,128)(2,1)} %q_hbm.1, ...), custom_call_target="tpu_custom_call" | custom-call | flops 5368709120 | bytes 5767168 | tf_op jit(solution)/shard_map/own/pallas_call | solution.py:416
  28.2 7.0 %all-to-all-done.1.pulled_ref = bf16[8,128,256]{2,1,0:T(8,128)(2,1)S(1)} async-done(((bf16[8,128,256]{2,1,0:T(8,128)(2,1)}), bf16[8,128,256]{2,1,0:T(8,128)(2,1)S(1)}, u32[]{:S(2)}, u32[]{:S(2)}) %all-to-all-start.1) | async-done | bytes 524320 | tf_op jit(solution)/shard_map/all_to_all | solution.py:413
  35.1 1.5 %units.1 = (bf16[256,1024]{1,0:T(8,128)(2,1)S(1)}, bf16[8,128,256]{2,1,0:T(8,128)(2,1)}) custom-call(s32[8,1,128]{2,1,0:T(1,128)S(1)} %get-tuple-element.24.wanted_ref, s32[8,128]{1,0:T(8,128)S(1)} %get-tuple-element.25.bits_ref, bf16[8,128,256]{2,1,0:T(8,128)(2,1)S(1)} %all-to-all-done.1.pulled_ref, bf16[256,1024]{1,0:T(8,128)(2,1)S(1)} %get-tuple-element.26.q_ref, ...), custom_call_target="tpu_custom_call" | custom-call | flops 335544320 | bytes 2621440 | tf_op jit(solution)/shard_map/units/pallas_call | solution.py:446
  36.7 3.2 %product.3 = (bf16[64,2048]{1,0:T(8,128)(2,1)S(1)}, bf16[64,2048]{1,0:T(8,128)(2,1)S(1)}, bf16[64,2048]{1,0:T(8,128)(2,1)S(1)}, bf16[64,2048]{1,0:T(8,128)(2,1)S(1)}) custom-call(bf16[256,1024]{1,0:T(8,128)(2,1)S(1)} %get-tuple-element.31.rows_ref, bf16[4096,1024]{1,0:T(8,128)(2,1)} %w_hbm.3), custom_call_target="tpu_custom_call" | custom-call | flops 1073741824 | bytes 4194304 | tf_op jit(solution)/shard_map/product/pallas_call | solution.py:467
  39.8 0.1 collective-permute-start.4
  39.9 7.5 %all-to-all-start.2 = ((bf16[8,128,256]{2,1,0:T(8,128)(2,1)}), bf16[8,128,256]{2,1,0:T(8,128)(2,1)S(1)}, u32[]{:S(2)}, u32[]{:S(2)}) async-start(bf16[8,128,256]{2,1,0:T(8,128)(2,1)} %get-tuple-element.40), calls=%async_computation.2 | async-start | bytes 1048576 | tf_op jit(solution)/shard_map/all_to_all | solution.py:460
  47.4 0.2 collective-permute-start.3
  47.6 3.1 %product.2 = (bf16[64,2048]{1,0:T(8,128)(2,1)S(1)}, bf16[64,2048]{1,0:T(8,128)(2,1)S(1)}, bf16[64,2048]{1,0:T(8,128)(2,1)S(1)}, bf16[64,2048]{1,0:T(8,128)(2,1)S(1)}) custom-call(bf16[256,1024]{1,0:T(8,128)(2,1)S(1)} %get-tuple-element.31.rows_ref, bf16[4096,1024]{1,0:T(8,128)(2,1)} %w_hbm.3), custom_call_target="tpu_custom_call" | custom-call | flops 1073741824 | bytes 4194304 | tf_op jit(solution)/shard_map/product/pallas_call | solution.py:467
  50.8 0.4 collective-permute-start
  51.1 0.2 collective-permute-start.1
  51.3 0.0 collective-permute-done.4
  51.3 0.1 add_convert_fusion
  51.4 1.5 %collective-permute-start.5 = (bf16[64,2048]{1,0:T(8,128)(2,1)S(1)}, bf16[64,2048]{1,0:T(8,128)(2,1)S(1)}, u32[]{:S(2)}, u32[]{:S(2)}) collective-permute-start(bf16[64,2048]{1,0:T(8,128)(2,1)S(1)} %add_convert_fusion), channel_id=1, source_target_pairs={{0,2},{1,3},{2,0},{3,1},{4,6},{5,7},{6,4},{7,5},{8,10},{9,11},{10,... | collective-permute-start | bytes 786440 | tf_op jit(solution)/shard_map/ppermute | solution.py:479
  52.9 0.0 collective-permute-done.1
  52.9 0.1 add_convert_fusion.1
  53.0 1.3 %collective-permute-start.2 = (bf16[64,2048]{1,0:T(8,128)(2,1)S(1)}, bf16[64,2048]{1,0:T(8,128)(2,1)S(1)}, u32[]{:S(2)}, u32[]{:S(2)}) collective-permute-start(bf16[64,2048]{1,0:T(8,128)(2,1)S(1)} %add_convert_fusion.1), channel_id=1, source_target_pairs={{0,2},{1,3},{2,0},{3,1},{4,6},{5,7},{6,4},{7,5},{8,10},{9,11},{10,... | collective-permute-start | bytes 786440 | tf_op jit(solution)/shard_map/ppermute | solution.py:479
  54.3 0.0 collective-permute-done.3.refs_4_
  54.3 0.0 collective-permute-done.refs_1_
  54.3 6.3 %collective-permute-done.5.refs_5_ = bf16[64,2048]{1,0:T(8,128)(2,1)S(1)} collective-permute-done((bf16[64,2048]{1,0:T(8,128)(2,1)S(1)}, bf16[64,2048]{1,0:T(8,128)(2,1)S(1)}, u32[]{:S(2)}, u32[]{:S(2)}) %collective-permute-start.5) | collective-permute-done | bytes 262176 | tf_op jit(solution)/shard_map/ppermute | solution.py:479
  60.6 5.0 %collective-permute-done.2.refs_2_ = bf16[64,2048]{1,0:T(8,128)(2,1)S(1)} collective-permute-done((bf16[64,2048]{1,0:T(8,128)(2,1)S(1)}, bf16[64,2048]{1,0:T(8,128)(2,1)S(1)}, u32[]{:S(2)}, u32[]{:S(2)}) %collective-permute-start.2) | collective-permute-done | bytes 262176 | tf_op jit(solution)/shard_map/ppermute | solution.py:479
  65.6 1.0 %join.1 = bf16[64,4096]{1,0:T(8,128)(2,1)} custom-call(bf16[64,2048]{1,0:T(8,128)(2,1)S(1)} %get-tuple-element.32.refs_0_, bf16[64,2048]{1,0:T(8,128)(2,1)S(1)} %collective-permute-done.refs_1_, bf16[64,2048]{1,0:T(8,128)(2,1)S(1)} %collective-permute-done.2.refs_2_, bf16[64,2048]{1,0:T(8,128)(2,1)S(1)} %get-tuple-element.36.refs_3_, ...), custom_call_target="tpu_custom_call" | custom-call | tf_op jit(solution)/shard_map/join/pallas_call | solution.py:498
  66.6 0.0 all-to-all-done.2.returned_ref
  66.6 3.3 %finish.1 = (bf16[256,1024]{1,0:T(8,128)(2,1)}, bf16[256,1024]{1,0:T(8,128)(2,1)}) custom-call(s32[8,1,128]{2,1,0:T(1,128)S(1)} %all_to_all.15.incoming_ref, bf16[8,128,256]{2,1,0:T(8,128)(2,1)S(1)} %all-to-all-done.2.returned_ref, f32[256,1024]{1,0:T(8,128)} %get-tuple-element.41.own_dk_hbm, f32[256,1024]{1,0:T(8,128)} %get-tuple-element.42.own_dv_hbm), custom_call_target="tpu_custom_call" | custom-call | tf_op jit(solution)/shard_map/finish/pallas_call | solution.py:485
Async XLA Ops:
  0.6 0.7 %copy-start = (s32[8,4,16]{2,1,0:T(4,128)S(1)}, s32[8,4,16]{2,1,0:T(4,128)}, u32[]{:S(2)}) copy-start(s32[8,4,16]{2,1,0:T(4,128)} %selected_ref.1) | copy-start | bytes 6148
  18.3 16.8 %all-to-all-start.1 = ((bf16[8,128,256]{2,1,0:T(8,128)(2,1)}), bf16[8,128,256]{2,1,0:T(8,128)(2,1)S(1)}, u32[]{:S(2)}, u32[]{:S(2)}) async-start(bf16[8,128,256]{2,1,0:T(8,128)(2,1)} %gather.1), calls=%async_computation.1 | async-start | bytes 1048576 | tf_op jit(solution)/shard_map/all_to_all | solution.py:413
  39.8 11.5 %collective-permute-start.4 = (bf16[64,2048]{1,0:T(8,128)(2,1)S(1)}, bf16[64,2048]{1,0:T(8,128)(2,1)S(1)}, u32[]{:S(2)}, u32[]{:S(2)}) collective-permute-start(bf16[64,2048]{1,0:T(8,128)(2,1)S(1)} %get-tuple-element.39), channel_id=1, source_target_pairs={{0,1},{1,0},{2,3},{3,2},{4,5},{5,4},{6,7},{7,6},{8,9},{9,8},{10,11... | collective-permute-start | bytes 786440 | tf_op jit(solution)/shard_map/ppermute | solution.py:477
  39.9 26.7 %all-to-all-start.2 = ((bf16[8,128,256]{2,1,0:T(8,128)(2,1)}), bf16[8,128,256]{2,1,0:T(8,128)(2,1)S(1)}, u32[]{:S(2)}, u32[]{:S(2)}) async-start(bf16[8,128,256]{2,1,0:T(8,128)(2,1)} %get-tuple-element.40), calls=%async_computation.2 | async-start | bytes 1048576 | tf_op jit(solution)/shard_map/all_to_all | solution.py:460
  47.4 6.9 %collective-permute-start.3 = (bf16[64,2048]{1,0:T(8,128)(2,1)S(1)}, bf16[64,2048]{1,0:T(8,128)(2,1)S(1)}, u32[]{:S(2)}, u32[]{:S(2)}) collective-permute-start(bf16[64,2048]{1,0:T(8,128)(2,1)S(1)} %get-tuple-element.37), channel_id=1, source_target_pairs={{0,1},{1,0},{2,3},{3,2},{4,5},{5,4},{6,7},{7,6},{8,9},{9,8},{10,11... | collective-permute-start | bytes 786440 | tf_op jit(solution)/shard_map/ppermute | solution.py:480
  50.8 3.5 %collective-permute-start = (bf16[64,2048]{1,0:T(8,128)(2,1)S(1)}, bf16[64,2048]{1,0:T(8,128)(2,1)S(1)}, u32[]{:S(2)}, u32[]{:S(2)}) collective-permute-start(bf16[64,2048]{1,0:T(8,128)(2,1)S(1)} %get-tuple-element.33), channel_id=1, source_target_pairs={{0,1},{1,0},{2,3},{3,2},{4,5},{5,4},{6,7},{7,6},{8,9},{9,8},{10,11... | collective-permute-start | bytes 786440 | tf_op jit(solution)/shard_map/ppermute | solution.py:480
  51.1 1.8 %collective-permute-start.1 = (bf16[64,2048]{1,0:T(8,128)(2,1)S(1)}, bf16[64,2048]{1,0:T(8,128)(2,1)S(1)}, u32[]{:S(2)}, u32[]{:S(2)}) collective-permute-start(bf16[64,2048]{1,0:T(8,128)(2,1)S(1)} %get-tuple-element.35), channel_id=1, source_target_pairs={{0,1},{1,0},{2,3},{3,2},{4,5},{5,4},{6,7},{7,6},{8,9},{9,8},{10,11... | collective-permute-start | bytes 786440 | tf_op jit(solution)/shard_map/ppermute | solution.py:477
  51.4 9.2 %collective-permute-start.5 = (bf16[64,2048]{1,0:T(8,128)(2,1)S(1)}, bf16[64,2048]{1,0:T(8,128)(2,1)S(1)}, u32[]{:S(2)}, u32[]{:S(2)}) collective-permute-start(bf16[64,2048]{1,0:T(8,128)(2,1)S(1)} %add_convert_fusion), channel_id=1, source_target_pairs={{0,2},{1,3},{2,0},{3,1},{4,6},{5,7},{6,4},{7,5},{8,10},{9,11},{10,... | collective-permute-start | bytes 786440 | tf_op jit(solution)/shard_map/ppermute | solution.py:479
  53.0 12.6 %collective-permute-start.2 = (bf16[64,2048]{1,0:T(8,128)(2,1)S(1)}, bf16[64,2048]{1,0:T(8,128)(2,1)S(1)}, u32[]{:S(2)}, u32[]{:S(2)}) collective-permute-start(bf16[64,2048]{1,0:T(8,128)(2,1)S(1)} %add_convert_fusion.1), channel_id=1, source_target_pairs={{0,2},{1,3},{2,0},{3,1},{4,6},{5,7},{6,4},{7,5},{8,10},{9,11},{10,... | collective-permute-start | bytes 786440 | tf_op jit(solution)/shard_map/ppermute | solution.py:479

commit v7 on v6

--- a/solution.py
+++ b/solution.py
@@ -9,7 +9,7 @@
 
 
 CAP = 2
-UNROLL = 4
+STEP_UNITS = 8
 PARTS = 2
 LANES = 128
 FAR = 1e30
@@ -233,6 +233,7 @@
     grads_hbm,
     dq_ref,
     grads_ref,
+    entries_ref,
     out_sem,
 ):
     tokens = q_ref.shape[0]
@@ -240,40 +241,54 @@
     block_size = grads_ref.shape[1] // CAP
     scale = head_size ** (-0.5)
     lane_block = lax.div(lax.broadcasted_iota(jnp.int32, (1, tokens), 1), block_size)
+    shards = wanted_ref.shape[0]
     dq_ref[...] = own_dq_ref[...]
 
-    def owner_step(step, carry):
-        sums = []
-        for at in range(UNROLL):
-            owner = step * UNROLL + at
-            for slot in range(CAP):
-                unit = wanted_ref[owner, 0, slot]
-                safe = jnp.maximum(unit, 0)
-                head = lax.div(safe, block_count)
-                block = lax.rem(safe, block_count)
-                bits = jnp.where(unit >= 0, bits_ref[head, owner * block_count + block], 0)
-                lanes = pl.ds(pl.multiple_of(head * head_size, head_size), head_size)
-                place = slice(slot * block_size, (slot + 1) * block_size)
-                q = q_ref[:, lanes]
-                do = do_ref[:, lanes]
-                k = pulled_ref[owner, place, :head_size]
-                v = pulled_ref[owner, place, head_size:]
-                chosen = jnp.bitwise_and(jnp.right_shift(bits, lane_block), 1) == 1
-                shift = jnp.where(chosen, lse_ref[pl.ds(head, 1), :], jnp.float32(FAR))
-                probs = jnp.exp(dot_nt(k, q) * scale - shift)
-                dprobs = dot_nt(v, do)
-                dscores = (probs * (dprobs - delta_ref[pl.ds(head, 1), :])).astype(jnp.bfloat16)
-                dk = (dot_nn(dscores, q) * scale).astype(grads_ref.dtype)
-                dv = dot_nn(probs.astype(jnp.bfloat16), do).astype(grads_ref.dtype)
-                sums.append((owner, place, dk, dv, lanes, dot_tn(dscores, k)))
-        for owner, place, dk, dv, lanes, value in sums:
-            grads_ref[owner, place, :head_size] = dk
-            grads_ref[owner, place, head_size:] = dv
+    def collect(owner, count):
+        for slot in range(CAP):
+            entries_ref[count] = owner * CAP + slot
+            count += (wanted_ref[owner, 0, slot] >= 0).astype(jnp.int32)
+        return count
+
+    count = lax.fori_loop(0, lax.axis_index("seq"), collect, 0)
+    for at in range(STEP_UNITS):
+        entries_ref[count + at] = -1
+
+    def units_step(step, carry):
+        results = []
+        for at in range(STEP_UNITS):
+            entry = entries_ref[step * STEP_UNITS + at]
+            valid = entry >= 0
+            safe = jnp.maximum(entry, 0)
+            owner = lax.div(safe, CAP)
+            slot = lax.rem(safe, CAP)
+            unit = jnp.maximum(wanted_ref[owner, 0, slot], 0)
+            head = lax.div(unit, block_count)
+            block = lax.rem(unit, block_count)
+            bits = jnp.where(valid, bits_ref[head, owner * block_count + block], 0)
+            lanes = pl.ds(pl.multiple_of(head * head_size, head_size), head_size)
+            place = pl.ds(pl.multiple_of(slot * block_size, block_size), block_size)
+            q = q_ref[:, lanes]
+            do = do_ref[:, lanes]
+            k = pulled_ref[owner, place, :head_size]
+            v = pulled_ref[owner, place, head_size:]
+            chosen = jnp.bitwise_and(jnp.right_shift(bits, lane_block), 1) == 1
+            shift = jnp.where(chosen, lse_ref[pl.ds(head, 1), :], jnp.float32(FAR))
+            probs = jnp.exp(dot_nt(k, q) * scale - shift)
+            dprobs = dot_nt(v, do)
+            dscores = (probs * (dprobs - delta_ref[pl.ds(head, 1), :])).astype(jnp.bfloat16)
+            dk = (dot_nn(dscores, q) * scale).astype(grads_ref.dtype)
+            dv = dot_nn(probs.astype(jnp.bfloat16), do).astype(grads_ref.dtype)
+            target = jnp.where(valid, owner, shards)
+            results.append((target, place, dk, dv, lanes, dot_tn(dscores, k)))
+        for target, place, dk, dv, lanes, value in results:
+            grads_ref[target, place, :head_size] = dk
+            grads_ref[target, place, head_size:] = dv
             dq_ref[:, lanes] += value
         return carry
 
-    lax.fori_loop(0, lax.div(lax.axis_index("seq") + UNROLL - 1, UNROLL), owner_step, 0)
-    store = pltpu.make_async_copy(grads_ref, grads_hbm, out_sem)
+    lax.fori_loop(0, lax.div(count + STEP_UNITS - 1, STEP_UNITS), units_step, 0)
+    store = pltpu.make_async_copy(grads_ref.at[pl.ds(0, shards)], grads_hbm, out_sem)
     store.start()
     part = tokens // 4
     here = lax.axis_index("head")
@@ -396,7 +411,6 @@
     )(selected)
     incoming = lax.all_to_all(wanted, "seq", split_axis=0, concat_axis=0, tiled=True)
     exchange = (shards, CAP * block_size, 2 * head_size)
-    assert shards % UNROLL == 0
     outgoing = pl.pallas_call(
         functools.partial(gather_kernel, block_count),
         out_shape=shape(exchange, bf16),
@@ -450,7 +464,8 @@
         out_specs=(VMEM, HBM),
         scratch_shapes=[
             pltpu.VMEM((tokens, row_width), f32),
-            pltpu.VMEM(exchange, bf16),
+            pltpu.VMEM((shards + 1,) + exchange[1:], bf16),
+            pltpu.SMEM((shards * CAP + STEP_UNITS,), jnp.int32),
             pltpu.SemaphoreType.DMA,
         ],
         compiler_params=params(),

time: 70.5 us -> 68.7 us (0.974)
  starting transfers between devices: 14.7 us -> 12.8 us
    all_to_all x1, starting transfers between devices: 7.49 us -> 5.64 us  [per_device(): lax.all_to_all(grads, 'seq', split_axis=0, concat_axis=0, tiled=True)]
where the time goes in v7:
time: 68.7 us; the launch traced here: 68.1 us
  Pallas kernels  21.9 us (32%)
  waiting for transfers between devices  18.3 us (27%)
  blocking collectives  13.6 us (20%)
  starting transfers between devices  12.8 us (19%)
  local copies, waits for them, and re-layouts  0.71 us (1%)
  between operations  0.71 us (1%)
    all_to_all x1, blocking collectives, per_device(): lax.all_to_all(wanted, 'seq', split_axis=0, concat_axis=0, tiled=True)  13.6 us
    ppermute x2, waiting for transfers between devices, per_device(): across_got = lax.ppermute(far_sum, 'head', across)  11.3 us
    all_to_all x1, waiting for transfers between devices, per_device(): lax.all_to_all(outgoing, 'seq', split_axis=0, concat_axis=0, tiled=True)  6.97 us
    pallas_call x1, Pallas kernels, per_device(): pl.pallas_call(functools.partial(own_kernel, block_count), out_shape=(sha...  6.34 us
    pallas_call x2, Pallas kernels, per_device(): pl.pallas_call(functools.partial(product_kernel, at * share), out_shape=(...  6.3 us
    all_to_all x1, starting transfers between devices, per_device(): lax.all_to_all(grads, 'seq', split_axis=0, concat_axis=0, tiled=True)  5.64 us
    all_to_all x1, starting transfers between devices, per_device(): lax.all_to_all(outgoing, 'seq', split_axis=0, concat_axis=0, tiled=True)  3.51 us
    pallas_call x1, Pallas kernels, per_device(): pl.pallas_call(functools.partial(finish_kernel, block_count), out_shape=(...  3.33 us
  transfers between devices with their start and end apart: 8, of which 3 were waited for; matrix products, arithmetic and copies ran while one was open for 0% of the time, Pallas kernels for 15%

profile of v7, /device:TPU:0, one launch (start us, length us, event | category | flops | bytes accessed | tf_op | source)
XLA Modules:
  0.0 68.1 jit_solution(17338504332518967870)
XLA Ops:
  0.6 0.0 copy-start
  0.6 0.7 %copy-done = s32[8,4,16]{2,1,0:T(4,128)S(1)} copy-done((s32[8,4,16]{2,1,0:T(4,128)S(1)}, s32[8,4,16]{2,1,0:T(4,128)}, u32[]{:S(2)}) %copy-start) | copy-done | bytes 2072
  1.3 0.6 index.1
  1.9 13.6 %all_to_all.15.incoming_ref = s32[8,1,128]{2,1,0:T(1,128)S(1)} all-to-all(s32[8,1,128]{2,1,0:T(1,128)S(1)} %get-tuple-element.24.wanted_ref), channel_id=1, replica_groups=mesh['seq'=8,'head'=4] {'seq'}, dimensions={0} | all-to-all | bytes 8192 | tf_op jit(solution)/shard_map/all_to_all | solution.py:412
  15.5 2.8 %gather.1 = bf16[8,128,256]{2,1,0:T(8,128)(2,1)} custom-call(s32[8,1,128]{2,1,0:T(1,128)S(1)} %all_to_all.15.incoming_ref, bf16[256,1024]{1,0:T(8,128)(2,1)} %k_hbm.1, bf16[256,1024]{1,0:T(8,128)(2,1)} %v_hbm.1), custom_call_target="tpu_custom_call" | custom-call | tf_op jit(solution)/shard_map/gather/pallas_call | solution.py:414
  18.3 3.5 %all-to-all-start.1 = ((bf16[8,128,256]{2,1,0:T(8,128)(2,1)}), bf16[8,128,256]{2,1,0:T(8,128)(2,1)S(1)}, u32[]{:S(2)}, u32[]{:S(2)}) async-start(bf16[8,128,256]{2,1,0:T(8,128)(2,1)} %gather.1), calls=%async_computation.1 | async-start | bytes 1048576 | tf_op jit(solution)/shard_map/all_to_all | solution.py:427
  21.8 6.3 %own.1 = (bf16[256,1024]{1,0:T(8,128)(2,1)S(1)}, bf16[256,1024]{1,0:T(8,128)(2,1)S(1)}, f32[8,256]{1,0:T(8,128)S(1)}, f32[8,256]{1,0:T(8,128)S(1)}, f32[256,1024...) custom-call(s32[8,128]{1,0:T(8,128)S(1)} %get-tuple-element.25.bits_ref, bf16[256,1024]{1,0:T(8,128)(2,1)} %q_hbm.1, ...), custom_call_target="tpu_custom_call" | custom-call | flops 5368709120 | bytes 5767168 | tf_op jit(solution)/shard_map/own/pallas_call | solution.py:430
  28.2 7.0 %all-to-all-done.1.pulled_ref = bf16[8,128,256]{2,1,0:T(8,128)(2,1)S(1)} async-done(((bf16[8,128,256]{2,1,0:T(8,128)(2,1)}), bf16[8,128,256]{2,1,0:T(8,128)(2,1)S(1)}, u32[]{:S(2)}, u32[]{:S(2)}) %all-to-all-start.1) | async-done | bytes 524320 | tf_op jit(solution)/shard_map/all_to_all | solution.py:427
  35.1 1.5 %units.1 = (bf16[256,1024]{1,0:T(8,128)(2,1)S(1)}, bf16[8,128,256]{2,1,0:T(8,128)(2,1)}) custom-call(s32[8,1,128]{2,1,0:T(1,128)S(1)} %get-tuple-element.24.wanted_ref, s32[8,128]{1,0:T(8,128)S(1)} %get-tuple-element.25.bits_ref, bf16[8,128,256]{2,1,0:T(8,128)(2,1)S(1)} %all-to-all-done.1.pulled_ref, bf16[256,1024]{1,0:T(8,128)(2,1)S(1)} %get-tuple-element.26.q_ref, ...), custom_call_target="tpu_custom_call" | custom-call | flops 335544320 | bytes 2621440 | tf_op jit(solution)/shard_map/units/pallas_call | solution.py:460
  36.7 3.2 %product.3 = (bf16[64,2048]{1,0:T(8,128)(2,1)S(1)}, bf16[64,2048]{1,0:T(8,128)(2,1)S(1)}, bf16[64,2048]{1,0:T(8,128)(2,1)S(1)}, bf16[64,2048]{1,0:T(8,128)(2,1)S(1)}) custom-call(bf16[256,1024]{1,0:T(8,128)(2,1)S(1)} %get-tuple-element.31.rows_ref, bf16[4096,1024]{1,0:T(8,128)(2,1)} %w_hbm.3), custom_call_target="tpu_custom_call" | custom-call | flops 1073741824 | bytes 4194304 | tf_op jit(solution)/shard_map/product/pallas_call | solution.py:482
  39.8 0.1 collective-permute-start.4
  39.9 5.6 %all-to-all-start.2 = ((bf16[8,128,256]{2,1,0:T(8,128)(2,1)}), bf16[8,128,256]{2,1,0:T(8,128)(2,1)S(1)}, u32[]{:S(2)}, u32[]{:S(2)}) async-start(bf16[8,128,256]{2,1,0:T(8,128)(2,1)} %get-tuple-element.40), calls=%async_computation.2 | async-start | bytes 1048576 | tf_op jit(solution)/shard_map/all_to_all | solution.py:475
  45.6 0.2 collective-permute-start.3
  45.8 3.1 %product.2 = (bf16[64,2048]{1,0:T(8,128)(2,1)S(1)}, bf16[64,2048]{1,0:T(8,128)(2,1)S(1)}, bf16[64,2048]{1,0:T(8,128)(2,1)S(1)}, bf16[64,2048]{1,0:T(8,128)(2,1)S(1)}) custom-call(bf16[256,1024]{1,0:T(8,128)(2,1)S(1)} %get-tuple-element.31.rows_ref, bf16[4096,1024]{1,0:T(8,128)(2,1)} %w_hbm.3), custom_call_target="tpu_custom_call" | custom-call | flops 1073741824 | bytes 4194304 | tf_op jit(solution)/shard_map/product/pallas_call | solution.py:482
  48.9 0.4 collective-permute-start
  49.3 0.2 collective-permute-start.1
  49.5 0.0 collective-permute-done.4
  49.5 0.1 add_convert_fusion
  49.6 1.5 %collective-permute-start.5 = (bf16[64,2048]{1,0:T(8,128)(2,1)S(1)}, bf16[64,2048]{1,0:T(8,128)(2,1)S(1)}, u32[]{:S(2)}, u32[]{:S(2)}) collective-permute-start(bf16[64,2048]{1,0:T(8,128)(2,1)S(1)} %add_convert_fusion), channel_id=1, source_target_pairs={{0,2},{1,3},{2,0},{3,1},{4,6},{5,7},{6,4},{7,5},{8,10},{9,11},{10,... | collective-permute-start | bytes 786440 | tf_op jit(solution)/shard_map/ppermute | solution.py:494
  51.1 0.0 collective-permute-done.1
  51.1 0.1 add_convert_fusion.1
  51.1 1.3 %collective-permute-start.2 = (bf16[64,2048]{1,0:T(8,128)(2,1)S(1)}, bf16[64,2048]{1,0:T(8,128)(2,1)S(1)}, u32[]{:S(2)}, u32[]{:S(2)}) collective-permute-start(bf16[64,2048]{1,0:T(8,128)(2,1)S(1)} %add_convert_fusion.1), channel_id=1, source_target_pairs={{0,2},{1,3},{2,0},{3,1},{4,6},{5,7},{6,4},{7,5},{8,10},{9,11},{10,... | collective-permute-start | bytes 786440 | tf_op jit(solution)/shard_map/ppermute | solution.py:494
  52.5 0.0 collective-permute-done.3.refs_4_
  52.5 0.0 collective-permute-done.refs_1_
  52.5 6.3 %collective-permute-done.5.refs_5_ = bf16[64,2048]{1,0:T(8,128)(2,1)S(1)} collective-permute-done((bf16[64,2048]{1,0:T(8,128)(2,1)S(1)}, bf16[64,2048]{1,0:T(8,128)(2,1)S(1)}, u32[]{:S(2)}, u32[]{:S(2)}) %collective-permute-start.5) | collective-permute-done | bytes 262176 | tf_op jit(solution)/shard_map/ppermute | solution.py:494
  58.8 5.0 %collective-permute-done.2.refs_2_ = bf16[64,2048]{1,0:T(8,128)(2,1)S(1)} collective-permute-done((bf16[64,2048]{1,0:T(8,128)(2,1)S(1)}, bf16[64,2048]{1,0:T(8,128)(2,1)S(1)}, u32[]{:S(2)}, u32[]{:S(2)}) %collective-permute-start.2) | collective-permute-done | bytes 262176 | tf_op jit(solution)/shard_map/ppermute | solution.py:494
  63.8 1.0 %join.1 = bf16[64,4096]{1,0:T(8,128)(2,1)} custom-call(bf16[64,2048]{1,0:T(8,128)(2,1)S(1)} %get-tuple-element.32.refs_0_, bf16[64,2048]{1,0:T(8,128)(2,1)S(1)} %collective-permute-done.refs_1_, bf16[64,2048]{1,0:T(8,128)(2,1)S(1)} %collective-permute-done.2.refs_2_, bf16[64,2048]{1,0:T(8,128)(2,1)S(1)} %get-tuple-element.36.refs_3_, ...), custom_call_target="tpu_custom_call" | custom-call | tf_op jit(solution)/shard_map/join/pallas_call | solution.py:513
  64.8 0.0 all-to-all-done.2.returned_ref
  64.8 3.3 %finish.1 = (bf16[256,1024]{1,0:T(8,128)(2,1)}, bf16[256,1024]{1,0:T(8,128)(2,1)}) custom-call(s32[8,1,128]{2,1,0:T(1,128)S(1)} %all_to_all.15.incoming_ref, bf16[8,128,256]{2,1,0:T(8,128)(2,1)S(1)} %all-to-all-done.2.returned_ref, f32[256,1024]{1,0:T(8,128)} %get-tuple-element.41.own_dk_hbm, f32[256,1024]{1,0:T(8,128)} %get-tuple-element.42.own_dv_hbm), custom_call_target="tpu_custom_call" | custom-call | tf_op jit(solution)/shard_map/finish/pallas_call | solution.py:500
Async XLA Ops:
  0.6 0.7 %copy-start = (s32[8,4,16]{2,1,0:T(4,128)S(1)}, s32[8,4,16]{2,1,0:T(4,128)}, u32[]{:S(2)}) copy-start(s32[8,4,16]{2,1,0:T(4,128)} %selected_ref.1) | copy-start | bytes 6148
  18.3 16.8 %all-to-all-start.1 = ((bf16[8,128,256]{2,1,0:T(8,128)(2,1)}), bf16[8,128,256]{2,1,0:T(8,128)(2,1)S(1)}, u32[]{:S(2)}, u32[]{:S(2)}) async-start(bf16[8,128,256]{2,1,0:T(8,128)(2,1)} %gather.1), calls=%async_computation.1 | async-start | bytes 1048576 | tf_op jit(solution)/shard_map/all_to_all | solution.py:427
  39.8 9.7 %collective-permute-start.4 = (bf16[64,2048]{1,0:T(8,128)(2,1)S(1)}, bf16[64,2048]{1,0:T(8,128)(2,1)S(1)}, u32[]{:S(2)}, u32[]{:S(2)}) collective-permute-start(bf16[64,2048]{1,0:T(8,128)(2,1)S(1)} %get-tuple-element.39), channel_id=1, source_target_pairs={{0,1},{1,0},{2,3},{3,2},{4,5},{5,4},{6,7},{7,6},{8,9},{9,8},{10,11... | collective-permute-start | bytes 786440 | tf_op jit(solution)/shard_map/ppermute | solution.py:492
  39.9 24.8 %all-to-all-start.2 = ((bf16[8,128,256]{2,1,0:T(8,128)(2,1)}), bf16[8,128,256]{2,1,0:T(8,128)(2,1)S(1)}, u32[]{:S(2)}, u32[]{:S(2)}) async-start(bf16[8,128,256]{2,1,0:T(8,128)(2,1)} %get-tuple-element.40), calls=%async_computation.2 | async-start | bytes 1048576 | tf_op jit(solution)/shard_map/all_to_all | solution.py:475
  45.6 6.9 %collective-permute-start.3 = (bf16[64,2048]{1,0:T(8,128)(2,1)S(1)}, bf16[64,2048]{1,0:T(8,128)(2,1)S(1)}, u32[]{:S(2)}, u32[]{:S(2)}) collective-permute-start(bf16[64,2048]{1,0:T(8,128)(2,1)S(1)} %get-tuple-element.37), channel_id=1, source_target_pairs={{0,1},{1,0},{2,3},{3,2},{4,5},{5,4},{6,7},{7,6},{8,9},{9,8},{10,11... | collective-permute-start | bytes 786440 | tf_op jit(solution)/shard_map/ppermute | solution.py:495
  48.9 3.5 %collective-permute-start = (bf16[64,2048]{1,0:T(8,128)(2,1)S(1)}, bf16[64,2048]{1,0:T(8,128)(2,1)S(1)}, u32[]{:S(2)}, u32[]{:S(2)}) collective-permute-start(bf16[64,2048]{1,0:T(8,128)(2,1)S(1)} %get-tuple-element.33), channel_id=1, source_target_pairs={{0,1},{1,0},{2,3},{3,2},{4,5},{5,4},{6,7},{7,6},{8,9},{9,8},{10,11... | collective-permute-start | bytes 786440 | tf_op jit(solution)/shard_map/ppermute | solution.py:495
  49.3 1.8 %collective-permute-start.1 = (bf16[64,2048]{1,0:T(8,128)(2,1)S(1)}, bf16[64,2048]{1,0:T(8,128)(2,1)S(1)}, u32[]{:S(2)}, u32[]{:S(2)}) collective-permute-start(bf16[64,2048]{1,0:T(8,128)(2,1)S(1)} %get-tuple-element.35), channel_id=1, source_target_pairs={{0,1},{1,0},{2,3},{3,2},{4,5},{5,4},{6,7},{7,6},{8,9},{9,8},{10,11... | collective-permute-start | bytes 786440 | tf_op jit(solution)/shard_map/ppermute | solution.py:492
  49.6 9.2 %collective-permute-start.5 = (bf16[64,2048]{1,0:T(8,128)(2,1)S(1)}, bf16[64,2048]{1,0:T(8,128)(2,1)S(1)}, u32[]{:S(2)}, u32[]{:S(2)}) collective-permute-start(bf16[64,2048]{1,0:T(8,128)(2,1)S(1)} %add_convert_fusion), channel_id=1, source_target_pairs={{0,2},{1,3},{2,0},{3,1},{4,6},{5,7},{6,4},{7,5},{8,10},{9,11},{10,... | collective-permute-start | bytes 786440 | tf_op jit(solution)/shard_map/ppermute | solution.py:494
  51.1 12.6 %collective-permute-start.2 = (bf16[64,2048]{1,0:T(8,128)(2,1)S(1)}, bf16[64,2048]{1,0:T(8,128)(2,1)S(1)}, u32[]{:S(2)}, u32[]{:S(2)}) collective-permute-start(bf16[64,2048]{1,0:T(8,128)(2,1)S(1)} %add_convert_fusion.1), channel_id=1, source_target_pairs={{0,2},{1,3},{2,0},{3,1},{4,6},{5,7},{6,4},{7,5},{8,10},{9,11},{10,... | collective-permute-start | bytes 786440 | tf_op jit(solution)/shard_map/ppermute | solution.py:494
